TPU v7x, 32 devices: a whole 2x2x4 slice. The times are simulated.
32 devices in a mesh: replica: 1, ctx: 32 (over z, y, x, core).
Axes of the slice: x: 2, y: 2, z: 4, core: 2. Of those that a mesh axis runs over, the one named last changes fastest.
Arguments:
- queries: bfloat16 [128, 4096], P(('replica', 'ctx')), may hold values from -4 to 6.2
- own_key: bfloat16 [128, 256], P(('replica', 'ctx')), may hold values from -12 to 12
- own_value: bfloat16 [128, 256], P(('replica', 'ctx')), may hold values from -40 to 40
- cache_keys: bfloat16 [2, 1024, 256], P('replica', 'ctx'), may hold values from -4 to 4.7
- cache_values: bfloat16 [2, 1024, 256], P('replica', 'ctx'), may hold values from -40 to 40
- prefix_of_row: int32 [128], P('replica'), may hold values from 0 to 1, as said below
- context_len: int32 [2], P('replica'), may hold values from 512 to 1024
- hidden_in: bfloat16 [128, 4096], P(('replica', 'ctx')), may hold values from -3 to 3
- w_out: bfloat16 [4096, 4096], P('ctx'), may hold values from -0.09375 to 0.09375
- norm_gain: float32 [4096], replicated, may hold values from 0.5 to 1.5
- expert_ids: int32 [128, 8], P(('replica', 'ctx')), may hold values from 0 to 15, all different within a row; in each aligned block of 4 rows (0 to 3, 4 to 7, ...) at most 4 rows name the same one
- route_weights: float32 [128, 8], P(('replica', 'ctx')), may hold values from 0.05 to 0.4
- gate_up_codes: bfloat16 [32, 4096, 768], P('ctx'), may hold values from -0.09375 to 0.09375
- gate_up_scales: float32 [32, 32, 6], P('ctx'), may hold values from 0.6 to 1.7
- down_codes: bfloat16 [32, 384, 4096], P('ctx'), may hold values from -0.21875 to 0.21875
- down_scales: float32 [32, 3, 32], P('ctx'), may hold values from 0.6 to 1.7
Outputs:
- attention_out: bfloat16 [128, 4096], P(('replica', 'ctx'))
- layer_out: bfloat16 [128, 4096], P(('replica', 'ctx'))
Inputs may be any that keep to these rules, and one draw needn't show every extreme that they name: `prefix_of_row`: the rows come in aligned blocks of 64 consecutive rows that all name one prefix. `expert_ids`: each row names 8 different experts; among the 4 rows of one device no expert is named more than 4 times.
All inputs are finite; a program needn't handle non-finite values.
Results may differ from a plain program's by a relative error of at most 0.014.
Values may be sent and summed in bfloat16 or wider, within the bound.
No kernel may reach another device: no remote copies, remote signals or barrier semaphores. Data moves between devices by JAX's collectives and lax.ppermute only.
A program may use at most 128 MiB of HBM per device.

v0:
```python
import math

import jax
import jax.numpy as jnp
from jax import lax
from jax.sharding import PartitionSpec as P

HD = 128
CAND = 64


NEG = -1e30
EPSILON = 1e-06


def swapped(value, axis, distance):
    return lax.ppermute(value, axis, [(i, i ^ 1 << distance) for i in range(lax.axis_size(axis))])


def dequantize(code_values, scales):
    rows_per = code_values.shape[0] // scales.shape[0]
    cols_per = code_values.shape[1] // scales.shape[1]
    spread = jnp.repeat(jnp.repeat(scales, rows_per, axis=0), cols_per, axis=1)
    return (code_values.astype(jnp.float32) * spread).astype(jnp.bfloat16)


def block_partials(query_heads, key_heads, value_heads, is_valid, score_scale):
    scores = (
        jnp.einsum(
            "brgqd,bstgd->brgqst", query_heads, key_heads, preferred_element_type=jnp.float32
        )
        * score_scale
    )
    valid_full = is_valid[:, None, None, None, :, :]
    masked = jnp.where(valid_full, scores, NEG)
    block_max = jnp.max(masked, axis=-1)
    weights = jnp.where(valid_full, jnp.exp(masked - block_max[..., None]), 0.0)
    block_total = jnp.sum(weights, axis=-1)
    numerator = jnp.einsum(
        "brgqst,bstgd->brgqsd",
        weights.astype(jnp.bfloat16),
        value_heads,
        preferred_element_type=jnp.float32,
    )
    block_out = (numerator / jnp.maximum(block_total, 1.0)[..., None]).astype(jnp.bfloat16)
    return (block_max, block_total, block_out)


def fold_blocks(block_max, block_total, block_out):
    local_top = jnp.max(block_max, axis=-1)
    factor = block_total * jnp.exp(block_max - local_top[..., None])
    numer = jnp.sum(factor[..., None] * block_out.astype(jnp.float32), axis=-2)
    denom = jnp.sum(factor, axis=-1)
    return (local_top, numer, denom)


def merge_pair(first, second):
    top = jnp.maximum(first[0], second[0])
    scale_first = jnp.exp(first[0] - top)
    scale_second = jnp.exp(second[0] - top)
    numer = first[1] * scale_first[..., None] + second[1] * scale_second[..., None]
    denom = first[2] * scale_first + second[2] * scale_second
    return (top, numer, denom)


def local(
    queries,
    own_key,
    own_value,
    cache_keys,
    cache_values,
    prefix_of_row,
    context_len,
    hidden_in,
    w_out,
    norm_gain,
    expert_ids,
    route_weights,
    gate_up_codes,
    gate_up_scales,
    down_codes,
    down_scales,
):
    shards = lax.axis_size("ctx")
    device = lax.axis_index("ctx")
    head_size = HD
    local_rows = queries.shape[0]
    key_groups = own_key.shape[1] // head_size
    per_group = queries.shape[1] // own_key.shape[1]
    head_count = key_groups * per_group
    ctx_local = cache_keys.shape[1]
    key_width = cache_keys.shape[2]
    score_scale = 1.0 / math.sqrt(head_size)
    block_prefix = prefix_of_row.reshape(-1, CAND)[:, 0]
    prefix_count = block_prefix.shape[0]
    group_size = CAND // local_rows
    group_bits = group_size.bit_length() - 1
    prefix_bits = (shards // group_size).bit_length() - 1
    group_index = device // group_size
    member = device % group_size
    relay = jnp.concatenate(
        [jnp.take(cache_keys, block_prefix, axis=0), jnp.take(cache_values, block_prefix, axis=0)],
        axis=-1,
    )
    relay_shape = relay.shape
    for bit in range(prefix_bits):
        low = 1 << bit
        view = relay.reshape((relay_shape[0] // (2 * low), 2, low) + relay_shape[1:])
        own_bit = group_index // low % 2
        sent = lax.dynamic_index_in_dim(view, 1 - own_bit, 1, False)
        got = swapped(sent, "ctx", group_bits + bit)
        view = lax.dynamic_update_index_in_dim(view, got, 1 - own_bit, 1)
        relay = view.reshape(relay_shape)
    held = queries
    for bit in range(group_bits):
        other = swapped(held, "ctx", bit)
        upper = device // (1 << bit) % 2
        held = jnp.where(
            upper == 0, jnp.concatenate([held, other], 0), jnp.concatenate([other, held], 0)
        )
    length = jnp.take(context_len, jnp.take(block_prefix, group_index))
    source_block = jnp.arange(prefix_count, dtype=jnp.int32) * group_size + member
    position = source_block[:, None] * ctx_local + jnp.arange(ctx_local, dtype=jnp.int32)[None, :]
    is_valid = (position < length)[None]
    query_heads = held.reshape(1, CAND, key_groups, per_group, head_size)
    key_heads = relay[..., :key_width].reshape(1, prefix_count, ctx_local, key_groups, head_size)
    value_heads = relay[..., key_width:].reshape(1, prefix_count, ctx_local, key_groups, head_size)
    block_max, block_total, block_out = block_partials(
        query_heads, key_heads, value_heads, is_valid, score_scale
    )
    block_max = block_max.reshape(CAND, head_count, prefix_count)
    block_total = block_total.reshape(CAND, head_count, prefix_count)
    block_out = block_out.reshape(CAND, head_count, prefix_count, head_size)
    state = fold_blocks(block_max, block_total, block_out)
    for bit in reversed(range(group_bits)):
        own_bit = device // (1 << bit) % 2
        parts = tuple((item.reshape((2, item.shape[0] // 2) + item.shape[1:]) for item in state))
        sent = tuple((lax.dynamic_index_in_dim(item, 1 - own_bit, 0, False) for item in parts))
        kept = tuple((lax.dynamic_index_in_dim(item, own_bit, 0, False) for item in parts))
        got = swapped(sent, "ctx", bit)
        state = merge_pair(kept, got)
    merged_top, merged_numer, merged_denom = state
    own_heads = queries.reshape(local_rows, key_groups, per_group, head_size)
    own_keys = own_key.reshape(local_rows, key_groups, head_size)
    own_score = (
        jnp.einsum(
            "rgqd,rgd->rgq", own_heads, own_keys, preferred_element_type=jnp.float32
        ).reshape(local_rows, head_count)
        * score_scale
    )
    top_score = jnp.maximum(merged_top, own_score)
    block_scale = jnp.exp(merged_top - top_score)
    own_weight = jnp.exp(own_score - top_score)
    own_term = own_value.reshape(local_rows, key_groups, 1, head_size).astype(
        jnp.float32
    ) * own_weight.reshape(local_rows, key_groups, per_group, 1)
    numerator_all = merged_numer * block_scale[..., None] + own_term.reshape(
        local_rows, head_count, head_size
    )
    denominator = merged_denom * block_scale + own_weight
    attended = (numerator_all / denominator[..., None]).reshape(local_rows, -1).astype(jnp.bfloat16)
    column_weights = lax.all_to_all(w_out, "ctx", split_axis=1, concat_axis=0, tiled=True)
    projected_cols = jnp.dot(
        lax.all_gather(attended, "ctx", axis=0, tiled=True),
        column_weights,
        preferred_element_type=jnp.float32,
    )
    projected = lax.all_to_all(
        projected_cols.astype(jnp.bfloat16), "ctx", split_axis=0, concat_axis=1, tiled=True
    ).astype(projected_cols.dtype)
    mixed_rows = hidden_in.astype(jnp.float32) + projected
    attention_out = mixed_rows.astype(jnp.bfloat16)
    mean_square = jnp.mean(mixed_rows * mixed_rows, axis=-1, keepdims=True)
    normed = (mixed_rows * lax.rsqrt(mean_square + EPSILON) * norm_gain).astype(jnp.bfloat16)
    experts_all = shards // 2
    per_row = expert_ids.shape[1]
    capacity = min(
        local_rows, max(2, 2 * ((local_rows * per_row + experts_all - 1) // experts_all))
    )
    pick_ids = expert_ids.reshape(-1)
    one_hot = (pick_ids[:, None] == jnp.arange(experts_all, dtype=jnp.int32)[None, :]).astype(
        jnp.int32
    )
    earlier = jnp.cumsum(one_hot, axis=0) - one_hot
    slot_index = jnp.sum(earlier * one_hot, axis=1)
    target = pick_ids * capacity + slot_index
    slot_range = jnp.arange(experts_all * capacity, dtype=jnp.int32)
    placed = slot_range[:, None] == target[None, :]
    placement_matrix = jnp.sum(
        placed.reshape(experts_all * capacity, local_rows, per_row).astype(jnp.float32), axis=2
    ).astype(jnp.bfloat16)
    bucket = jnp.dot(placement_matrix, normed, preferred_element_type=jnp.float32).astype(
        jnp.bfloat16
    )
    feature_width = bucket.shape[1]
    outgoing = jnp.broadcast_to(
        bucket.reshape(experts_all, 1, capacity, feature_width),
        (experts_all, 2, capacity, feature_width),
    ).reshape(shards, capacity, feature_width)
    gate_up = dequantize(gate_up_codes[0], gate_up_scales[0])
    down_proj = dequantize(down_codes[0], down_scales[0])
    half_width = down_proj.shape[0]
    received = lax.all_to_all(outgoing, "ctx", split_axis=0, concat_axis=0, tiled=True)
    sources, slot_count, width_in = received.shape
    flat_rows = received.reshape(sources * slot_count, width_in)
    projected_in = jnp.dot(flat_rows, gate_up, preferred_element_type=jnp.float32)
    activated = (jax.nn.silu(projected_in[:, :half_width]) * projected_in[:, half_width:]).astype(
        jnp.bfloat16
    )
    result = jnp.dot(activated, down_proj, preferred_element_type=jnp.float32).astype(jnp.bfloat16)
    results = result.reshape(sources, slot_count, width_in)
    returned = lax.all_to_all(results, "ctx", split_axis=0, concat_axis=0, tiled=True)
    halves = returned.reshape(experts_all, 2, capacity, feature_width).astype(jnp.float32)
    summed = (halves[:, 0] + halves[:, 1]).reshape(experts_all * capacity, feature_width)
    weighted = jnp.where(placed, route_weights.reshape(1, -1), 0.0)
    combine = jnp.sum(weighted.reshape(experts_all * capacity, local_rows, per_row), axis=2).T
    expert_sum = jnp.dot(combine, summed, precision=lax.Precision.HIGHEST)
    layer_out = (mixed_rows + expert_sum).astype(jnp.bfloat16)
    return (attention_out, layer_out)


def solution(mesh):
    return jax.shard_map(
        local,
        mesh=mesh,
        in_specs=(
            P(("replica", "ctx"), None),
            P(("replica", "ctx"), None),
            P(("replica", "ctx"), None),
            P("replica", "ctx", None),
            P("replica", "ctx", None),
            P("replica"),
            P("replica"),
            P(("replica", "ctx"), None),
            P("ctx", None),
            P(),
            P(("replica", "ctx"), None),
            P(("replica", "ctx"), None),
            P("ctx", None, None),
            P("ctx", None, None),
            P("ctx", None, None),
            P("ctx", None, None),
        ),
        out_specs=(P(("replica", "ctx"), None), P(("replica", "ctx"), None)),
        check_vma=False,
    )
```

profile of v0, /device:TPU:0, one launch (start us, length us, event | category | flops | bytes accessed | tf_op | source)
XLA Modules:
  0.0 231.8 jit_solution(662376032517230085)
XLA Ops:
  7.2 0.7 reshape.312
  8.1 0.5 gather_fusion
  8.7 1.3 gather_fusion.1
  10.1 4.1 %collective-permute-start = (bf16[1,1,32,512]{3,2,1,0:T(8,128)(2,1)S(1)}, bf16[1,1,32,512]{3,2,1,0:T(8,128)(2,1)S(1)}, u32[]{:S(2)}, u32[]{:S(2)}) collective-permute-start(bf16[1,1,32,512]{3,2,1,0:T(8,128)(2,1)S(1)} %fusion.37), channel_id=1, source_target_pairs={{0,16},{1,17},{2,18},{3,19},{4,20},{5,21},{6,22},{7,23},{8,24},{9,... | collective-permute-start | bytes 98312 | tf_op jit(solution)/shard_map/ppermute | solution.py:17
  14.2 2.3 copy.157
  16.5 3.9 %all-to-all-start = ((bf16[128,32,128]{0,2,1:T(8,128)(2,1)}), bf16[128,32,128]{0,2,1:T(8,128)(2,1)S(1)}, u32[]{:S(2)}, u32[]{:S(2)}) async-start(bf16[128,32,128]{0,2,1:T(8,128)(2,1)} %bitcast.58), calls=%async_computation | async-start | bytes 2097152 | tf_op jit(solution)/shard_map/all_to_all | solution.py:162
  20.5 0.5 constant_dynamic-slice_fusion
  21.7 1.2 dynamic-slice.6
  23.8 0.8 copy.174
  24.5 0.7 reshape.431
  25.2 0.9 maximum_select_fusion.6
  26.1 1.8 collective-permute-start.2
  28.0 4.2 %collective-permute-done.2 = bf16[8,4096]{1,0:T(8,128)(2,1)S(1)} collective-permute-done((bf16[8,4096]{1,0:T(8,128)(2,1)S(1)}, bf16[8,4096]{1,0:T(8,128)(2,1)S(1)}, u32[]{:S(2)}, u32[]{:S(2)}) %collective-permute-start.2) | collective-permute-done | bytes 65568 | tf_op jit(solution)/shard_map/ppermute | solution.py:17
  32.2 0.8 collective-permute-start.3
  33.0 5.8 %collective-permute-done.3 = bf16[16,4096]{1,0:T(8,128)(2,1)S(1)} collective-permute-done((bf16[16,4096]{1,0:T(8,128)(2,1)S(1)}, bf16[16,4096]{1,0:T(8,128)(2,1)S(1)}, u32[]{:S(2)}, u32[]{:S(2)}) %collective-permute-start.3) | collective-permute-done | bytes 131104 | tf_op jit(solution)/shard_map/ppermute | solution.py:17
  38.9 1.9 collective-permute-start.4
  40.9 0.9 maximum_select_fusion.5
  42.1 7.1 %collective-permute-done.4 = bf16[32,4096]{1,0:T(8,128)(2,1)S(1)} collective-permute-done((bf16[32,4096]{1,0:T(8,128)(2,1)S(1)}, bf16[32,4096]{1,0:T(8,128)(2,1)S(1)}, u32[]{:S(2)}, u32[]{:S(2)}) %collective-permute-start.4) | collective-permute-done | bytes 262176 | tf_op jit(solution)/shard_map/ppermute | solution.py:17
  49.3 0.6 fusion.79
  49.9 0.4 fusion.71
  50.8 2.0 collective-permute-start.5
  52.9 1.8 multiply_reduce_fusion
  54.9 0.3 copy.190
  55.4 1.6 collective-permute-start.7
  56.9 0.5 collective-permute-start.14
  57.6 1.5 collective-permute-done.7
  59.1 1.5 collective-permute-done.14
  60.6 1.4 collective-permute-start.9
  62.1 0.6 collective-permute-start.15
  62.7 4.5 %collective-permute-done.6 = f32[32,32,128]{2,1,0:T(8,128)S(1)} collective-permute-done((f32[32,32,128]{2,1,0:T(8,128)S(1)}, f32[32,32,128]{2,1,0:T(8,128)S(1)}, u32[]{:S(2)}, u32[]{:S(2)}) %collective-permute-start.6) | collective-permute-done | bytes 524320 | tf_op jit(solution)/shard_map/ppermute | solution.py:17
  67.2 0.4 fusion.20
  67.6 2.6 %collective-permute-start.8 = (f32[16,32,128]{2,1,0:T(8,128)S(1)}, f32[16,32,128]{2,1,0:T(8,128)S(1)}, u32[]{:S(2)}, u32[]{:S(2)}) collective-permute-start(f32[16,32,128]{2,1,0:T(8,128)S(1)} %dynamic-slice_bitcast_fusion), channel_id=1, source_target_pairs={{0,4},{1,5},{2,6},{3,7},{4,0},{5,1},{6,2},{7,3},{8,12},{9,13},{10,... | collective-permute-start | bytes 786440 | tf_op jit(solution)/shard_map/ppermute | solution.py:17
  70.4 4.6 %collective-permute-done.8 = f32[16,32,128]{2,1,0:T(8,128)S(1)} collective-permute-done((f32[16,32,128]{2,1,0:T(8,128)S(1)}, f32[16,32,128]{2,1,0:T(8,128)S(1)}, u32[]{:S(2)}, u32[]{:S(2)}) %collective-permute-start.8) | collective-permute-done | bytes 262176 | tf_op jit(solution)/shard_map/ppermute | solution.py:17
  75.0 0.2 fusion.25
  75.2 1.2 collective-permute-start.10
  76.4 0.5 collective-permute-start.16
  76.9 3.3 %collective-permute-done.10 = f32[8,32,128]{2,1,0:T(8,128)S(1)} collective-permute-done((f32[8,32,128]{2,1,0:T(8,128)S(1)}, f32[8,32,128]{2,1,0:T(8,128)S(1)}, u32[]{:S(2)}, u32[]{:S(2)}) %collective-permute-start.10) | collective-permute-done | bytes 131104 | tf_op jit(solution)/shard_map/ppermute | solution.py:17
  80.5 1.2 collective-permute-done.12
  81.9 0.6 reshape.418
  82.8 0.2 select_reduce_fusion.1
  83.1 0.7 copy.158
  83.7 52.9 %all-gather.3.cloned.1.call-done = bf16[32,4,4096]{2,1,0:T(4,128)(2,1)} async-done(((bf16[1,4,4096]{2,1,0:T(4,128)(2,1)}), bf16[32,4,4096]{2,1,0:T(4,128)(2,1)}) %all-gather.3.cloned.1.call-update) | async-done | bytes 1048592 | tf_op jit(solution)/shard_map/all_gather | solution.py:164
  136.7 1.3 reshape.419
  138.0 1.0 convolution_convert_fusion.2
  139.0 3.6 %all-to-all-start.1 = ((bf16[32,4,128]{2,1,0:T(4,128)(2,1)}), bf16[32,4,128]{2,1,0:T(4,128)(2,1)S(1)}, u32[]{:S(2)}, u32[]{:S(2)}) async-start(bf16[32,4,128]{2,1,0:T(4,128)(2,1)} %bitcast.61), calls=%async_computation.1 | async-start | bytes 65536 | tf_op jit(solution)/shard_map/all_to_all | solution.py:168
  142.7 7.2 %all-to-all-done.1 = bf16[32,4,128]{2,1,0:T(4,128)(2,1)S(1)} async-done(((bf16[32,4,128]{2,1,0:T(4,128)(2,1)}), bf16[32,4,128]{2,1,0:T(4,128)(2,1)S(1)}, u32[]{:S(2)}, u32[]{:S(2)}) %all-to-all-start.1) | async-done | bytes 32800 | tf_op jit(solution)/shard_map/all_to_all | solution.py:168
  149.9 0.8 multiply_reduce_fusion.1
  150.7 0.4 convolution_convert_fusion.1
  151.0 0.2 broadcast_in_dim.98
  151.2 1.5 broadcast_in_dim.99
  152.8 2.8 %all-to-all-start.2 = ((bf16[32,4,4096]{2,1,0:T(4,128)(2,1)}), bf16[32,4,4096]{2,1,0:T(4,128)(2,1)S(1)}, u32[]{:S(2)}, u32[]{:S(2)}) async-start(bf16[32,4,4096]{2,1,0:T(4,128)(2,1)} %bitcast.64), calls=%async_computation.2 | async-start | bytes 2097152 | tf_op jit(solution)/shard_map/all_to_all | solution.py:203
  155.6 8.8 %copy.159 = bf16[1,4096,768]{1,2,0:T(8,128)(2,1)} copy(bf16[1,4096,768]{2,1,0:T(8,128)(2,1)} %param.30) | data formatting | bytes 12582912 | tf_op args[12]
  164.6 7.3 %fusion = bf16[4096,6,128]{0,2,1:T(8,128)(2,1)} fusion(bf16[4096,6,128]{0,2,1:T(8,128)(2,1)} %bitcast.243, f32[4096,6]{0,1:T(8,128)S(1)} %bitcast.256), kind=kLoop, calls=%fused_computation.3 | loop fusion | flops 9437184 | bytes 12681216 | tf_op jit(solution)/shard_map/convert_element_type | solution.py:24
  171.9 9.7 %all-to-all-done.2 = bf16[32,4,4096]{2,1,0:T(4,128)(2,1)S(1)} async-done(((bf16[32,4,4096]{2,1,0:T(4,128)(2,1)}), bf16[32,4,4096]{2,1,0:T(4,128)(2,1)S(1)}, u32[]{:S(2)}, u32[]{:S(2)}) %all-to-all-start.2) | async-done | bytes 1048608 | tf_op jit(solution)/shard_map/all_to_all | solution.py:203
  181.6 0.3 reshape.331
  181.9 5.1 %fusion.81 = f32[128,768]{1,0:T(8,128)S(1)} fusion(bf16[128,4096]{1,0:T(8,128)(2,1)S(1)} %reshape.331, bf16[4096,768]{0,1:T(8,128)(2,1)} %bitcast.244), kind=kOutput, calls=%fused_computation.162 | convolution fusion | flops 805306368 | bytes 7733248 | tf_op jit(solution)/shard_map/dot_general | solution.py:206
  187.1 1.8 broadcast_in_dim.103
  188.9 3.9 %convolution_convert_fusion = bf16[128,4096]{1,0:T(8,128)(2,1)S(1)} fusion(f32[48,8,32,128]{3,2,1,0:T(8,128)S(1)} %bitcast.245, bf16[1,384,4096]{2,1,0:T(8,128)(2,1)S(1)} %copy-done.1, f32[128,768]{1,0:T(8,128)S(1)} %fusion.81), kind=kOutput, calls=%fused_computation.6 | convolution fusion | flops 408190976 | bytes 10878976 | tf_op jit(solution)/shard_map/dot_general | solution.py:210
  192.8 0.4 reshape.335
  193.2 29.6 %all_to_all.42 = bf16[32,4,4096]{2,1,0:T(4,128)(2,1)S(1)} all-to-all(bf16[32,4,4096]{2,1,0:T(4,128)(2,1)S(1)} %reshape.335), channel_id=1, replica_groups=mesh['replica'=1,'ctx'=32] {'ctx'}, dimensions={0} | all-to-all | bytes 2097152 | tf_op jit(solution)/shard_map/all_to_all | solution.py:212
  222.8 0.2 convert.6
  223.0 0.3 slice_add_fusion
  223.3 0.4 add.224
  223.7 1.2 fusion.2
  (95 shorter events, 3.0 us)
Async XLA Ops:
  7.2 1.0 copy-start
  10.1 17.9 %collective-permute-start = (bf16[1,1,32,512]{3,2,1,0:T(8,128)(2,1)S(1)}, bf16[1,1,32,512]{3,2,1,0:T(8,128)(2,1)S(1)}, u32[]{:S(2)}, u32[]{:S(2)}) collective-permute-start(bf16[1,1,32,512]{3,2,1,0:T(8,128)(2,1)S(1)} %fusion.37), channel_id=1, source_target_pairs={{0,16},{1,17},{2,18},{3,19},{4,20},{5,21},{6,22},{7,23},{8,24},{9,... | collective-permute-start | bytes 98312 | tf_op jit(solution)/shard_map/ppermute | solution.py:17
  14.2 11.0 %collective-permute-start.1 = (bf16[4,4096]{1,0:T(4,128)(2,1)}, bf16[4,4096]{1,0:T(4,128)(2,1)S(1)}, u32[]{:S(2)}, u32[]{:S(2)}) collective-permute-start(bf16[4,4096]{1,0:T(4,128)(2,1)} %param.18), channel_id=1, source_target_pairs={{0,1},{1,0},{2,3},{3,2},{4,5},{5,4},{6,7},{7,6},{8,9},{9,8},{10,11... | collective-permute-start | bytes 98312 | tf_op jit(solution)/shard_map/ppermute | solution.py:17
  16.5 66.5 %all-to-all-start = ((bf16[128,32,128]{0,2,1:T(8,128)(2,1)}), bf16[128,32,128]{0,2,1:T(8,128)(2,1)S(1)}, u32[]{:S(2)}, u32[]{:S(2)}) async-start(bf16[128,32,128]{0,2,1:T(8,128)(2,1)} %bitcast.58), calls=%async_computation | async-start | bytes 2097152 | tf_op jit(solution)/shard_map/all_to_all | solution.py:162
  20.5 116.2 %all-gather.3.cloned.1.call-start = ((), (), s32[]{:S(2)}) async-start(), calls=%async_computation.4 | async-start | bytes 1081344 | tf_op jit(solution)/shard_map/all_gather | solution.py:164
  26.1 6.1 %collective-permute-start.2 = (bf16[8,4096]{1,0:T(8,128)(2,1)S(1)}, bf16[8,4096]{1,0:T(8,128)(2,1)S(1)}, u32[]{:S(2)}, u32[]{:S(2)}) collective-permute-start(bf16[8,4096]{1,0:T(8,128)(2,1)S(1)} %maximum_select_fusion.6), channel_id=1, source_target_pairs={{0,2},{1,3},{2,0},{3,1},{4,6},{5,7},{6,4},{7,5},{8,10},{9,11},{10,... | collective-permute-start | bytes 196616 | tf_op jit(solution)/shard_map/ppermute | solution.py:17
  32.2 6.6 %collective-permute-start.3 = (bf16[16,4096]{1,0:T(8,128)(2,1)S(1)}, bf16[16,4096]{1,0:T(8,128)(2,1)S(1)}, u32[]{:S(2)}, u32[]{:S(2)}) collective-permute-start(bf16[16,4096]{1,0:T(8,128)(2,1)S(1)} %maximum_select_fusion.4), channel_id=1, source_target_pairs={{0,4},{1,5},{2,6},{3,7},{4,0},{5,1},{6,2},{7,3},{8,12},{9,13},{10,... | collective-permute-start | bytes 393224 | tf_op jit(solution)/shard_map/ppermute | solution.py:17
  38.9 10.2 %collective-permute-start.4 = (bf16[32,4096]{1,0:T(8,128)(2,1)S(1)}, bf16[32,4096]{1,0:T(8,128)(2,1)S(1)}, u32[]{:S(2)}, u32[]{:S(2)}) collective-permute-start(bf16[32,4096]{1,0:T(8,128)(2,1)S(1)} %maximum_select_fusion.2), channel_id=1, source_target_pairs={{0,8},{1,9},{2,10},{3,11},{4,12},{5,13},{6,14},{7,15},{8,0},{9,1},... | collective-permute-start | bytes 786440 | tf_op jit(solution)/shard_map/ppermute | solution.py:17
  50.7 4.6 %collective-permute-start.13 = (f32[32,32]{1,0:T(8,128)S(1)}, f32[32,32]{1,0:T(8,128)S(1)}, u32[]{:S(2)}, u32[]{:S(2)}) collective-permute-start(f32[32,32]{1,0:T(8,128)S(1)} %bitcast.275), channel_id=1, source_target_pairs={{0,8},{1,9},{2,10},{3,11},{4,12},{5,13},{6,14},{7,15},{8,0},{9,1},... | collective-permute-start | bytes 12296 | tf_op jit(solution)/shard_map/ppermute | solution.py:17
  50.8 4.5 %collective-permute-start.5 = (f32[32,32]{1,0:T(8,128)S(1)}, f32[32,32]{1,0:T(8,128)S(1)}, u32[]{:S(2)}, u32[]{:S(2)}) collective-permute-start(f32[32,32]{1,0:T(8,128)S(1)} %bitcast.276), channel_id=1, source_target_pairs={{0,8},{1,9},{2,10},{3,11},{4,12},{5,13},{6,14},{7,15},{8,0},{9,1},... | collective-permute-start | bytes 12296 | tf_op jit(solution)/shard_map/ppermute | solution.py:17
  52.9 17.5 %copy-start.6 = (bf16[4,256]{1,0:T(4,128)(2,1)S(1)}, bf16[4,256]{1,0:T(4,128)(2,1)}, u32[]{:S(2)}) copy-start(bf16[4,256]{1,0:T(4,128)(2,1)} %param.20) | copy-start | bytes 6148
  52.9 29.7 %copy-start.4 = (s32[4,8]{1,0:T(4,128)S(1)}, s32[4,8]{1,0:T(4,128)}, u32[]{:S(2)}) copy-start(s32[4,8]{1,0:T(4,128)} %param.28) | copy-start | bytes 388
  54.7 87.9 %copy-start.7 = (f32[4,8]{1,0:T(4,128)S(1)}, f32[4,8]{1,0:T(4,128)}, u32[]{:S(2)}) copy-start(f32[4,8]{1,0:T(4,128)} %param.29) | copy-start | bytes 388
  54.7 95.2 %copy-start.2 = (bf16[4,4096]{1,0:T(4,128)(2,1)S(1)}, bf16[4,4096]{1,0:T(4,128)(2,1)}, u32[]{:S(2)}) copy-start(bf16[4,4096]{1,0:T(4,128)(2,1)} %param.25) | copy-start | bytes 98308
  54.8 95.9 %copy-start.3 = (f32[4096]{0:T(1024)S(1)}, f32[4096]{0:T(1024)}, u32[]{:S(2)}) copy-start(f32[4096]{0:T(1024)} %param.27) | copy-start | bytes 49156
  55.2 12.0 %collective-permute-start.6 = (f32[32,32,128]{2,1,0:T(8,128)S(1)}, f32[32,32,128]{2,1,0:T(8,128)S(1)}, u32[]{:S(2)}, u32[]{:S(2)}) collective-permute-start(f32[32,32,128]{2,1,0:T(8,128)S(1)} %bitcast.258), channel_id=1, source_target_pairs={{0,8},{1,9},{2,10},{3,11},{4,12},{5,13},{6,14},{7,15},{8,0},{9,1},... | collective-permute-start | bytes 1572872 | tf_op jit(solution)/shard_map/ppermute | solution.py:17
  55.4 3.7 %collective-permute-start.7 = (f32[16,32]{1,0:T(8,128)S(1)}, f32[16,32]{1,0:T(8,128)S(1)}, u32[]{:S(2)}, u32[]{:S(2)}) collective-permute-start(f32[16,32]{1,0:T(8,128)S(1)} %dynamic-slice_bitcast_fusion.4), channel_id=1, source_target_pairs={{0,4},{1,5},{2,6},{3,7},{4,0},{5,1},{6,2},{7,3},{8,12},{9,13},{10,... | collective-permute-start | bytes 6152 | tf_op jit(solution)/shard_map/ppermute | solution.py:17
  56.9 3.7 %collective-permute-start.14 = (f32[16,32]{1,0:T(8,128)S(1)}, f32[16,32]{1,0:T(8,128)S(1)}, u32[]{:S(2)}, u32[]{:S(2)}) collective-permute-start(f32[16,32]{1,0:T(8,128)S(1)} %dynamic-slice_bitcast_fusion.3), channel_id=1, source_target_pairs={{0,4},{1,5},{2,6},{3,7},{4,0},{5,1},{6,2},{7,3},{8,12},{9,13},{10,... | collective-permute-start | bytes 6152 | tf_op jit(solution)/shard_map/ppermute | solution.py:17
  60.6 9.7 %collective-permute-start.9 = (f32[8,32]{1,0:T(8,128)S(1)}, f32[8,32]{1,0:T(8,128)S(1)}, u32[]{:S(2)}, u32[]{:S(2)}) collective-permute-start(f32[8,32]{1,0:T(8,128)S(1)} %fusion.49), channel_id=1, source_target_pairs={{0,2},{1,3},{2,0},{3,1},{4,6},{5,7},{6,4},{7,5},{8,10},{9,11},{10,... | collective-permute-start | bytes 3080 | tf_op jit(solution)/shard_map/ppermute | solution.py:17
  62.1 8.3 %collective-permute-start.15 = (f32[8,32]{1,0:T(8,128)S(1)}, f32[8,32]{1,0:T(8,128)S(1)}, u32[]{:S(2)}, u32[]{:S(2)}) collective-permute-start(f32[8,32]{1,0:T(8,128)S(1)} %fusion.53), channel_id=1, source_target_pairs={{0,2},{1,3},{2,0},{3,1},{4,6},{5,7},{6,4},{7,5},{8,10},{9,11},{10,... | collective-permute-start | bytes 3080 | tf_op jit(solution)/shard_map/ppermute | solution.py:17
  67.6 7.4 %collective-permute-start.8 = (f32[16,32,128]{2,1,0:T(8,128)S(1)}, f32[16,32,128]{2,1,0:T(8,128)S(1)}, u32[]{:S(2)}, u32[]{:S(2)}) collective-permute-start(f32[16,32,128]{2,1,0:T(8,128)S(1)} %dynamic-slice_bitcast_fusion), channel_id=1, source_target_pairs={{0,4},{1,5},{2,6},{3,7},{4,0},{5,1},{6,2},{7,3},{8,12},{9,13},{10,... | collective-permute-start | bytes 786440 | tf_op jit(solution)/shard_map/ppermute | solution.py:17
  75.2 5.0 %collective-permute-start.10 = (f32[8,32,128]{2,1,0:T(8,128)S(1)}, f32[8,32,128]{2,1,0:T(8,128)S(1)}, u32[]{:S(2)}, u32[]{:S(2)}) collective-permute-start(f32[8,32,128]{2,1,0:T(8,128)S(1)} %dynamic-slice_bitcast_fusion.1), channel_id=1, source_target_pairs={{0,2},{1,3},{2,0},{3,1},{4,6},{5,7},{6,4},{7,5},{8,10},{9,11},{10,... | collective-permute-start | bytes 393224 | tf_op jit(solution)/shard_map/ppermute | solution.py:17
  76.4 4.1 %collective-permute-start.11 = (f32[4,32]{1,0:T(4,128)S(1)}, f32[4,32]{1,0:T(4,128)S(1)}, u32[]{:S(2)}, u32[]{:S(2)}) collective-permute-start(f32[4,32]{1,0:T(4,128)S(1)} %fusion.58), channel_id=1, source_target_pairs={{0,1},{1,0},{2,3},{3,2},{4,5},{5,4},{6,7},{7,6},{8,9},{9,8},{10,11... | collective-permute-start | bytes 1544 | tf_op jit(solution)/shard_map/ppermute | solution.py:17
  76.4 4.1 %collective-permute-start.16 = (f32[4,32]{1,0:T(4,128)S(1)}, f32[4,32]{1,0:T(4,128)S(1)}, u32[]{:S(2)}, u32[]{:S(2)}) collective-permute-start(f32[4,32]{1,0:T(4,128)S(1)} %fusion.64), channel_id=1, source_target_pairs={{0,1},{1,0},{2,3},{3,2},{4,5},{5,4},{6,7},{7,6},{8,9},{9,8},{10,11... | collective-permute-start | bytes 1544 | tf_op jit(solution)/shard_map/ppermute | solution.py:17
  80.4 1.3 collective-permute-start.12
  139.0 10.8 %all-to-all-start.1 = ((bf16[32,4,128]{2,1,0:T(4,128)(2,1)}), bf16[32,4,128]{2,1,0:T(4,128)(2,1)S(1)}, u32[]{:S(2)}, u32[]{:S(2)}) async-start(bf16[32,4,128]{2,1,0:T(4,128)(2,1)} %bitcast.61), calls=%async_computation.1 | async-start | bytes 65536 | tf_op jit(solution)/shard_map/all_to_all | solution.py:168
  152.8 28.8 %all-to-all-start.2 = ((bf16[32,4,4096]{2,1,0:T(4,128)(2,1)}), bf16[32,4,4096]{2,1,0:T(4,128)(2,1)S(1)}, u32[]{:S(2)}, u32[]{:S(2)}) async-start(bf16[32,4,4096]{2,1,0:T(4,128)(2,1)} %bitcast.64), calls=%async_computation.2 | async-start | bytes 2097152 | tf_op jit(solution)/shard_map/all_to_all | solution.py:203
  155.6 8.8 %copy-start.5 = (f32[1,32,6]{1,0,2:T(1,128)S(1)}, f32[1,32,6]{1,0,2:T(1,128)}, u32[]{:S(2)}) copy-start(f32[1,32,6]{1,0,2:T(1,128)} %param.31) | copy-start | bytes 2308
  155.6 9.0 %copy-start.8 = (f32[1,3,32]{2,0,1:T(1,128)S(1)}, f32[1,3,32]{2,0,1:T(1,128)}, u32[]{:S(2)}) copy-start(f32[1,3,32]{2,0,1:T(1,128)} %param.33) | copy-start | bytes 1156
  181.9 7.0 %copy-start.1 = (bf16[1,384,4096]{2,1,0:T(8,128)(2,1)S(1)}, bf16[1,384,4096]{2,1,0:T(8,128)(2,1)}, u32[]{:S(2)}) copy-start(bf16[1,384,4096]{2,1,0:T(8,128)(2,1)} %param.32) | copy-start | bytes 9437188
Sparse Core Ops, SparseCore 0:
  82.7 53.9 all-gather.2
where the time goes:
time: 233 us; the launch traced here: 232 us
  waiting for transfers between devices  104 us (45%)
  starting transfers between devices  29.8 us (13%)
  blocking collectives  29.6 us (13%)
  local copies, waits for them, and re-layouts  25.9 us (11%)
  between operations  16 us (7%)
  matrix products  14.2 us (6%)
  other arithmetic  12.7 us (5%)
    all_gather x1, waiting for transfers between devices, local(): lax.all_gather(attended, 'ctx', axis=0, tiled=True)  52.9 us
    ppermute x17, waiting for transfers between devices, swapped(): lax.ppermute(value, axis, [(i, i ^ 1 << distance) for i in range(lax.axis...  33.8 us
    all_to_all x1, blocking collectives, local(): lax.all_to_all(results, 'ctx', split_axis=0, concat_axis=0, tiled=True)  29.6 us
    ppermute x17, starting transfers between devices, swapped(): lax.ppermute(value, axis, [(i, i ^ 1 << distance) for i in range(lax.axis...  19.4 us
    unnamed x30, local copies, waits for them, and re-layouts  14.4 us
    all_to_all x1, waiting for transfers between devices, local(): lax.all_to_all(outgoing, 'ctx', split_axis=0, concat_axis=0, tiled=True)  9.66 us
    convert_element_type x1, other arithmetic, dequantize(): return (code_values.astype(jnp.float32) * spread).astype(jnp.bfloat16)  7.35 us
    all_to_all x1, waiting for transfers between devices, local(): lax.all_to_all(projected_cols.astype(jnp.bfloat16), 'ctx', split_axis=0,...  7.15 us
  transfers between devices with their start and end apart: 21, of which 12 were waited for; matrix products, arithmetic and copies ran while one was open for 13% of the time, Pallas kernels for 0%

commit v1 on v0

v1 whole, which is shorter than its diff:
```python
import functools
import math

import jax
import jax.numpy as jnp
from jax import lax
from jax.experimental import pallas as pl
from jax.experimental.pallas import tpu as pltpu
from jax.sharding import PartitionSpec as P

HD = 128
CAND = 64

NEG = -1e30
EPSILON = 1e-06
LOW = 2
MID = 4


def swapped(value, offset):
    return lax.ppermute(value, "ctx", [(i, i ^ offset) for i in range(lax.axis_size("ctx"))])


def stage_offsets(shards):
    low = [i for i in range(LOW)]
    mid = [i * LOW for i in range(MID)]
    high = [i * LOW * MID for i in range(shards // (LOW * MID))]
    return low, mid, high


def dequantize(code_values, scales):
    rows_per = code_values.shape[0] // scales.shape[0]
    cols_per = code_values.shape[1] // scales.shape[1]
    spread = jnp.repeat(jnp.repeat(scales, rows_per, axis=0), cols_per, axis=1)
    return (code_values.astype(jnp.float32) * spread).astype(jnp.bfloat16)


def pack_body(info, q, own_key, own_value, keys, values, *outs, feature, per_group):
    device = info[0]
    prefixes, ctx_local, _ = keys.shape
    rows = q.shape[0]
    kv_rows = prefixes * ctx_local

    def head_of(target):
        return (target * feature) // HD

    for zx, out in enumerate(outs):
        group = head_of(device ^ (zx * LOW * MID)) // per_group
        lanes = pl.ds(pl.multiple_of(group * HD, HD), HD)
        out[0:kv_rows, 0:HD] = keys[:, :, lanes].reshape(kv_rows, HD)
        out[0:kv_rows, HD : 2 * HD] = values[:, :, lanes].reshape(kv_rows, HD)
        for mx in range(MID):
            top = kv_rows + mx * rows
            for cx in range(LOW):
                head = head_of(device ^ (zx * LOW * MID + mx * LOW + cx))
                out[top : top + rows, cx * HD : (cx + 1) * HD] = q[:, pl.ds(pl.multiple_of(head * HD, HD), HD)]
        top = kv_rows + MID * rows
        out[top : top + rows, 0:HD] = own_key[:, lanes]
        out[top : top + rows, HD : 2 * HD] = own_value[:, lanes]


def repack_body(*refs, kv_rows, rows):
    outs = refs[-MID:]
    parts = refs[:-MID]
    for zx, part in enumerate(parts):
        for mx, out in enumerate(outs):
            out[zx, 0:kv_rows, :] = part[0:kv_rows, :]
            top = kv_rows + mx * rows
            own = kv_rows + MID * rows
            out[zx, kv_rows : kv_rows + rows, :] = part[top : top + rows, :]
            out[zx, kv_rows + rows : kv_rows + 2 * rows, :] = part[own : own + rows, :]


def attend_body(info, prefix_of, lengths, mine, other, w_out, keep, send, att, *, ctx_local, kv_rows, rows):
    device = info[0]
    mid, high = mine.shape[0], mine.shape[1]
    pieces = mid * high
    span = CAND // (LOW * mid * rows)
    scale = 1.0 / math.sqrt(HD)
    tile = 2 * rows
    pick_rows = lax.broadcasted_iota(jnp.int32, (CAND, CAND * 2), 0)
    pick_cols = lax.broadcasted_iota(jnp.int32, (CAND, CAND * 2), 1)
    wanted = pick_rows // rows * tile + pick_rows % rows
    pick_query = (pick_cols == wanted).astype(jnp.bfloat16)
    pick_own = (pick_cols == wanted + rows).astype(jnp.bfloat16)
    column = lax.broadcasted_iota(jnp.int32, (CAND, pieces * ctx_local), 1)
    piece = column // ctx_local
    within = column % ctx_local
    relative = (piece % high) * (LOW * MID) + (piece // high) * LOW
    own_group = device // (LOW * mid * span)
    for zg in range(high // span):
        prefix = prefix_of[own_group ^ zg]
        length = lengths[prefix]
        zs = slice(zg * span, (zg + 1) * span)
        tail_mine = mine[:, zs, kv_rows : kv_rows + tile, :].reshape(CAND, 2 * HD)
        tail_other = other[:, zs, kv_rows : kv_rows + tile, :].reshape(CAND, 2 * HD)
        padded = jnp.concatenate([tail_mine[:, 0:HD], tail_other[:, HD : 2 * HD]], axis=0)
        query = jnp.dot(pick_query, padded, preferred_element_type=jnp.float32)
        own = jnp.dot(
            pick_own, jnp.concatenate([tail_mine, tail_other], axis=0), preferred_element_type=jnp.float32
        )
        own_score = jnp.sum(query * own[:, 0:HD], axis=1, keepdims=True) * scale
        query = query.astype(jnp.bfloat16)
        top = own_score
        all_scores = []
        for cx, source in enumerate((mine, other)):
            at = pl.ds(pl.multiple_of(prefix * ctx_local, ctx_local), ctx_local)
            key = source[:, :, at, 0:HD].reshape(pieces * ctx_local, HD)
            scores = (
                lax.dot_general(query, key, (((1,), (1,)), ((), ())), preferred_element_type=jnp.float32) * scale
            )
            position = (device ^ (relative + cx)) * ctx_local + within
            scores = jnp.where(position < length, scores, NEG)
            top = jnp.maximum(top, jnp.max(scores, axis=1, keepdims=True))
            all_scores.append(scores)
        own_weight = jnp.exp(own_score - top)
        numer = own_weight * own[:, HD : 2 * HD]
        denom = own_weight
        for scores, source in zip(all_scores, (mine, other)):
            at = pl.ds(pl.multiple_of(prefix * ctx_local, ctx_local), ctx_local)
            value = source[:, :, at, HD : 2 * HD].reshape(pieces * ctx_local, HD)
            weights = jnp.exp(scores - top)
            denom = denom + jnp.sum(weights, axis=1, keepdims=True)
            numer = numer + jnp.dot(weights.astype(jnp.bfloat16), value, preferred_element_type=jnp.float32)
        attended = numer / denom
        chunk = span * rows
        att[:, zg * chunk : (zg + 1) * chunk, :] = attended.reshape(LOW * mid, chunk, HD)
    half = keep.shape[0]
    attended = att[...].reshape(2 * half, HD).astype(jnp.bfloat16)
    keep[...] = jnp.dot(attended[0:half], w_out[...], preferred_element_type=jnp.float32)
    send[...] = jnp.dot(attended[half:], w_out[...], preferred_element_type=jnp.float32).astype(jnp.bfloat16)


VMEM = pl.BlockSpec(memory_space=pltpu.VMEM)
SMEM = pl.BlockSpec(memory_space=pltpu.SMEM)


def scatter_sum(keep, send, mid, high):
    width = keep.shape[1]
    summed = keep + swapped(send, 1).astype(jnp.float32)
    for offsets in (mid, high):
        parts = summed.reshape(len(offsets), -1, width)
        total = parts[0]
        got = [swapped(parts[i].astype(jnp.bfloat16), offsets[i]) for i in range(1, len(offsets))]
        for item in got:
            total = total + item.astype(jnp.float32)
        summed = total
    return summed


def local(
    queries,
    own_key,
    own_value,
    cache_keys,
    cache_values,
    prefix_of_row,
    context_len,
    hidden_in,
    w_out,
    norm_gain,
    expert_ids,
    route_weights,
    gate_up_codes,
    gate_up_scales,
    down_codes,
    down_scales,
):
    shards = lax.axis_size("ctx")
    device = lax.axis_index("ctx")
    rows = queries.shape[0]
    width = hidden_in.shape[1]
    key_groups = own_key.shape[1] // HD
    head_count = queries.shape[1] // HD
    per_group = head_count // key_groups
    prefixes, ctx_local, _ = cache_keys.shape
    kv_rows = prefixes * ctx_local
    feature = w_out.shape[0]
    low, mid, high = stage_offsets(shards)
    info = device.reshape(1).astype(jnp.int32)
    block_prefix = prefix_of_row.reshape(-1, CAND)[:, 0]

    message_rows = kv_rows + MID * rows + 2 * rows
    messages = pl.pallas_call(
        functools.partial(pack_body, feature=feature, per_group=per_group),
        in_specs=[SMEM] + [VMEM] * 5,
        out_specs=[VMEM] * len(high),
        out_shape=[jax.ShapeDtypeStruct((message_rows, 2 * HD), jnp.bfloat16)] * len(high),
        name="pack",
    )(info, queries, own_key, own_value, cache_keys, cache_values)
    got = [messages[0]] + [swapped(messages[i], high[i]) for i in range(1, len(high))]
    piece = jax.ShapeDtypeStruct((len(high), kv_rows + 2 * rows, 2 * HD), jnp.bfloat16)
    messages = pl.pallas_call(
        functools.partial(repack_body, kv_rows=kv_rows, rows=rows),
        in_specs=[VMEM] * len(high),
        out_specs=[VMEM] * MID,
        out_shape=[piece] * MID,
        name="repack",
    )(*got)
    mine = jnp.stack([messages[0]] + [swapped(messages[i], mid[i]) for i in range(1, MID)], axis=0)
    other = swapped(mine, low[1])

    if feature < HD:
        w_full = lax.dynamic_update_slice(
            jnp.zeros((HD, w_out.shape[1]), w_out.dtype), w_out, ((device * feature) % HD, 0)
        )
    else:
        w_full = w_out
    half = shards * rows // 2
    keep, send = pl.pallas_call(
        functools.partial(attend_body, ctx_local=ctx_local, kv_rows=kv_rows, rows=rows),
        in_specs=[SMEM] * 3 + [VMEM] * 3,
        out_specs=[VMEM] * 2,
        out_shape=[
            jax.ShapeDtypeStruct((half, width), jnp.float32),
            jax.ShapeDtypeStruct((half, width), jnp.bfloat16),
        ],
        scratch_shapes=[pltpu.VMEM((LOW * MID, len(high) * rows, HD), jnp.float32)],
        name="attend",
    )(info, block_prefix, context_len, mine, other, w_full)

    projected = scatter_sum(keep, send, mid, high)
    mixed = hidden_in.astype(jnp.float32) + projected
    attention_out = mixed.astype(jnp.bfloat16)
    mean_square = jnp.mean(mixed * mixed, axis=-1, keepdims=True)
    normed = (mixed * lax.rsqrt(mean_square + EPSILON) * norm_gain).astype(jnp.bfloat16)

    experts_all = shards // 2
    hit = expert_ids[:, :, None] == jnp.arange(experts_all, dtype=jnp.int32)[None, None, :]
    combine = jnp.sum(jnp.where(hit, route_weights[:, :, None], 0.0), axis=1)
    coarse = lax.reduce_precision(combine, 8, 7)
    fine = combine - coarse
    extra = -(2 * experts_all) % HD
    tail = jnp.concatenate([coarse, fine, jnp.zeros((rows, extra), jnp.float32)], axis=1)
    held = jnp.concatenate([normed, tail.astype(jnp.bfloat16)], axis=1)
    for offsets in (high, mid, low):
        held = jnp.concatenate([held] + [swapped(held, o) for o in offsets[1:]], axis=0)
    lane = lax.broadcasted_iota(jnp.int32, (1, 2 * experts_all + extra), 1)
    expert = device // 2
    chosen = (lane == expert) | (lane == expert + experts_all)
    row_weight = jnp.sum(jnp.where(chosen, held[:, width:].astype(jnp.float32), 0.0), axis=1, keepdims=True)

    gate_up = dequantize(gate_up_codes[0], gate_up_scales[0])
    down_proj = dequantize(down_codes[0], down_scales[0])
    half_width = down_proj.shape[0]
    projected_in = jnp.dot(held[:, :width], gate_up, preferred_element_type=jnp.float32)
    activated = (jax.nn.silu(projected_in[:, :half_width]) * projected_in[:, half_width:]).astype(jnp.bfloat16)
    result = jnp.dot(activated, down_proj, preferred_element_type=jnp.float32) * row_weight
    expert_sum = scatter_sum(result[:half], result[half:].astype(jnp.bfloat16), mid, high)
    layer_out = (mixed + expert_sum).astype(jnp.bfloat16)
    return (attention_out, layer_out)


def solution(mesh):
    return jax.shard_map(
        local,
        mesh=mesh,
        in_specs=(
            P(("replica", "ctx"), None),
            P(("replica", "ctx"), None),
            P(("replica", "ctx"), None),
            P("replica", "ctx", None),
            P("replica", "ctx", None),
            P("replica"),
            P("replica"),
            P(("replica", "ctx"), None),
            P("ctx", None),
            P(),
            P(("replica", "ctx"), None),
            P(("replica", "ctx"), None),
            P("ctx", None, None),
            P("ctx", None, None),
            P("ctx", None, None),
            P("ctx", None, None),
        ),
        out_specs=(P(("replica", "ctx"), None), P(("replica", "ctx"), None)),
        check_vma=False,
    )
```

time: 233 us -> 120 us (0.52)
  waiting for transfers between devices: 104 us -> 42.2 us
  blocking collectives: 29.6 us -> 0 us
  between operations: 16 us -> 0.97 us
  local copies, waits for them, and re-layouts: 25.9 us -> 15 us
  Pallas kernels: 0 us -> 7.44 us
  matrix products: 14.2 us -> 9.1 us
  starting transfers between devices: 29.8 us -> 33.9 us
    all_gather x1 -> x0, waiting for transfers between devices: 52.9 us -> none  [local(): lax.all_gather(attended, 'ctx', axis=0, tiled=True)]
    all_to_all x1 -> x0, blocking collectives: 29.6 us -> none  [local(): lax.all_to_all(results, 'ctx', split_axis=0, concat_axis=0, tiled=True)]
    all_to_all x3 -> x0, waiting for transfers between devices: 16.8 us -> none  [the longest x1 9.66 us: local(): lax.all_to_all(outgoing, 'ctx', split_axis=0, concat_axis=0, tiled=True)]
    ppermute x17 -> x28, starting transfers between devices: 19.4 us -> 33.9 us  [swapped(): lax.ppermute(value, 'ctx', [(i, i ^ offset) for i in range(lax.axis_size(...]
    all_to_all x3 -> x0, starting transfers between devices: 10.3 us -> none  [the longest x1 3.94 us: local(): lax.all_to_all(w_out, 'ctx', split_axis=1, concat_axis=0, tiled=True)]
    ppermute x17 -> x28, waiting for transfers between devices: 33.8 us -> 42.2 us  [swapped(): lax.ppermute(value, 'ctx', [(i, i ^ offset) for i in range(lax.axis_size(...]
    pallas_call x0 -> x3, Pallas kernels: none -> 7.44 us  [the longest x1 3.99 us: local(): pl.pallas_call(functools.partial(attend_body, ctx_local=ctx_local, kv_row...]
    dot_general x7 -> x1, matrix products: 10.3 us -> 5.13 us  [local(): jnp.dot(held[:, :width], gate_up, preferred_element_type=jnp.float32)]
  transfers between devices with their start and end apart: 21 -> 28, of which waited for: 12 -> 21; matrix products, arithmetic and copies ran while one was open for 13% -> 15% of each run, Pallas kernels for 0% -> 0%
where the time goes in v1:
time: 120 us
  waiting for transfers between devices  42.2 us (35%)
  starting transfers between devices  33.9 us (28%)
  local copies, waits for them, and re-layouts  15 us (12%)
  other arithmetic  11.2 us (9%)
  matrix products  9.1 us (8%)
  Pallas kernels  7.44 us (6%)
    ppermute x28, waiting for transfers between devices, swapped(): lax.ppermute(value, 'ctx', [(i, i ^ offset) for i in range(lax.axis_size(...  42.2 us
    ppermute x28, starting transfers between devices, swapped(): lax.ppermute(value, 'ctx', [(i, i ^ offset) for i in range(lax.axis_size(...  33.9 us
    unnamed x29, local copies, waits for them, and re-layouts  10.4 us
    convert_element_type x1, other arithmetic, dequantize(): return (code_values.astype(jnp.float32) * spread).astype(jnp.bfloat16)  7.31 us
    dot_general x1, matrix products, local(): jnp.dot(held[:, :width], gate_up, preferred_element_type=jnp.float32)  5.13 us
    pallas_call x1, Pallas kernels, local(): pl.pallas_call(functools.partial(attend_body, ctx_local=ctx_local, kv_row...  3.99 us
    dot_general x1, matrix products, local(): jnp.dot(activated, down_proj, preferred_element_type=jnp.float32)  3.97 us
  transfers between devices with their start and end apart: 28, of which 21 were waited for; matrix products, arithmetic and copies ran while one was open for 15% of the time, Pallas kernels for 0%

profile of v1, /device:TPU:0, one launch (start us, length us, event | category | flops | bytes accessed | tf_op | source)
XLA Modules:
  0.0 119.8 jit_solution(1544814794397543998)
XLA Ops:
  0.7 1.7 %pack.1 = (bf16[88,256]{1,0:T(8,128)(2,1)}, bf16[88,256]{1,0:T(8,128)(2,1)}, bf16[88,256]{1,0:T(8,128)(2,1)}, bf16[88,256]{1,0:T(8,128)(2,1)}) custom-call(s32[1]{0:T(128)} %bitcast.info, bf16[4,4096]{1,0:T(4,128)(2,1)} %q.1, bf16[4,256]{1,0:T(4,128)(2,1)} %own_key.1, bf16[4,256]{1,0:T(4,128)(2,1)} %own_value.1, bf16[2,32,256]{2,1,0:T(8,128)(2,1)} %keys.1, ...), custom_call_target="tpu_custom_call" | custom-call | tf_op jit(solution)/shard_map/pack/pallas_call | solution.py:184
  2.4 3.1 %collective-permute-start = (bf16[88,256]{1,0:T(8,128)(2,1)}, bf16[88,256]{1,0:T(8,128)(2,1)S(1)}, u32[]{:S(2)}, u32[]{:S(2)}) collective-permute-start(bf16[88,256]{1,0:T(8,128)(2,1)} %get-tuple-element.13), channel_id=1, source_target_pairs={{0,8},{1,9},{2,10},{3,11},{4,12},{5,13},{6,14},{7,15},{8,0},{9,1},... | collective-permute-start | bytes 135176 | tf_op jit(solution)/shard_map/ppermute | solution.py:21
  5.4 2.6 %collective-permute-start.1 = (bf16[88,256]{1,0:T(8,128)(2,1)}, bf16[88,256]{1,0:T(8,128)(2,1)S(1)}, u32[]{:S(2)}, u32[]{:S(2)}) collective-permute-start(bf16[88,256]{1,0:T(8,128)(2,1)} %get-tuple-element.14), channel_id=1, source_target_pairs={{0,16},{1,17},{2,18},{3,19},{4,20},{5,21},{6,22},{7,23},{8,24},{9,... | collective-permute-start | bytes 135176 | tf_op jit(solution)/shard_map/ppermute | solution.py:21
  8.0 3.4 %collective-permute-done.1.refs_2_ = bf16[88,256]{1,0:T(8,128)(2,1)S(1)} collective-permute-done((bf16[88,256]{1,0:T(8,128)(2,1)}, bf16[88,256]{1,0:T(8,128)(2,1)S(1)}, u32[]{:S(2)}, u32[]{:S(2)}) %collective-permute-start.1) | collective-permute-done | bytes 45088 | tf_op jit(solution)/shard_map/ppermute | solution.py:21
  11.5 2.6 %collective-permute-done.2.refs_3_ = bf16[88,256]{1,0:T(8,128)(2,1)S(1)} collective-permute-done((bf16[88,256]{1,0:T(8,128)(2,1)}, bf16[88,256]{1,0:T(8,128)(2,1)S(1)}, u32[]{:S(2)}, u32[]{:S(2)}) %collective-permute-start.2) | collective-permute-done | bytes 45088 | tf_op jit(solution)/shard_map/ppermute | solution.py:21
  14.1 0.6 copy-done.5
  14.7 1.7 %repack.1 = (bf16[4,72,256]{2,1,0:T(8,128)(2,1)}, bf16[4,72,256]{2,1,0:T(8,128)(2,1)}, bf16[4,72,256]{2,1,0:T(8,128)(2,1)}, bf16[4,72,256]{2,1,0:T(8,128)(2,1)}) custom-call(bf16[88,256]{1,0:T(8,128)(2,1)} %get-tuple-element.12.refs_0_, bf16[88,256]{1,0:T(8,128)(2,1)} %copy-done.3, bf16[88,256]{1,0:T(8,128)(2,1)} %copy-done.4, bf16[88,256]{1,0:T(8,128)(2,1)} %copy-done.5), custom_call_target="tpu_custom_call" | custom-call | tf_op jit(solution)/shard_map/repack/pallas_call | solution.py:193
  16.4 1.5 %collective-permute-start.3 = (bf16[4,72,256]{2,1,0:T(8,128)(2,1)}, bf16[4,72,256]{2,1,0:T(8,128)(2,1)S(1)}, u32[]{:S(2)}, u32[]{:S(2)}) collective-permute-start(bf16[4,72,256]{2,1,0:T(8,128)(2,1)} %get-tuple-element.17), channel_id=1, source_target_pairs={{0,2},{1,3},{2,0},{3,1},{4,6},{5,7},{6,4},{7,5},{8,10},{9,11},{10,... | collective-permute-start | bytes 442376 | tf_op jit(solution)/shard_map/ppermute | solution.py:21
  17.9 1.5 %collective-permute-start.4 = (bf16[4,72,256]{2,1,0:T(8,128)(2,1)}, bf16[4,72,256]{2,1,0:T(8,128)(2,1)S(1)}, u32[]{:S(2)}, u32[]{:S(2)}) collective-permute-start(bf16[4,72,256]{2,1,0:T(8,128)(2,1)} %get-tuple-element.18), channel_id=1, source_target_pairs={{0,4},{1,5},{2,6},{3,7},{4,0},{5,1},{6,2},{7,3},{8,12},{9,13},{10,... | collective-permute-start | bytes 442376 | tf_op jit(solution)/shard_map/ppermute | solution.py:21
  19.5 0.5 collective-permute-start.5
  19.9 3.1 %collective-permute-done.3 = bf16[4,72,256]{2,1,0:T(8,128)(2,1)S(1)} collective-permute-done((bf16[4,72,256]{2,1,0:T(8,128)(2,1)}, bf16[4,72,256]{2,1,0:T(8,128)(2,1)S(1)}, u32[]{:S(2)}, u32[]{:S(2)}) %collective-permute-start.3) | collective-permute-done | bytes 147488 | tf_op jit(solution)/shard_map/ppermute | solution.py:21
  23.0 2.8 %collective-permute-done.4 = bf16[4,72,256]{2,1,0:T(8,128)(2,1)S(1)} collective-permute-done((bf16[4,72,256]{2,1,0:T(8,128)(2,1)}, bf16[4,72,256]{2,1,0:T(8,128)(2,1)S(1)}, u32[]{:S(2)}, u32[]{:S(2)}) %collective-permute-start.4) | collective-permute-done | bytes 147488 | tf_op jit(solution)/shard_map/ppermute | solution.py:21
  25.8 1.0 pad_maximum_fusion.mine
  26.9 0.8 reshape.86
  27.7 0.6 slice_reduce_fusion.prefix_of
  28.3 0.6 collective-permute-done.6.other
  28.9 0.8 copy-done.2
  29.7 4.0 %attend.1 = (f32[64,4096]{1,0:T(8,128)}, bf16[64,4096]{1,0:T(8,128)(2,1)}) custom-call(s32[1]{0:T(128)} %bitcast.info, s32[2]{0:T(128)} %slice_reduce_fusion.prefix_of, s32[2]{0:T(128)} %lengths.1, bf16[4,4,72,256]{3,2,1,0:T(8,128)(2,1)} %copy-done.1, bf16[4,4,72,256]{3,2,1,0:T(8,128)(2,1)} %copy-done.2, bf16[128,4096]{1,0:T(8,128)(2,1)} %w_out.1), custom_call_target="tpu_custom_call" | custom-call | tf_op jit(solution)/shard_map/attend/pallas_call | solution.py:210
  33.7 0.1 collective-permute-start.7
  33.9 2.0 %collective-permute-done.7 = bf16[64,4096]{1,0:T(8,128)(2,1)S(1)} collective-permute-done((bf16[64,4096]{1,0:T(8,128)(2,1)}, bf16[64,4096]{1,0:T(8,128)(2,1)S(1)}, u32[]{:S(2)}, u32[]{:S(2)}) %collective-permute-start.7) | collective-permute-done | bytes 524320 | tf_op jit(solution)/shard_map/ppermute | solution.py:21
  35.9 1.3 %fusion.28 = (bf16[64,4096]{1,0:T(8,128)(2,1)S(1)}, f32[64,4096]{1,0:T(8,128)S(1)}) fusion(f32[64,4096]{1,0:T(8,128)} %get-tuple-element.20, bf16[64,4096]{1,0:T(8,128)(2,1)S(1)} %collective-permute-done.7), kind=kLoop, calls=%fused_computation.50 | loop fusion | flops 786432 | bytes 3145728 | tf_op jit(solution)/shard_map/convert.17
  37.2 0.8 collective-permute-start.10
  38.0 1.8 %collective-permute-start.8 = (bf16[16,4096]{1,0:T(8,128)(2,1)S(1)}, bf16[16,4096]{1,0:T(8,128)(2,1)S(1)}, u32[]{:S(2)}, u32[]{:S(2)}) collective-permute-start(bf16[16,4096]{1,0:T(8,128)(2,1)S(1)} %get-tuple-element.35), channel_id=1, source_target_pairs={{0,2},{1,3},{2,0},{3,1},{4,6},{5,7},{6,4},{7,5},{8,10},{9,11},{10,... | collective-permute-start | bytes 393224 | tf_op jit(solution)/shard_map/ppermute | solution.py:21
  39.8 1.0 collective-permute-start.9
  40.9 3.7 %collective-permute-done.10 = bf16[16,4096]{1,0:T(8,128)(2,1)S(1)} collective-permute-done((bf16[16,4096]{1,0:T(8,128)(2,1)S(1)}, bf16[16,4096]{1,0:T(8,128)(2,1)S(1)}, u32[]{:S(2)}, u32[]{:S(2)}) %collective-permute-start.10) | collective-permute-done | bytes 131104 | tf_op jit(solution)/shard_map/ppermute | solution.py:21
  44.6 1.5 %collective-permute-done.8 = bf16[16,4096]{1,0:T(8,128)(2,1)S(1)} collective-permute-done((bf16[16,4096]{1,0:T(8,128)(2,1)S(1)}, bf16[16,4096]{1,0:T(8,128)(2,1)S(1)}, u32[]{:S(2)}, u32[]{:S(2)}) %collective-permute-start.8) | collective-permute-done | bytes 131104 | tf_op jit(solution)/shard_map/ppermute | solution.py:21
  46.1 0.5 collective-permute-done.9
  46.8 1.3 %collective-permute-start.12 = (bf16[4,4096]{1,0:T(4,128)(2,1)S(1)}, bf16[4,4096]{1,0:T(4,128)(2,1)S(1)}, u32[]{:S(2)}, u32[]{:S(2)}) collective-permute-start(bf16[4,4096]{1,0:T(4,128)(2,1)S(1)} %get-tuple-element.43), channel_id=1, source_target_pairs={{0,16},{1,17},{2,18},{3,19},{4,20},{5,21},{6,22},{7,23},{8,24},{9,... | collective-permute-start | bytes 98312 | tf_op jit(solution)/shard_map/ppermute | solution.py:21
  48.0 3.1 %collective-permute-start.13 = (bf16[4,4096]{1,0:T(4,128)(2,1)S(1)}, bf16[4,4096]{1,0:T(4,128)(2,1)S(1)}, u32[]{:S(2)}, u32[]{:S(2)}) collective-permute-start(bf16[4,4096]{1,0:T(4,128)(2,1)S(1)} %get-tuple-element.42), channel_id=1, source_target_pairs={{0,24},{1,25},{2,26},{3,27},{4,28},{5,29},{6,30},{7,31},{8,16},{9,... | collective-permute-start | bytes 98312 | tf_op jit(solution)/shard_map/ppermute | solution.py:21
  51.2 1.2 collective-permute-done.12
  52.4 1.4 %collective-permute-done.13 = bf16[4,4096]{1,0:T(4,128)(2,1)S(1)} collective-permute-done((bf16[4,4096]{1,0:T(4,128)(2,1)S(1)}, bf16[4,4096]{1,0:T(4,128)(2,1)S(1)}, u32[]{:S(2)}, u32[]{:S(2)}) %collective-permute-start.13) | collective-permute-done | bytes 32800 | tf_op jit(solution)/shard_map/ppermute | solution.py:21
  53.8 0.2 multiply_reduce_fusion
  54.0 0.1 concatenate.17
  54.2 3.7 %collective-permute-start.15 = (bf16[4,4224]{1,0:T(4,128)(2,1)S(1)}, bf16[4,4224]{1,0:T(4,128)(2,1)S(1)}, u32[]{:S(2)}, u32[]{:S(2)}) collective-permute-start(bf16[4,4224]{1,0:T(4,128)(2,1)S(1)} %concatenate.17), channel_id=1, source_target_pairs={{0,16},{1,17},{2,18},{3,19},{4,20},{5,21},{6,22},{7,23},{8,24},{9,... | collective-permute-start | bytes 101384 | tf_op jit(solution)/shard_map/ppermute | solution.py:21
  57.8 0.7 collective-permute-start.16
  58.6 1.2 collective-permute-done.15
  59.7 3.8 %collective-permute-done.16 = bf16[4,4224]{1,0:T(4,128)(2,1)S(1)} collective-permute-done((bf16[4,4224]{1,0:T(4,128)(2,1)S(1)}, bf16[4,4224]{1,0:T(4,128)(2,1)S(1)}, u32[]{:S(2)}, u32[]{:S(2)}) %collective-permute-start.16) | collective-permute-done | bytes 33824 | tf_op jit(solution)/shard_map/ppermute | solution.py:21
  63.6 0.5 collective-permute-start.17
  64.1 0.9 collective-permute-start.18
  65.0 2.2 %collective-permute-start.19 = (bf16[16,4224]{1,0:T(8,128)(2,1)S(1)}, bf16[16,4224]{1,0:T(8,128)(2,1)S(1)}, u32[]{:S(2)}, u32[]{:S(2)}) collective-permute-start(bf16[16,4224]{1,0:T(8,128)(2,1)S(1)} %pad_maximum_fusion.1), channel_id=1, source_target_pairs={{0,6},{1,7},{2,4},{3,5},{4,2},{5,3},{6,0},{7,1},{8,14},{9,15},{10,... | collective-permute-start | bytes 405512 | tf_op jit(solution)/shard_map/ppermute | solution.py:21
  67.2 1.5 %collective-permute-done.17 = bf16[16,4224]{1,0:T(8,128)(2,1)S(1)} collective-permute-done((bf16[16,4224]{1,0:T(8,128)(2,1)S(1)}, bf16[16,4224]{1,0:T(8,128)(2,1)S(1)}, u32[]{:S(2)}, u32[]{:S(2)}) %collective-permute-start.17) | collective-permute-done | bytes 135200 | tf_op jit(solution)/shard_map/ppermute | solution.py:21
  68.7 0.4 collective-permute-done.18
  69.1 1.8 %collective-permute-done.19 = bf16[16,4224]{1,0:T(8,128)(2,1)S(1)} collective-permute-done((bf16[16,4224]{1,0:T(8,128)(2,1)S(1)}, bf16[16,4224]{1,0:T(8,128)(2,1)S(1)}, u32[]{:S(2)}, u32[]{:S(2)}) %collective-permute-start.19) | collective-permute-done | bytes 135200 | tf_op jit(solution)/shard_map/ppermute | solution.py:21
  70.9 0.5 concatenate.19
  71.5 8.7 %copy.20 = bf16[1,4096,768]{1,2,0:T(8,128)(2,1)} copy(bf16[1,4096,768]{2,1,0:T(8,128)(2,1)} %param.28) | data formatting | bytes 12582912 | tf_op args[12]
  80.4 7.3 %fusion = bf16[4096,768]{0,1:T(8,128)(2,1)} fusion(bf16[1,4096,768]{1,2,0:T(8,128)(2,1)} %copy.20, f32[4096,6]{0,1:T(8,128)S(1)} %bitcast.39), kind=kLoop, calls=%fused_computation.1 | loop fusion | flops 9437184 | bytes 12681216 | tf_op jit(solution)/shard_map/convert_element_type | solution.py:35
  87.8 0.6 concatenate.20
  88.4 5.1 %fusion.4 = f32[128,768]{1,0:T(8,128)S(1)} fusion(bf16[4096,768]{0,1:T(8,128)(2,1)} %fusion, bf16[128,4224]{1,0:T(8,128)(2,1)S(1)} %concatenate.20), kind=kOutput, calls=%fused_computation.8 | convolution fusion | flops 805306368 | bytes 7733248 | tf_op jit(solution)/shard_map/dot_general | solution.py:246
  93.5 0.1 select_reduce_fusion
  93.6 1.8 %broadcast_in_dim.51 = f32[384,32,128]{2,1,0:T(8,128)S(1)} broadcast(f32[384,32]{1,0:T(8,128)S(1)} %bitcast.38), dimensions={0,1} | broadcast | bytes 6340608 | tf_op jit(solution)/shard_map/broadcast_in_dim | solution.py:34
  95.4 4.0 %convolution_multiply_fusion = f32[128,4096]{1,0:T(8,128)S(1)} fusion(f32[48,8,32,128]{3,2,1,0:T(8,128)S(1)} %bitcast.37, bf16[1,384,4096]{2,1,0:T(8,128)(2,1)S(1)} %copy-done, f32[128]{0:T(128)S(1)} %select_reduce_fusion, f32[128,768]{1,0:T(8,128)S(1)} %fusion.4), kind=kOutput, calls=%fused_computation.4 | convolution fusion | flops 408190976 | bytes 11928064 | tf_op jit(solution)/shard_map/dot_general | solution.py:248
  99.5 0.6 collective-permute-start.21
  100.0 1.5 %collective-permute-done.21 = bf16[64,4096]{1,0:T(8,128)(2,1)S(1)} collective-permute-done((bf16[64,4096]{1,0:T(8,128)(2,1)S(1)}, bf16[64,4096]{1,0:T(8,128)(2,1)S(1)}, u32[]{:S(2)}, u32[]{:S(2)}) %collective-permute-start.21) | collective-permute-done | bytes 524320 | tf_op jit(solution)/shard_map/ppermute | solution.py:21
  101.6 0.2 fusion.24
  101.8 1.8 %collective-permute-start.22 = (bf16[16,4096]{1,0:T(8,128)(2,1)S(1)}, bf16[16,4096]{1,0:T(8,128)(2,1)S(1)}, u32[]{:S(2)}, u32[]{:S(2)}) collective-permute-start(bf16[16,4096]{1,0:T(8,128)(2,1)S(1)} %get-tuple-element.32), channel_id=1, source_target_pairs={{0,2},{1,3},{2,0},{3,1},{4,6},{5,7},{6,4},{7,5},{8,10},{9,11},{10,... | collective-permute-start | bytes 393224 | tf_op jit(solution)/shard_map/ppermute | solution.py:21
  103.6 1.0 collective-permute-start.23
  104.6 0.7 collective-permute-start.24
  105.3 2.5 %collective-permute-done.22 = bf16[16,4096]{1,0:T(8,128)(2,1)S(1)} collective-permute-done((bf16[16,4096]{1,0:T(8,128)(2,1)S(1)}, bf16[16,4096]{1,0:T(8,128)(2,1)S(1)}, u32[]{:S(2)}, u32[]{:S(2)}) %collective-permute-start.22) | collective-permute-done | bytes 131104 | tf_op jit(solution)/shard_map/ppermute | solution.py:21
  107.8 4.1 %collective-permute-done.23 = bf16[16,4096]{1,0:T(8,128)(2,1)S(1)} collective-permute-done((bf16[16,4096]{1,0:T(8,128)(2,1)S(1)}, bf16[16,4096]{1,0:T(8,128)(2,1)S(1)}, u32[]{:S(2)}, u32[]{:S(2)}) %collective-permute-start.23) | collective-permute-done | bytes 131104 | tf_op jit(solution)/shard_map/ppermute | solution.py:21
  112.1 1.3 %collective-permute-start.26 = (bf16[4,4096]{1,0:T(4,128)(2,1)S(1)}, bf16[4,4096]{1,0:T(4,128)(2,1)S(1)}, u32[]{:S(2)}, u32[]{:S(2)}) collective-permute-start(bf16[4,4096]{1,0:T(4,128)(2,1)S(1)} %get-tuple-element.40), channel_id=1, source_target_pairs={{0,16},{1,17},{2,18},{3,19},{4,20},{5,21},{6,22},{7,23},{8,24},{9,... | collective-permute-start | bytes 98312 | tf_op jit(solution)/shard_map/ppermute | solution.py:21
  113.4 3.1 %collective-permute-start.27 = (bf16[4,4096]{1,0:T(4,128)(2,1)S(1)}, bf16[4,4096]{1,0:T(4,128)(2,1)S(1)}, u32[]{:S(2)}, u32[]{:S(2)}) collective-permute-start(bf16[4,4096]{1,0:T(4,128)(2,1)S(1)} %get-tuple-element.39), channel_id=1, source_target_pairs={{0,24},{1,25},{2,26},{3,27},{4,28},{5,29},{6,30},{7,31},{8,16},{9,... | collective-permute-start | bytes 98312 | tf_op jit(solution)/shard_map/ppermute | solution.py:21
  116.5 0.5 collective-permute-done.26
  117.0 2.1 %collective-permute-done.27 = bf16[4,4096]{1,0:T(4,128)(2,1)S(1)} collective-permute-done((bf16[4,4096]{1,0:T(4,128)(2,1)S(1)}, bf16[4,4096]{1,0:T(4,128)(2,1)S(1)}, u32[]{:S(2)}, u32[]{:S(2)}) %collective-permute-start.27) | collective-permute-done | bytes 32800 | tf_op jit(solution)/shard_map/ppermute | solution.py:21
  119.1 0.7 fusion.16
  (54 shorter events, 1.2 us)
Async XLA Ops:
  0.6 40.2 %copy-start.10 = (s32[4,8]{1,0:T(4,128)S(1)}, s32[4,8]{1,0:T(4,128)}, u32[]{:S(2)}) copy-start(s32[4,8]{1,0:T(4,128)} %param.26) | copy-start | bytes 388
  0.6 40.2 %copy-start.9 = (f32[4,8]{1,0:T(4,128)S(1)}, f32[4,8]{1,0:T(4,128)}, u32[]{:S(2)}) copy-start(f32[4,8]{1,0:T(4,128)} %param.27) | copy-start | bytes 388
  0.7 53.1 %copy-start.6 = (bf16[4,4096]{1,0:T(4,128)(2,1)S(1)}, bf16[4,4096]{1,0:T(4,128)(2,1)}, u32[]{:S(2)}) copy-start(bf16[4,4096]{1,0:T(4,128)(2,1)} %param.23) | copy-start | bytes 98308
  0.7 53.3 %copy-start.7 = (f32[4096]{0:T(1024)S(1)}, f32[4096]{0:T(1024)}, u32[]{:S(2)}) copy-start(f32[4096]{0:T(1024)} %param.25) | copy-start | bytes 49156
  2.4 5.6 %collective-permute-start = (bf16[88,256]{1,0:T(8,128)(2,1)}, bf16[88,256]{1,0:T(8,128)(2,1)S(1)}, u32[]{:S(2)}, u32[]{:S(2)}) collective-permute-start(bf16[88,256]{1,0:T(8,128)(2,1)} %get-tuple-element.13), channel_id=1, source_target_pairs={{0,8},{1,9},{2,10},{3,11},{4,12},{5,13},{6,14},{7,15},{8,0},{9,1},... | collective-permute-start | bytes 135176 | tf_op jit(solution)/shard_map/ppermute | solution.py:21
  5.4 6.0 %collective-permute-start.1 = (bf16[88,256]{1,0:T(8,128)(2,1)}, bf16[88,256]{1,0:T(8,128)(2,1)S(1)}, u32[]{:S(2)}, u32[]{:S(2)}) collective-permute-start(bf16[88,256]{1,0:T(8,128)(2,1)} %get-tuple-element.14), channel_id=1, source_target_pairs={{0,16},{1,17},{2,18},{3,19},{4,20},{5,21},{6,22},{7,23},{8,24},{9,... | collective-permute-start | bytes 135176 | tf_op jit(solution)/shard_map/ppermute | solution.py:21
  8.0 6.1 %collective-permute-start.2 = (bf16[88,256]{1,0:T(8,128)(2,1)}, bf16[88,256]{1,0:T(8,128)(2,1)S(1)}, u32[]{:S(2)}, u32[]{:S(2)}) collective-permute-start(bf16[88,256]{1,0:T(8,128)(2,1)} %get-tuple-element.15), channel_id=1, source_target_pairs={{0,24},{1,25},{2,26},{3,27},{4,28},{5,29},{6,30},{7,31},{8,16},{9,... | collective-permute-start | bytes 135176 | tf_op jit(solution)/shard_map/ppermute | solution.py:21
  8.0 6.1 %copy-start.3 = (bf16[88,256]{1,0:T(8,128)(2,1)}, bf16[88,256]{1,0:T(8,128)(2,1)S(1)}, u32[]{:S(2)}) copy-start(bf16[88,256]{1,0:T(8,128)(2,1)S(1)} %collective-permute-done.refs_1_) | copy-start | bytes 135172
  11.4 2.6 %copy-start.4 = (bf16[88,256]{1,0:T(8,128)(2,1)}, bf16[88,256]{1,0:T(8,128)(2,1)S(1)}, u32[]{:S(2)}) copy-start(bf16[88,256]{1,0:T(8,128)(2,1)S(1)} %collective-permute-done.1.refs_2_) | copy-start | bytes 135172
  14.1 0.6 copy-start.5
  16.4 6.6 %collective-permute-start.3 = (bf16[4,72,256]{2,1,0:T(8,128)(2,1)}, bf16[4,72,256]{2,1,0:T(8,128)(2,1)S(1)}, u32[]{:S(2)}, u32[]{:S(2)}) collective-permute-start(bf16[4,72,256]{2,1,0:T(8,128)(2,1)} %get-tuple-element.17), channel_id=1, source_target_pairs={{0,2},{1,3},{2,0},{3,1},{4,6},{5,7},{6,4},{7,5},{8,10},{9,11},{10,... | collective-permute-start | bytes 442376 | tf_op jit(solution)/shard_map/ppermute | solution.py:21
  17.9 7.9 %collective-permute-start.4 = (bf16[4,72,256]{2,1,0:T(8,128)(2,1)}, bf16[4,72,256]{2,1,0:T(8,128)(2,1)S(1)}, u32[]{:S(2)}, u32[]{:S(2)}) collective-permute-start(bf16[4,72,256]{2,1,0:T(8,128)(2,1)} %get-tuple-element.18), channel_id=1, source_target_pairs={{0,4},{1,5},{2,6},{3,7},{4,0},{5,1},{6,2},{7,3},{8,12},{9,13},{10,... | collective-permute-start | bytes 442376 | tf_op jit(solution)/shard_map/ppermute | solution.py:21
  19.5 6.4 %collective-permute-start.5 = (bf16[4,72,256]{2,1,0:T(8,128)(2,1)}, bf16[4,72,256]{2,1,0:T(8,128)(2,1)S(1)}, u32[]{:S(2)}, u32[]{:S(2)}) collective-permute-start(bf16[4,72,256]{2,1,0:T(8,128)(2,1)} %get-tuple-element.19), channel_id=1, source_target_pairs={{0,6},{1,7},{2,4},{3,5},{4,2},{5,3},{6,0},{7,1},{8,14},{9,15},{10,... | collective-permute-start | bytes 442376 | tf_op jit(solution)/shard_map/ppermute | solution.py:21
  26.8 2.1 %copy-start.1 = (bf16[4,4,72,256]{3,2,1,0:T(8,128)(2,1)}, bf16[4,4,72,256]{3,2,1,0:T(8,128)(2,1)S(1)}, u32[]{:S(2)}) copy-start(bf16[4,4,72,256]{3,2,1,0:T(8,128)(2,1)S(1)} %pad_maximum_fusion.mine) | copy-start | bytes 1769476
  26.8 2.1 %collective-permute-start.6 = (bf16[4,4,72,256]{3,2,1,0:T(8,128)(2,1)S(1)}, bf16[4,4,72,256]{3,2,1,0:T(8,128)(2,1)S(1)}, u32[]{:S(2)}, u32[]{:S(2)}) collective-permute-start(bf16[4,4,72,256]{3,2,1,0:T(8,128)(2,1)S(1)} %pad_maximum_fusion.mine), channel_id=1, source_target_pairs={{0,1},{1,0},{2,3},{3,2},{4,5},{5,4},{6,7},{7,6},{8,9},{9,8},{10,11... | collective-permute-start | bytes 1769480 | tf_op jit(solution)/shard_map/ppermute | solution.py:21
  28.9 0.8 copy-start.2
  33.7 2.1 %collective-permute-start.7 = (bf16[64,4096]{1,0:T(8,128)(2,1)}, bf16[64,4096]{1,0:T(8,128)(2,1)S(1)}, u32[]{:S(2)}, u32[]{:S(2)}) collective-permute-start(bf16[64,4096]{1,0:T(8,128)(2,1)} %get-tuple-element.21), channel_id=1, source_target_pairs={{0,1},{1,0},{2,3},{3,2},{4,5},{5,4},{6,7},{7,6},{8,9},{9,8},{10,11... | collective-permute-start | bytes 1572872 | tf_op jit(solution)/shard_map/ppermute | solution.py:21
  37.2 7.3 %collective-permute-start.10 = (bf16[16,4096]{1,0:T(8,128)(2,1)S(1)}, bf16[16,4096]{1,0:T(8,128)(2,1)S(1)}, u32[]{:S(2)}, u32[]{:S(2)}) collective-permute-start(bf16[16,4096]{1,0:T(8,128)(2,1)S(1)} %get-tuple-element.36), channel_id=1, source_target_pairs={{0,6},{1,7},{2,4},{3,5},{4,2},{5,3},{6,0},{7,1},{8,14},{9,15},{10,... | collective-permute-start | bytes 393224 | tf_op jit(solution)/shard_map/ppermute | solution.py:21
  38.0 8.1 %collective-permute-start.8 = (bf16[16,4096]{1,0:T(8,128)(2,1)S(1)}, bf16[16,4096]{1,0:T(8,128)(2,1)S(1)}, u32[]{:S(2)}, u32[]{:S(2)}) collective-permute-start(bf16[16,4096]{1,0:T(8,128)(2,1)S(1)} %get-tuple-element.35), channel_id=1, source_target_pairs={{0,2},{1,3},{2,0},{3,1},{4,6},{5,7},{6,4},{7,5},{8,10},{9,11},{10,... | collective-permute-start | bytes 393224 | tf_op jit(solution)/shard_map/ppermute | solution.py:21
  39.8 6.8 %collective-permute-start.9 = (bf16[16,4096]{1,0:T(8,128)(2,1)S(1)}, bf16[16,4096]{1,0:T(8,128)(2,1)S(1)}, u32[]{:S(2)}, u32[]{:S(2)}) collective-permute-start(bf16[16,4096]{1,0:T(8,128)(2,1)S(1)} %get-tuple-element.37), channel_id=1, source_target_pairs={{0,4},{1,5},{2,6},{3,7},{4,0},{5,1},{6,2},{7,3},{8,12},{9,13},{10,... | collective-permute-start | bytes 393224 | tf_op jit(solution)/shard_map/ppermute | solution.py:21
  46.7 4.5 %collective-permute-start.11 = (bf16[4,4096]{1,0:T(4,128)(2,1)S(1)}, bf16[4,4096]{1,0:T(4,128)(2,1)S(1)}, u32[]{:S(2)}, u32[]{:S(2)}) collective-permute-start(bf16[4,4096]{1,0:T(4,128)(2,1)S(1)} %get-tuple-element.41), channel_id=1, source_target_pairs={{0,8},{1,9},{2,10},{3,11},{4,12},{5,13},{6,14},{7,15},{8,0},{9,1},... | collective-permute-start | bytes 98312 | tf_op jit(solution)/shard_map/ppermute | solution.py:21
  46.8 5.6 %collective-permute-start.12 = (bf16[4,4096]{1,0:T(4,128)(2,1)S(1)}, bf16[4,4096]{1,0:T(4,128)(2,1)S(1)}, u32[]{:S(2)}, u32[]{:S(2)}) collective-permute-start(bf16[4,4096]{1,0:T(4,128)(2,1)S(1)} %get-tuple-element.43), channel_id=1, source_target_pairs={{0,16},{1,17},{2,18},{3,19},{4,20},{5,21},{6,22},{7,23},{8,24},{9,... | collective-permute-start | bytes 98312 | tf_op jit(solution)/shard_map/ppermute | solution.py:21
  48.0 5.7 %collective-permute-start.13 = (bf16[4,4096]{1,0:T(4,128)(2,1)S(1)}, bf16[4,4096]{1,0:T(4,128)(2,1)S(1)}, u32[]{:S(2)}, u32[]{:S(2)}) collective-permute-start(bf16[4,4096]{1,0:T(4,128)(2,1)S(1)} %get-tuple-element.42), channel_id=1, source_target_pairs={{0,24},{1,25},{2,26},{3,27},{4,28},{5,29},{6,30},{7,31},{8,16},{9,... | collective-permute-start | bytes 98312 | tf_op jit(solution)/shard_map/ppermute | solution.py:21
  54.1 4.4 %collective-permute-start.14 = (bf16[4,4224]{1,0:T(4,128)(2,1)S(1)}, bf16[4,4224]{1,0:T(4,128)(2,1)S(1)}, u32[]{:S(2)}, u32[]{:S(2)}) collective-permute-start(bf16[4,4224]{1,0:T(4,128)(2,1)S(1)} %concatenate.17), channel_id=1, source_target_pairs={{0,8},{1,9},{2,10},{3,11},{4,12},{5,13},{6,14},{7,15},{8,0},{9,1},... | collective-permute-start | bytes 101384 | tf_op jit(solution)/shard_map/ppermute | solution.py:21
  54.2 5.6 %collective-permute-start.15 = (bf16[4,4224]{1,0:T(4,128)(2,1)S(1)}, bf16[4,4224]{1,0:T(4,128)(2,1)S(1)}, u32[]{:S(2)}, u32[]{:S(2)}) collective-permute-start(bf16[4,4224]{1,0:T(4,128)(2,1)S(1)} %concatenate.17), channel_id=1, source_target_pairs={{0,16},{1,17},{2,18},{3,19},{4,20},{5,21},{6,22},{7,23},{8,24},{9,... | collective-permute-start | bytes 101384 | tf_op jit(solution)/shard_map/ppermute | solution.py:21
  57.8 5.7 %collective-permute-start.16 = (bf16[4,4224]{1,0:T(4,128)(2,1)S(1)}, bf16[4,4224]{1,0:T(4,128)(2,1)S(1)}, u32[]{:S(2)}, u32[]{:S(2)}) collective-permute-start(bf16[4,4224]{1,0:T(4,128)(2,1)S(1)} %concatenate.17), channel_id=1, source_target_pairs={{0,24},{1,25},{2,26},{3,27},{4,28},{5,29},{6,30},{7,31},{8,16},{9,... | collective-permute-start | bytes 101384 | tf_op jit(solution)/shard_map/ppermute | solution.py:21
  63.6 5.1 %collective-permute-start.17 = (bf16[16,4224]{1,0:T(8,128)(2,1)S(1)}, bf16[16,4224]{1,0:T(8,128)(2,1)S(1)}, u32[]{:S(2)}, u32[]{:S(2)}) collective-permute-start(bf16[16,4224]{1,0:T(8,128)(2,1)S(1)} %pad_maximum_fusion.1), channel_id=1, source_target_pairs={{0,2},{1,3},{2,0},{3,1},{4,6},{5,7},{6,4},{7,5},{8,10},{9,11},{10,... | collective-permute-start | bytes 405512 | tf_op jit(solution)/shard_map/ppermute | solution.py:21
  64.1 5.0 %collective-permute-start.18 = (bf16[16,4224]{1,0:T(8,128)(2,1)S(1)}, bf16[16,4224]{1,0:T(8,128)(2,1)S(1)}, u32[]{:S(2)}, u32[]{:S(2)}) collective-permute-start(bf16[16,4224]{1,0:T(8,128)(2,1)S(1)} %pad_maximum_fusion.1), channel_id=1, source_target_pairs={{0,4},{1,5},{2,6},{3,7},{4,0},{5,1},{6,2},{7,3},{8,12},{9,13},{10,... | collective-permute-start | bytes 405512 | tf_op jit(solution)/shard_map/ppermute | solution.py:21
  65.0 5.9 %collective-permute-start.19 = (bf16[16,4224]{1,0:T(8,128)(2,1)S(1)}, bf16[16,4224]{1,0:T(8,128)(2,1)S(1)}, u32[]{:S(2)}, u32[]{:S(2)}) collective-permute-start(bf16[16,4224]{1,0:T(8,128)(2,1)S(1)} %pad_maximum_fusion.1), channel_id=1, source_target_pairs={{0,6},{1,7},{2,4},{3,5},{4,2},{5,3},{6,0},{7,1},{8,14},{9,15},{10,... | collective-permute-start | bytes 405512 | tf_op jit(solution)/shard_map/ppermute | solution.py:21
  71.4 16.3 %collective-permute-start.20 = (bf16[64,4224]{1,0:T(8,128)(2,1)S(1)}, bf16[64,4224]{1,0:T(8,128)(2,1)S(1)}, u32[]{:S(2)}, u32[]{:S(2)}) collective-permute-start(bf16[64,4224]{1,0:T(8,128)(2,1)S(1)} %concatenate.19), channel_id=1, source_target_pairs={{0,1},{1,0},{2,3},{3,2},{4,5},{5,4},{6,7},{7,6},{8,9},{9,8},{10,11... | collective-permute-start | bytes 1622024 | tf_op jit(solution)/shard_map/ppermute | solution.py:21
  71.5 8.8 %copy-start.8 = (f32[1,32,6]{1,0,2:T(1,128)S(1)}, f32[1,32,6]{1,0,2:T(1,128)}, u32[]{:S(2)}) copy-start(f32[1,32,6]{1,0,2:T(1,128)} %param.29) | copy-start | bytes 2308
  71.5 8.9 %copy-start.11 = (f32[1,3,32]{2,0,1:T(1,128)S(1)}, f32[1,3,32]{2,0,1:T(1,128)}, u32[]{:S(2)}) copy-start(f32[1,3,32]{2,0,1:T(1,128)} %param.31) | copy-start | bytes 1156
  88.4 7.1 %copy-start = (bf16[1,384,4096]{2,1,0:T(8,128)(2,1)S(1)}, bf16[1,384,4096]{2,1,0:T(8,128)(2,1)}, u32[]{:S(2)}) copy-start(bf16[1,384,4096]{2,1,0:T(8,128)(2,1)} %param.30) | copy-start | bytes 9437188
  99.5 2.1 %collective-permute-start.21 = (bf16[64,4096]{1,0:T(8,128)(2,1)S(1)}, bf16[64,4096]{1,0:T(8,128)(2,1)S(1)}, u32[]{:S(2)}, u32[]{:S(2)}) collective-permute-start(bf16[64,4096]{1,0:T(8,128)(2,1)S(1)} %slice.181), channel_id=1, source_target_pairs={{0,1},{1,0},{2,3},{3,2},{4,5},{5,4},{6,7},{7,6},{8,9},{9,8},{10,11... | collective-permute-start | bytes 1572872 | tf_op jit(solution)/shard_map/ppermute | solution.py:21
  101.8 6.0 %collective-permute-start.22 = (bf16[16,4096]{1,0:T(8,128)(2,1)S(1)}, bf16[16,4096]{1,0:T(8,128)(2,1)S(1)}, u32[]{:S(2)}, u32[]{:S(2)}) collective-permute-start(bf16[16,4096]{1,0:T(8,128)(2,1)S(1)} %get-tuple-element.32), channel_id=1, source_target_pairs={{0,2},{1,3},{2,0},{3,1},{4,6},{5,7},{6,4},{7,5},{8,10},{9,11},{10,... | collective-permute-start | bytes 393224 | tf_op jit(solution)/shard_map/ppermute | solution.py:21
  103.6 8.3 %collective-permute-start.23 = (bf16[16,4096]{1,0:T(8,128)(2,1)S(1)}, bf16[16,4096]{1,0:T(8,128)(2,1)S(1)}, u32[]{:S(2)}, u32[]{:S(2)}) collective-permute-start(bf16[16,4096]{1,0:T(8,128)(2,1)S(1)} %get-tuple-element.34), channel_id=1, source_target_pairs={{0,4},{1,5},{2,6},{3,7},{4,0},{5,1},{6,2},{7,3},{8,12},{9,13},{10,... | collective-permute-start | bytes 393224 | tf_op jit(solution)/shard_map/ppermute | solution.py:21
  104.6 7.3 %collective-permute-start.24 = (bf16[16,4096]{1,0:T(8,128)(2,1)S(1)}, bf16[16,4096]{1,0:T(8,128)(2,1)S(1)}, u32[]{:S(2)}, u32[]{:S(2)}) collective-permute-start(bf16[16,4096]{1,0:T(8,128)(2,1)S(1)} %get-tuple-element.33), channel_id=1, source_target_pairs={{0,6},{1,7},{2,4},{3,5},{4,2},{5,3},{6,0},{7,1},{8,14},{9,15},{10,... | collective-permute-start | bytes 393224 | tf_op jit(solution)/shard_map/ppermute | solution.py:21
  112.0 4.5 %collective-permute-start.25 = (bf16[4,4096]{1,0:T(4,128)(2,1)S(1)}, bf16[4,4096]{1,0:T(4,128)(2,1)S(1)}, u32[]{:S(2)}, u32[]{:S(2)}) collective-permute-start(bf16[4,4096]{1,0:T(4,128)(2,1)S(1)} %get-tuple-element.38), channel_id=1, source_target_pairs={{0,8},{1,9},{2,10},{3,11},{4,12},{5,13},{6,14},{7,15},{8,0},{9,1},... | collective-permute-start | bytes 98312 | tf_op jit(solution)/shard_map/ppermute | solution.py:21
  112.1 4.9 %collective-permute-start.26 = (bf16[4,4096]{1,0:T(4,128)(2,1)S(1)}, bf16[4,4096]{1,0:T(4,128)(2,1)S(1)}, u32[]{:S(2)}, u32[]{:S(2)}) collective-permute-start(bf16[4,4096]{1,0:T(4,128)(2,1)S(1)} %get-tuple-element.40), channel_id=1, source_target_pairs={{0,16},{1,17},{2,18},{3,19},{4,20},{5,21},{6,22},{7,23},{8,24},{9,... | collective-permute-start | bytes 98312 | tf_op jit(solution)/shard_map/ppermute | solution.py:21
  113.4 5.7 %collective-permute-start.27 = (bf16[4,4096]{1,0:T(4,128)(2,1)S(1)}, bf16[4,4096]{1,0:T(4,128)(2,1)S(1)}, u32[]{:S(2)}, u32[]{:S(2)}) collective-permute-start(bf16[4,4096]{1,0:T(4,128)(2,1)S(1)} %get-tuple-element.39), channel_id=1, source_target_pairs={{0,24},{1,25},{2,26},{3,27},{4,28},{5,29},{6,30},{7,31},{8,16},{9,... | collective-permute-start | bytes 98312 | tf_op jit(solution)/shard_map/ppermute | solution.py:21

commit v2 on v1

--- a/solution.py
+++ b/solution.py
@@ -8,6 +8,7 @@
 from jax.experimental.pallas import tpu as pltpu
 from jax.sharding import PartitionSpec as P
 
+
 HD = 128
 CAND = 64
 
@@ -15,10 +16,18 @@
 EPSILON = 1e-06
 LOW = 2
 MID = 4
+BLK = 128
+STRIP = 2**19
+DEPTH = 4
+SMALL_VMEM = 8 * 2**20
 
 
 def swapped(value, offset):
     return lax.ppermute(value, "ctx", [(i, i ^ offset) for i in range(lax.axis_size("ctx"))])
+
+
+def in_hbm(value):
+    return pltpu.with_memory_space_constraint(value, pltpu.HBM)
 
 
 def stage_offsets(shards):
@@ -28,15 +37,15 @@
     return low, mid, high
 
 
-def dequantize(code_values, scales):
-    rows_per = code_values.shape[0] // scales.shape[0]
-    cols_per = code_values.shape[1] // scales.shape[1]
-    spread = jnp.repeat(jnp.repeat(scales, rows_per, axis=0), cols_per, axis=1)
-    return (code_values.astype(jnp.float32) * spread).astype(jnp.bfloat16)
-
-
-def pack_body(info, q, own_key, own_value, keys, values, *outs, feature, per_group):
-    device = info[0]
+def pack_body(*refs, feature, per_group, count):
+    sources, outs, held, sems = refs[:5], refs[5 : 5 + count], refs[5 + count : 10 + count], refs[10 + count]
+    copies = [pltpu.make_async_copy(source, to, sems.at[i]) for i, (source, to) in enumerate(zip(sources, held))]
+    for copy in copies:
+        copy.start()
+    for copy in copies:
+        copy.wait()
+    q, own_key, own_value, keys, values = held
+    device = lax.axis_index("ctx")
     prefixes, ctx_local, _ = keys.shape
     rows = q.shape[0]
     kv_rows = prefixes * ctx_local
@@ -59,7 +68,7 @@
         out[top : top + rows, HD : 2 * HD] = own_value[:, lanes]
 
 
-def repack_body(*refs, kv_rows, rows):
+def repack_body(after, *refs, kv_rows, rows):
     outs = refs[-MID:]
     parts = refs[:-MID]
     for zx, part in enumerate(parts):
@@ -71,11 +80,13 @@
             out[zx, kv_rows + rows : kv_rows + 2 * rows, :] = part[own : own + rows, :]
 
 
-def attend_body(info, prefix_of, lengths, mine, other, w_out, keep, send, att, *, ctx_local, kv_rows, rows):
-    device = info[0]
-    mid, high = mine.shape[0], mine.shape[1]
-    pieces = mid * high
-    span = CAND // (LOW * mid * rows)
+def attend_body(info, *refs, ctx_local, kv_rows, rows):
+    mine, other = refs[:MID], refs[MID : 2 * MID]
+    w_out, keep, send, att = refs[2 * MID :]
+    device = lax.axis_index("ctx")
+    high = mine[0].shape[0]
+    pieces = MID * high
+    span = CAND // (LOW * MID * rows)
     scale = 1.0 / math.sqrt(HD)
     tile = 2 * rows
     pick_rows = lax.broadcasted_iota(jnp.int32, (CAND, CAND * 2), 0)
@@ -87,13 +98,20 @@
     piece = column // ctx_local
     within = column % ctx_local
     relative = (piece % high) * (LOW * MID) + (piece // high) * LOW
-    own_group = device // (LOW * mid * span)
+    own_group = device // (LOW * MID * span)
+
+    def joined(parts, zs, at, lanes, depth):
+        return jnp.concatenate([part[zs, at, lanes].reshape(depth, -1) for part in parts], axis=0)
+
     for zg in range(high // span):
-        prefix = prefix_of[own_group ^ zg]
-        length = lengths[prefix]
+        prefix = info[own_group ^ zg]
+        length = info[high // span + prefix]
         zs = slice(zg * span, (zg + 1) * span)
-        tail_mine = mine[:, zs, kv_rows : kv_rows + tile, :].reshape(CAND, 2 * HD)
-        tail_other = other[:, zs, kv_rows : kv_rows + tile, :].reshape(CAND, 2 * HD)
+        tails = slice(kv_rows, kv_rows + tile)
+        at = pl.ds(pl.multiple_of(prefix * ctx_local, ctx_local), ctx_local)
+        every = slice(0, high)
+        tail_mine = joined(mine, zs, tails, slice(0, 2 * HD), span * tile)
+        tail_other = joined(other, zs, tails, slice(0, 2 * HD), span * tile)
         padded = jnp.concatenate([tail_mine[:, 0:HD], tail_other[:, HD : 2 * HD]], axis=0)
         query = jnp.dot(pick_query, padded, preferred_element_type=jnp.float32)
         own = jnp.dot(
@@ -104,8 +122,7 @@
         top = own_score
         all_scores = []
         for cx, source in enumerate((mine, other)):
-            at = pl.ds(pl.multiple_of(prefix * ctx_local, ctx_local), ctx_local)
-            key = source[:, :, at, 0:HD].reshape(pieces * ctx_local, HD)
+            key = joined(source, every, at, slice(0, HD), high * ctx_local)
             scores = (
                 lax.dot_general(query, key, (((1,), (1,)), ((), ())), preferred_element_type=jnp.float32) * scale
             )
@@ -117,22 +134,128 @@
         numer = own_weight * own[:, HD : 2 * HD]
         denom = own_weight
         for scores, source in zip(all_scores, (mine, other)):
-            at = pl.ds(pl.multiple_of(prefix * ctx_local, ctx_local), ctx_local)
-            value = source[:, :, at, HD : 2 * HD].reshape(pieces * ctx_local, HD)
+            value = joined(source, every, at, slice(HD, 2 * HD), high * ctx_local)
             weights = jnp.exp(scores - top)
             denom = denom + jnp.sum(weights, axis=1, keepdims=True)
             numer = numer + jnp.dot(weights.astype(jnp.bfloat16), value, preferred_element_type=jnp.float32)
         attended = numer / denom
         chunk = span * rows
-        att[:, zg * chunk : (zg + 1) * chunk, :] = attended.reshape(LOW * mid, chunk, HD)
+        att[:, zg * chunk : (zg + 1) * chunk, :] = attended.reshape(LOW * MID, chunk, HD)
     half = keep.shape[0]
     attended = att[...].reshape(2 * half, HD).astype(jnp.bfloat16)
-    keep[...] = jnp.dot(attended[0:half], w_out[...], preferred_element_type=jnp.float32)
-    send[...] = jnp.dot(attended[half:], w_out[...], preferred_element_type=jnp.float32).astype(jnp.bfloat16)
+    out = jnp.dot(attended, w_out[...], preferred_element_type=jnp.float32)
+    keep[...] = out[0:half]
+    send[...] = out[half:].astype(jnp.bfloat16)
+
+
+def dequantize_strips(out, codes, scales, first, count, offset):
+    for i in range(first, first + count):
+        rows = slice(i * BLK, (i + 1) * BLK)
+        for j in range(codes.shape[1] // BLK):
+            lanes = slice(j * BLK, (j + 1) * BLK)
+            out[rows, lanes] = (codes[rows, lanes].astype(jnp.float32) * scales[offset + i, j]).astype(jnp.bfloat16)
+
+
+def strip_rows(shape):
+    blocks = shape[0] // BLK
+    count = max(1, min(blocks, STRIP // (BLK * shape[1])))
+    while blocks % count:
+        count -= 1
+    return count * BLK
+
+
+def prepare_body(*refs, ranges, fetched):
+    count = len(ranges)
+    scales, sources, plain = refs[:count], refs[count : 2 * count], refs[2 * count : 2 * count + fetched]
+    refs = refs[2 * count + fetched :]
+    outs, fetch, held, sems = refs[:count], refs[count : count + fetched], refs[count + fetched : -1], refs[-1]
+    jobs = []
+    for scale, source, to, out, (start, size) in zip(scales, sources, held, outs, ranges):
+        step = strip_rows((size, source.shape[1]))
+        for first in range(0, size, step):
+            copy = pltpu.make_async_copy(
+                source.at[pl.ds(start + first, step)], to.at[pl.ds(first, step)], sems.at[len(jobs)]
+            )
+            jobs.append((copy, (out, to, scale, first // BLK, step // BLK, start // BLK)))
+    direct = [pltpu.make_async_copy(a, to, sems.at[len(jobs) + i]) for i, (a, to) in enumerate(zip(plain, fetch))]
+    for copy, _ in jobs[:DEPTH]:
+        copy.start()
+    for copy in direct:
+        copy.start()
+    for i, (copy, job) in enumerate(jobs):
+        copy.wait()
+        if i + DEPTH < len(jobs):
+            jobs[i + DEPTH][0].start()
+        dequantize_strips(*job)
+    for copy in direct:
+        copy.wait()
+
+
+def prepared(weights, fetch=()):
+    scales = [item[0] for item in weights]
+    codes = [item[1] for item in weights]
+    ranges = tuple(item[2:] for item in weights)
+    fetch = list(fetch)
+    shapes = [(size, a.shape[1]) for a, (_, size) in zip(codes, ranges)]
+    steps = sum(shape[0] // strip_rows(shape) for shape in shapes)
+    return pl.pallas_call(
+        functools.partial(prepare_body, ranges=ranges, fetched=len(fetch)),
+        in_specs=[SMEM] * len(codes) + [HBM] * (len(codes) + len(fetch)),
+        out_specs=[VMEM] * (len(codes) + len(fetch)),
+        out_shape=[pltpu.VMEM(shape, jnp.bfloat16) for shape in shapes] + [pltpu.VMEM(a.shape, a.dtype) for a in fetch],
+        scratch_shapes=[pltpu.VMEM(shape, jnp.bfloat16) for shape in shapes]
+        + [pltpu.SemaphoreType.DMA((steps + len(fetch),))],
+        compiler_params=pltpu.CompilerParams(vmem_limit_bytes=2 * sum(math.prod(shape) for shape in shapes) + 2**20),
+        name="prepare",
+    )(*scales, *(in_hbm(item) for item in codes + fetch))
+
+
+def join_body(*refs):
+    out = refs[-1]
+    rows = refs[0].shape[0]
+    for i, part in enumerate(refs[:-1]):
+        out[i * rows : (i + 1) * rows, :] = part[...]
+
+
+def joined(parts):
+    rows, width = parts[0].shape
+    return pl.pallas_call(
+        join_body,
+        in_specs=[VMEM] * len(parts),
+        out_specs=VMEM,
+        out_shape=jax.ShapeDtypeStruct((len(parts) * rows, width), parts[0].dtype),
+        compiler_params=pltpu.CompilerParams(vmem_limit_bytes=SMALL_VMEM),
+        name="join",
+    )(*parts)
+
+
+def expert_body(*refs, width, experts):
+    parts = refs[: 2 * MID]
+    gate_first, gate_rest, down, keep, send, x = refs[2 * MID :]
+    expert = lax.axis_index("ctx") // 2
+    some = parts[0].shape[0]
+    half = keep.shape[0]
+    for i, part in enumerate(parts):
+        x[i * some : (i + 1) * some, :] = part[:, 0:width]
+    tail = jnp.concatenate([part[:, width:] for part in parts], axis=0).astype(jnp.float32)
+    lane = lax.broadcasted_iota(jnp.int32, tail.shape, 1)
+    chosen = (lane == expert) | (lane == expert + experts)
+    weight = jnp.sum(jnp.where(chosen, tail, 0.0), axis=1, keepdims=True)
+    hidden = down.shape[0]
+    first = gate_first.shape[0]
+    act = jnp.dot(x[:, :first], gate_first[...], preferred_element_type=jnp.float32)
+    act += jnp.dot(x[:, first:], gate_rest[...], preferred_element_type=jnp.float32)
+    gate, up = act[:, :hidden], act[:, hidden:]
+    active = (gate / (1.0 + jnp.exp(-gate)) * up).astype(jnp.bfloat16)
+    out = jnp.dot(active, down[...], preferred_element_type=jnp.float32) * weight
+    keep[...] = out[0:half]
+    send[...] = out[half:].astype(jnp.bfloat16)
 
 
 VMEM = pl.BlockSpec(memory_space=pltpu.VMEM)
 SMEM = pl.BlockSpec(memory_space=pltpu.SMEM)
+HBM = pl.BlockSpec(memory_space=pltpu.HBM)
+ANY = pl.BlockSpec(memory_space=pl.ANY)
 
 
 def scatter_sum(keep, send, mid, high):
@@ -177,28 +300,31 @@
     kv_rows = prefixes * ctx_local
     feature = w_out.shape[0]
     low, mid, high = stage_offsets(shards)
-    info = device.reshape(1).astype(jnp.int32)
-    block_prefix = prefix_of_row.reshape(-1, CAND)[:, 0]
-
-    message_rows = kv_rows + MID * rows + 2 * rows
+    info = jnp.concatenate([prefix_of_row[::CAND], context_len])
+
+    inputs = (queries, own_key, own_value, cache_keys, cache_values)
+    message = jax.ShapeDtypeStruct((kv_rows + MID * rows + 2 * rows, 2 * HD), jnp.bfloat16)
     messages = pl.pallas_call(
-        functools.partial(pack_body, feature=feature, per_group=per_group),
-        in_specs=[SMEM] + [VMEM] * 5,
+        functools.partial(pack_body, feature=feature, per_group=per_group, count=len(high)),
+        in_specs=[HBM] * len(inputs),
         out_specs=[VMEM] * len(high),
-        out_shape=[jax.ShapeDtypeStruct((message_rows, 2 * HD), jnp.bfloat16)] * len(high),
+        out_shape=[message] * len(high),
+        scratch_shapes=[pltpu.VMEM(a.shape, a.dtype) for a in inputs] + [pltpu.SemaphoreType.DMA((len(inputs),))],
+        compiler_params=pltpu.CompilerParams(vmem_limit_bytes=SMALL_VMEM),
         name="pack",
-    )(info, queries, own_key, own_value, cache_keys, cache_values)
+    )(*(in_hbm(item) for item in inputs))
     got = [messages[0]] + [swapped(messages[i], high[i]) for i in range(1, len(high))]
     piece = jax.ShapeDtypeStruct((len(high), kv_rows + 2 * rows, 2 * HD), jnp.bfloat16)
     messages = pl.pallas_call(
         functools.partial(repack_body, kv_rows=kv_rows, rows=rows),
-        in_specs=[VMEM] * len(high),
+        in_specs=[ANY] + [VMEM] * len(high),
         out_specs=[VMEM] * MID,
         out_shape=[piece] * MID,
+        compiler_params=pltpu.CompilerParams(vmem_limit_bytes=2 * SMALL_VMEM),
         name="repack",
-    )(*got)
-    mine = jnp.stack([messages[0]] + [swapped(messages[i], mid[i]) for i in range(1, MID)], axis=0)
-    other = swapped(mine, low[1])
+    )(info, *got)
+    mine = [messages[0]] + [swapped(messages[i], mid[i]) for i in range(1, MID)]
+    other = [swapped(item, low[1]) for item in mine]
 
     if feature < HD:
         w_full = lax.dynamic_update_slice(
@@ -206,18 +332,27 @@
         )
     else:
         w_full = w_out
+    codes, scales = gate_up_codes[0], gate_up_scales[0]
+    first = codes.shape[0] // 2
+    gate_first, w_full = prepared([(scales, codes, 0, first)], [w_full])
+    (down,) = prepared([(down_scales[0], down_codes[0], 0, down_codes.shape[1])])
+    (gate_rest,) = prepared([(scales, codes, first, codes.shape[0] - first)])
     half = shards * rows // 2
+    attend_vmem = 8 * 2**20 + 2 * MID * piece.size * 2 + w_full.size * 2 + half * width * 10
     keep, send = pl.pallas_call(
         functools.partial(attend_body, ctx_local=ctx_local, kv_rows=kv_rows, rows=rows),
-        in_specs=[SMEM] * 3 + [VMEM] * 3,
+        in_specs=[SMEM] + [VMEM] * (2 * MID + 1),
         out_specs=[VMEM] * 2,
         out_shape=[
             jax.ShapeDtypeStruct((half, width), jnp.float32),
             jax.ShapeDtypeStruct((half, width), jnp.bfloat16),
         ],
-        scratch_shapes=[pltpu.VMEM((LOW * MID, len(high) * rows, HD), jnp.float32)],
+        scratch_shapes=[
+            pltpu.VMEM((LOW * MID, len(high) * rows, HD), jnp.float32),
+        ],
+        compiler_params=pltpu.CompilerParams(vmem_limit_bytes=attend_vmem),
         name="attend",
-    )(info, block_prefix, context_len, mine, other, w_full)
+    )(info, *mine, *other, w_full)
 
     projected = scatter_sum(keep, send, mid, high)
     mixed = hidden_in.astype(jnp.float32) + projected
@@ -233,20 +368,25 @@
     extra = -(2 * experts_all) % HD
     tail = jnp.concatenate([coarse, fine, jnp.zeros((rows, extra), jnp.float32)], axis=1)
     held = jnp.concatenate([normed, tail.astype(jnp.bfloat16)], axis=1)
-    for offsets in (high, mid, low):
-        held = jnp.concatenate([held] + [swapped(held, o) for o in offsets[1:]], axis=0)
-    lane = lax.broadcasted_iota(jnp.int32, (1, 2 * experts_all + extra), 1)
-    expert = device // 2
-    chosen = (lane == expert) | (lane == expert + experts_all)
-    row_weight = jnp.sum(jnp.where(chosen, held[:, width:].astype(jnp.float32), 0.0), axis=1, keepdims=True)
-
-    gate_up = dequantize(gate_up_codes[0], gate_up_scales[0])
-    down_proj = dequantize(down_codes[0], down_scales[0])
-    half_width = down_proj.shape[0]
-    projected_in = jnp.dot(held[:, :width], gate_up, preferred_element_type=jnp.float32)
-    activated = (jax.nn.silu(projected_in[:, :half_width]) * projected_in[:, half_width:]).astype(jnp.bfloat16)
-    result = jnp.dot(activated, down_proj, preferred_element_type=jnp.float32) * row_weight
-    expert_sum = scatter_sum(result[:half], result[half:].astype(jnp.bfloat16), mid, high)
+    held = joined([held] + [swapped(held, o) for o in high[1:]])
+    mine = [held] + [swapped(held, o) for o in mid[1:]]
+    other = [swapped(item, low[1]) for item in mine]
+    expert_vmem = 4 * 2**20 + 2 * half * width * 15
+    keep, send = pl.pallas_call(
+        functools.partial(expert_body, width=width, experts=experts_all),
+        in_specs=[VMEM] * (2 * MID + 3),
+        out_specs=[VMEM] * 2,
+        out_shape=[
+            jax.ShapeDtypeStruct((half, width), jnp.float32),
+            jax.ShapeDtypeStruct((half, width), jnp.bfloat16),
+        ],
+        scratch_shapes=[
+            pltpu.VMEM((2 * half, width), jnp.bfloat16),
+        ],
+        compiler_params=pltpu.CompilerParams(vmem_limit_bytes=expert_vmem),
+        name="expert",
+    )(*mine, *other, gate_first, gate_rest, down)
+    expert_sum = scatter_sum(keep, send, mid, high)
     layer_out = (mixed + expert_sum).astype(jnp.bfloat16)
     return (attention_out, layer_out)
 

time: 120 us -> 93.6 us (0.78)
  local copies, waits for them, and re-layouts: 15 us -> 1.78 us
  matrix products: 9.1 us -> 0 us
  other arithmetic: 11.2 us -> 2.15 us
  Pallas kernels: 7.44 us -> 14.6 us
  waiting for transfers between devices: 42.2 us -> 39.4 us
    pallas_call x0 -> x5, Pallas kernels: none -> 10.9 us  [the longest x3 8.63 us: prepared(): pl.pallas_call(functools.partial(prepare_body, ranges=ranges, fetched=len...]
    unnamed x29 -> x12, local copies, waits for them, and re-layouts: 10.4 us -> 0.8 us
    dot_general x2 -> x0, matrix products: 9.1 us -> none  [the longest x1 5.13 us: local(): jnp.dot(held[:, :width], gate_up, preferred_element_type=jnp.float32)]
    convert_element_type x1 -> x0, other arithmetic: 7.31 us -> none  [dequantize(): return (code_values.astype(jnp.float32) * spread).astype(jnp.bfloat16)]
    ppermute x28 -> x34, waiting for transfers between devices: 42.2 us -> 39.4 us  [swapped(): lax.ppermute(value, 'ctx', [(i, i ^ offset) for i in range(lax.axis_size(...]
    another operation x6 -> x5, other arithmetic: 2.63 us -> 0.4 us
    broadcast_in_dim x2 -> x0, local copies, waits for them, and re-layouts: 1.79 us -> none  [dequantize(): spread = jnp.repeat(jnp.repeat(scales, rows_per, axis=0), cols_per, axis=1)]
    pallas_call x1, Pallas kernels: 1.73 us -> 0.04 us  [local(): pl.pallas_call(functools.partial(repack_body, kv_rows=kv_rows, rows=rows)...]
  transfers between devices with their start and end apart: 28 -> 34, of which waited for: 21 -> 19; matrix products, arithmetic and copies ran while one was open for 15% -> 3% of each run, Pallas kernels for 0% -> 9%
where the time goes in v2:
time: 93.6 us; the launch traced here: 93.3 us
  waiting for transfers between devices  39.4 us (42%)
  starting transfers between devices  34.4 us (37%)
  Pallas kernels  14.6 us (16%)
  other arithmetic  2.15 us (2%)
  local copies, waits for them, and re-layouts  1.78 us (2%)
  between operations  0.94 us (1%)
    ppermute x34, waiting for transfers between devices, swapped(): lax.ppermute(value, 'ctx', [(i, i ^ offset) for i in range(lax.axis_size(...  39.4 us
    ppermute x34, starting transfers between devices, swapped(): lax.ppermute(value, 'ctx', [(i, i ^ offset) for i in range(lax.axis_size(...  34.4 us
    pallas_call x3, Pallas kernels, prepared(): pl.pallas_call(functools.partial(prepare_body, ranges=ranges, fetched=len...  8.63 us
    pallas_call x1, Pallas kernels, local(): pl.pallas_call(functools.partial(attend_body, ctx_local=ctx_local, kv_row...  2.62 us
    pallas_call x1, Pallas kernels, local(): pl.pallas_call(functools.partial(expert_body, width=width, experts=expert...  2.22 us
  transfers between devices with their start and end apart: 34, of which 19 were waited for; matrix products, arithmetic and copies ran while one was open for 3% of the time, Pallas kernels for 9%

profile of v2, /device:TPU:0, one launch (start us, length us, event | category | flops | bytes accessed | tf_op | source)
XLA Modules:
  0.0 93.3 jit_solution(72049880726476838)
XLA Ops:
  0.6 1.1 %pack.1 = (bf16[88,256]{1,0:T(8,128)(2,1)S(1)}, bf16[88,256]{1,0:T(8,128)(2,1)S(1)}, bf16[88,256]{1,0:T(8,128)(2,1)S(1)}, bf16[88,256]{1,0:T(8,128)(2,1)S(1)}) custom-call(bf16[4,4096]{1,0:T(4,128)(2,1)} %refs_0_.1, bf16[4,256]{1,0:T(4,128)(2,1)} %refs_1_.1, bf16[4,256]{1,0:T(4,128)(2,1)} %refs_2_.2, bf16[2,32,256]{2,1,0:T(8,128)(2,1)} %refs_3_.1, ...), custom_call_target="tpu_custom_call" | custom-call | tf_op jit(solution)/shard_map/pack/pallas_call | solution.py:307
  1.7 3.1 %collective-permute-start = (bf16[88,256]{1,0:T(8,128)(2,1)S(1)}, bf16[88,256]{1,0:T(8,128)(2,1)S(1)}, u32[]{:S(2)}, u32[]{:S(2)}) collective-permute-start(bf16[88,256]{1,0:T(8,128)(2,1)S(1)} %get-tuple-element.17), channel_id=1, source_target_pairs={{0,8},{1,9},{2,10},{3,11},{4,12},{5,13},{6,14},{7,15},{8,0},{9,1},... | collective-permute-start | bytes 135176 | tf_op jit(solution)/shard_map/ppermute | solution.py:26
  4.8 2.6 %collective-permute-start.1 = (bf16[88,256]{1,0:T(8,128)(2,1)S(1)}, bf16[88,256]{1,0:T(8,128)(2,1)S(1)}, u32[]{:S(2)}, u32[]{:S(2)}) collective-permute-start(bf16[88,256]{1,0:T(8,128)(2,1)S(1)} %get-tuple-element.18), channel_id=1, source_target_pairs={{0,16},{1,17},{2,18},{3,19},{4,20},{5,21},{6,22},{7,23},{8,24},{9,... | collective-permute-start | bytes 135176 | tf_op jit(solution)/shard_map/ppermute | solution.py:26
  7.4 0.7 slice.79
  8.2 0.7 pad_add_fusion.after.info
  8.9 1.7 %collective-permute-done.1.refs_2_ = bf16[88,256]{1,0:T(8,128)(2,1)S(1)} collective-permute-done((bf16[88,256]{1,0:T(8,128)(2,1)S(1)}, bf16[88,256]{1,0:T(8,128)(2,1)S(1)}, u32[]{:S(2)}, u32[]{:S(2)}) %collective-permute-start.1) | collective-permute-done | bytes 45088 | tf_op jit(solution)/shard_map/ppermute | solution.py:26
  10.6 2.6 %collective-permute-done.2.refs_3_ = bf16[88,256]{1,0:T(8,128)(2,1)S(1)} collective-permute-done((bf16[88,256]{1,0:T(8,128)(2,1)S(1)}, bf16[88,256]{1,0:T(8,128)(2,1)S(1)}, u32[]{:S(2)}, u32[]{:S(2)}) %collective-permute-start.2) | collective-permute-done | bytes 45088 | tf_op jit(solution)/shard_map/ppermute | solution.py:26
  13.3 1.6 %collective-permute-start.3 = (bf16[4,72,256]{2,1,0:T(8,128)(2,1)S(1)}, bf16[4,72,256]{2,1,0:T(8,128)(2,1)S(1)}, u32[]{:S(2)}, u32[]{:S(2)}) collective-permute-start(bf16[4,72,256]{2,1,0:T(8,128)(2,1)S(1)} %get-tuple-element.21), channel_id=1, source_target_pairs={{0,2},{1,3},{2,0},{3,1},{4,6},{5,7},{6,4},{7,5},{8,10},{9,11},{10,... | collective-permute-start | bytes 442376 | tf_op jit(solution)/shard_map/ppermute | solution.py:26
  14.9 1.5 %collective-permute-start.4 = (bf16[4,72,256]{2,1,0:T(8,128)(2,1)S(1)}, bf16[4,72,256]{2,1,0:T(8,128)(2,1)}, u32[]{:S(2)}, u32[]{:S(2)}) collective-permute-start(bf16[4,72,256]{2,1,0:T(8,128)(2,1)S(1)} %get-tuple-element.22), channel_id=1, source_target_pairs={{0,4},{1,5},{2,6},{3,7},{4,0},{5,1},{6,2},{7,3},{8,12},{9,13},{10,... | collective-permute-start | bytes 442376 | tf_op jit(solution)/shard_map/ppermute | solution.py:26
  16.4 0.5 collective-permute-start.5
  16.9 2.9 %collective-permute-done.3.refs_1_ = bf16[4,72,256]{2,1,0:T(8,128)(2,1)S(1)} collective-permute-done((bf16[4,72,256]{2,1,0:T(8,128)(2,1)S(1)}, bf16[4,72,256]{2,1,0:T(8,128)(2,1)S(1)}, u32[]{:S(2)}, u32[]{:S(2)}) %collective-permute-start.3) | collective-permute-done | bytes 147488 | tf_op jit(solution)/shard_map/ppermute | solution.py:26
  19.8 2.9 %collective-permute-done.4.refs_2_ = bf16[4,72,256]{2,1,0:T(8,128)(2,1)} collective-permute-done((bf16[4,72,256]{2,1,0:T(8,128)(2,1)S(1)}, bf16[4,72,256]{2,1,0:T(8,128)(2,1)}, u32[]{:S(2)}, u32[]{:S(2)}) %collective-permute-start.4) | collective-permute-done | bytes 147488 | tf_op jit(solution)/shard_map/ppermute | solution.py:26
  22.7 0.5 collective-permute-start.9
  23.2 0.8 copy.19
  23.9 3.0 %prepare.3 = (bf16[2048,768]{1,0:T(8,128)(2,1)S(1)}, bf16[128,4096]{1,0:T(8,128)(2,1)S(1)}) custom-call(f32[32,6]{1,0:T(8,128)S(1)} %bitcast.6, bf16[4096,768]{1,0:T(8,128)(2,1)} %bitcast.9, bf16[128,4096]{1,0:T(8,128)(2,1)} %refs_2_.3), custom_call_target="tpu_custom_call" | custom-call | tf_op jit(solution)/shard_map/prepare/pallas_call | solution.py:201
  27.0 2.6 %attend.1 = (f32[64,4096]{1,0:T(8,128)S(1)}, bf16[64,4096]{1,0:T(8,128)(2,1)S(1)}) custom-call(s32[4]{0:T(128)S(1)} %pad_add_fusion.after.info, bf16[4,72,256]{2,1,0:T(8,128)(2,1)S(1)} %get-tuple-element.20.refs_0_, bf16[4,72,256]{2,1,0:T(8,128)(2,1)S(1)} %collective-permute-done.3.refs_1_, bf16[4,72,256]{2,1,0:T(8,128)(2,1)} %collective-permute-done.4.refs_2_, ...), custom_call_target="tpu_custom_call" | custom-call | tf_op jit(solution)/shard_map/attend/pallas_call | solution.py:342
  29.7 0.0 copy-start
  29.7 0.1 collective-permute-start.10
  29.8 1.9 %collective-permute-done.10 = bf16[64,4096]{1,0:T(8,128)(2,1)S(1)} collective-permute-done((bf16[64,4096]{1,0:T(8,128)(2,1)S(1)}, bf16[64,4096]{1,0:T(8,128)(2,1)S(1)}, u32[]{:S(2)}, u32[]{:S(2)}) %collective-permute-start.10) | collective-permute-done | bytes 524320 | tf_op jit(solution)/shard_map/ppermute | solution.py:26
  31.7 0.1 fusion.18
  31.8 0.1 collective-permute-start.11
  31.9 1.2 %collective-permute-start.12 = (bf16[16,4096]{1,0:T(8,128)(2,1)S(1)}, bf16[16,4096]{1,0:T(8,128)(2,1)S(1)}, u32[]{:S(2)}, u32[]{:S(2)}) collective-permute-start(bf16[16,4096]{1,0:T(8,128)(2,1)S(1)} %get-tuple-element.45), channel_id=1, source_target_pairs={{0,4},{1,5},{2,6},{3,7},{4,0},{5,1},{6,2},{7,3},{8,12},{9,13},{10,... | collective-permute-start | bytes 393224 | tf_op jit(solution)/shard_map/ppermute | solution.py:26
  33.2 2.2 %collective-permute-start.13 = (bf16[16,4096]{1,0:T(8,128)(2,1)S(1)}, bf16[16,4096]{1,0:T(8,128)(2,1)S(1)}, u32[]{:S(2)}, u32[]{:S(2)}) collective-permute-start(bf16[16,4096]{1,0:T(8,128)(2,1)S(1)} %get-tuple-element.44), channel_id=1, source_target_pairs={{0,6},{1,7},{2,4},{3,5},{4,2},{5,3},{6,0},{7,1},{8,14},{9,15},{10,... | collective-permute-start | bytes 393224 | tf_op jit(solution)/shard_map/ppermute | solution.py:26
  35.4 0.1 select_reduce_fusion
  35.5 2.8 %collective-permute-done.11 = bf16[16,4096]{1,0:T(8,128)(2,1)S(1)} collective-permute-done((bf16[16,4096]{1,0:T(8,128)(2,1)S(1)}, bf16[16,4096]{1,0:T(8,128)(2,1)S(1)}, u32[]{:S(2)}, u32[]{:S(2)}) %collective-permute-start.11) | collective-permute-done | bytes 131104 | tf_op jit(solution)/shard_map/ppermute | solution.py:26
  38.3 2.4 %collective-permute-done.13 = bf16[16,4096]{1,0:T(8,128)(2,1)S(1)} collective-permute-done((bf16[16,4096]{1,0:T(8,128)(2,1)S(1)}, bf16[16,4096]{1,0:T(8,128)(2,1)S(1)}, u32[]{:S(2)}, u32[]{:S(2)}) %collective-permute-start.13) | collective-permute-done | bytes 131104 | tf_op jit(solution)/shard_map/ppermute | solution.py:26
  40.7 0.1 fusion.16
  40.8 0.1 collective-permute-start.14
  40.9 1.3 %collective-permute-start.15 = (bf16[4,4096]{1,0:T(4,128)(2,1)S(1)}, bf16[4,4096]{1,0:T(4,128)(2,1)S(1)}, u32[]{:S(2)}, u32[]{:S(2)}) collective-permute-start(bf16[4,4096]{1,0:T(4,128)(2,1)S(1)} %get-tuple-element.51), channel_id=1, source_target_pairs={{0,16},{1,17},{2,18},{3,19},{4,20},{5,21},{6,22},{7,23},{8,24},{9,... | collective-permute-start | bytes 98312 | tf_op jit(solution)/shard_map/ppermute | solution.py:26
  42.2 3.1 %collective-permute-start.16 = (bf16[4,4096]{1,0:T(4,128)(2,1)S(1)}, bf16[4,4096]{1,0:T(4,128)(2,1)S(1)}, u32[]{:S(2)}, u32[]{:S(2)}) collective-permute-start(bf16[4,4096]{1,0:T(4,128)(2,1)S(1)} %get-tuple-element.50), channel_id=1, source_target_pairs={{0,24},{1,25},{2,26},{3,27},{4,28},{5,29},{6,30},{7,31},{8,16},{9,... | collective-permute-start | bytes 98312 | tf_op jit(solution)/shard_map/ppermute | solution.py:26
  45.3 0.7 collective-permute-done.15
  46.0 1.9 %collective-permute-done.16 = bf16[4,4096]{1,0:T(4,128)(2,1)S(1)} collective-permute-done((bf16[4,4096]{1,0:T(4,128)(2,1)S(1)}, bf16[4,4096]{1,0:T(4,128)(2,1)S(1)}, u32[]{:S(2)}, u32[]{:S(2)}) %collective-permute-start.16) | collective-permute-done | bytes 32800 | tf_op jit(solution)/shard_map/ppermute | solution.py:26
  47.9 0.2 multiply_reduce_fusion
  48.1 0.1 multiply_convert_fusion
  48.2 0.1 concatenate.10.refs_0_
  48.3 0.0 collective-permute-start.17
  48.3 3.9 %collective-permute-start.18 = (bf16[4,4224]{1,0:T(4,128)(2,1)S(1)}, bf16[4,4224]{1,0:T(4,128)(2,1)S(1)}, u32[]{:S(2)}, u32[]{:S(2)}) collective-permute-start(bf16[4,4224]{1,0:T(4,128)(2,1)S(1)} %concatenate.10.refs_0_), channel_id=1, source_target_pairs={{0,16},{1,17},{2,18},{3,19},{4,20},{5,21},{6,22},{7,23},{8,24},{9,... | collective-permute-start | bytes 101384 | tf_op jit(solution)/shard_map/ppermute | solution.py:26
  52.3 0.4 collective-permute-start.19
  52.7 2.0 %collective-permute-done.18.refs_2_ = bf16[4,4224]{1,0:T(4,128)(2,1)S(1)} collective-permute-done((bf16[4,4224]{1,0:T(4,128)(2,1)S(1)}, bf16[4,4224]{1,0:T(4,128)(2,1)S(1)}, u32[]{:S(2)}, u32[]{:S(2)}) %collective-permute-start.18) | collective-permute-done | bytes 33824 | tf_op jit(solution)/shard_map/ppermute | solution.py:26
  54.7 3.3 %collective-permute-done.19.refs_3_ = bf16[4,4224]{1,0:T(4,128)(2,1)S(1)} collective-permute-done((bf16[4,4224]{1,0:T(4,128)(2,1)S(1)}, bf16[4,4224]{1,0:T(4,128)(2,1)S(1)}, u32[]{:S(2)}, u32[]{:S(2)}) %collective-permute-start.19) | collective-permute-done | bytes 33824 | tf_op jit(solution)/shard_map/ppermute | solution.py:26
  58.0 1.1 %collective-permute-start.20 = (bf16[16,4224]{1,0:T(8,128)(2,1)S(1)}, bf16[16,4224]{1,0:T(8,128)(2,1)S(1)}, u32[]{:S(2)}, u32[]{:S(2)}) collective-permute-start(bf16[16,4224]{1,0:T(8,128)(2,1)S(1)} %join.1.refs_0_), channel_id=1, source_target_pairs={{0,2},{1,3},{2,0},{3,1},{4,6},{5,7},{6,4},{7,5},{8,10},{9,11},{10,... | collective-permute-start | bytes 405512 | tf_op jit(solution)/shard_map/ppermute | solution.py:26
  59.2 1.0 %collective-permute-start.21 = (bf16[16,4224]{1,0:T(8,128)(2,1)S(1)}, bf16[16,4224]{1,0:T(8,128)(2,1)S(1)}, u32[]{:S(2)}, u32[]{:S(2)}) collective-permute-start(bf16[16,4224]{1,0:T(8,128)(2,1)S(1)} %join.1.refs_0_), channel_id=1, source_target_pairs={{0,4},{1,5},{2,6},{3,7},{4,0},{5,1},{6,2},{7,3},{8,12},{9,13},{10,... | collective-permute-start | bytes 405512 | tf_op jit(solution)/shard_map/ppermute | solution.py:26
  60.2 1.4 %collective-permute-start.22 = (bf16[16,4224]{1,0:T(8,128)(2,1)S(1)}, bf16[16,4224]{1,0:T(8,128)(2,1)S(1)}, u32[]{:S(2)}, u32[]{:S(2)}) collective-permute-start(bf16[16,4224]{1,0:T(8,128)(2,1)S(1)} %join.1.refs_0_), channel_id=1, source_target_pairs={{0,6},{1,7},{2,4},{3,5},{4,2},{5,3},{6,0},{7,1},{8,14},{9,15},{10,... | collective-permute-start | bytes 405512 | tf_op jit(solution)/shard_map/ppermute | solution.py:26
  61.6 1.5 %collective-permute-done.20.refs_1_ = bf16[16,4224]{1,0:T(8,128)(2,1)S(1)} collective-permute-done((bf16[16,4224]{1,0:T(8,128)(2,1)S(1)}, bf16[16,4224]{1,0:T(8,128)(2,1)S(1)}, u32[]{:S(2)}, u32[]{:S(2)}) %collective-permute-start.20) | collective-permute-done | bytes 135200 | tf_op jit(solution)/shard_map/ppermute | solution.py:26
  63.1 1.1 %collective-permute-done.21.refs_2_ = bf16[16,4224]{1,0:T(8,128)(2,1)S(1)} collective-permute-done((bf16[16,4224]{1,0:T(8,128)(2,1)S(1)}, bf16[16,4224]{1,0:T(8,128)(2,1)S(1)}, u32[]{:S(2)}, u32[]{:S(2)}) %collective-permute-start.21) | collective-permute-done | bytes 135200 | tf_op jit(solution)/shard_map/ppermute | solution.py:26
  64.2 1.9 %collective-permute-done.22.refs_3_ = bf16[16,4224]{1,0:T(8,128)(2,1)S(1)} collective-permute-done((bf16[16,4224]{1,0:T(8,128)(2,1)S(1)}, bf16[16,4224]{1,0:T(8,128)(2,1)S(1)}, u32[]{:S(2)}, u32[]{:S(2)}) %collective-permute-start.22) | collective-permute-done | bytes 135200 | tf_op jit(solution)/shard_map/ppermute | solution.py:26
  66.1 2.8 %prepare.4.refs_9_ = bf16[2048,768]{1,0:T(8,128)(2,1)S(1)} custom-call(f32[32,6]{1,0:T(8,128)S(1)} %bitcast.7, bf16[4096,768]{1,0:T(8,128)(2,1)} %bitcast.10), custom_call_target="tpu_custom_call" | custom-call | tf_op jit(solution)/shard_map/prepare/pallas_call | solution.py:201
  69.0 2.8 %prepare.5.refs_10_ = bf16[384,4096]{1,0:T(8,128)(2,1)S(1)} custom-call(f32[3,32]{1,0:T(4,128)S(1)} %bitcast.8, bf16[384,4096]{1,0:T(8,128)(2,1)} %bitcast.11), custom_call_target="tpu_custom_call" | custom-call | tf_op jit(solution)/shard_map/prepare/pallas_call | solution.py:201
  71.8 2.2 %expert.1 = (f32[64,4096]{1,0:T(8,128)S(1)}, bf16[64,4096]{1,0:T(8,128)(2,1)S(1)}) custom-call(bf16[16,4224]{1,0:T(8,128)(2,1)S(1)} %join.1.refs_0_, bf16[16,4224]{1,0:T(8,128)(2,1)S(1)} %collective-permute-done.20.refs_1_, bf16[16,4224]{1,0:T(8,128)(2,1)S(1)} %collective-permute-done.21.refs_2_, bf16[16,4224]{1,0:T(8,128)(2,1)S(1)} %collective-permute-done.22.refs_3_, ...), custom_call_target="tpu_custom_call" | custom-call | tf_op jit(solution)/shard_map/expert/pallas_call | solution.py:375
  74.0 0.6 collective-permute-start.27
  74.6 1.5 %collective-permute-done.27 = bf16[64,4096]{1,0:T(8,128)(2,1)S(1)} collective-permute-done((bf16[64,4096]{1,0:T(8,128)(2,1)S(1)}, bf16[64,4096]{1,0:T(8,128)(2,1)S(1)}, u32[]{:S(2)}, u32[]{:S(2)}) %collective-permute-start.27) | collective-permute-done | bytes 524320 | tf_op jit(solution)/shard_map/ppermute | solution.py:26
  76.1 0.1 fusion.14
  76.3 1.0 %collective-permute-start.28 = (bf16[16,4096]{1,0:T(8,128)(2,1)S(1)}, bf16[16,4096]{1,0:T(8,128)(2,1)S(1)}, u32[]{:S(2)}, u32[]{:S(2)}) collective-permute-start(bf16[16,4096]{1,0:T(8,128)(2,1)S(1)} %get-tuple-element.40), channel_id=1, source_target_pairs={{0,2},{1,3},{2,0},{3,1},{4,6},{5,7},{6,4},{7,5},{8,10},{9,11},{10,... | collective-permute-start | bytes 393224 | tf_op jit(solution)/shard_map/ppermute | solution.py:26
  77.3 1.0 %collective-permute-start.29 = (bf16[16,4096]{1,0:T(8,128)(2,1)S(1)}, bf16[16,4096]{1,0:T(8,128)(2,1)S(1)}, u32[]{:S(2)}, u32[]{:S(2)}) collective-permute-start(bf16[16,4096]{1,0:T(8,128)(2,1)S(1)} %get-tuple-element.42), channel_id=1, source_target_pairs={{0,4},{1,5},{2,6},{3,7},{4,0},{5,1},{6,2},{7,3},{8,12},{9,13},{10,... | collective-permute-start | bytes 393224 | tf_op jit(solution)/shard_map/ppermute | solution.py:26
  78.3 1.5 %collective-permute-start.30 = (bf16[16,4096]{1,0:T(8,128)(2,1)S(1)}, bf16[16,4096]{1,0:T(8,128)(2,1)S(1)}, u32[]{:S(2)}, u32[]{:S(2)}) collective-permute-start(bf16[16,4096]{1,0:T(8,128)(2,1)S(1)} %get-tuple-element.41), channel_id=1, source_target_pairs={{0,6},{1,7},{2,4},{3,5},{4,2},{5,3},{6,0},{7,1},{8,14},{9,15},{10,... | collective-permute-start | bytes 393224 | tf_op jit(solution)/shard_map/ppermute | solution.py:26
  79.8 2.9 %collective-permute-done.28 = bf16[16,4096]{1,0:T(8,128)(2,1)S(1)} collective-permute-done((bf16[16,4096]{1,0:T(8,128)(2,1)S(1)}, bf16[16,4096]{1,0:T(8,128)(2,1)S(1)}, u32[]{:S(2)}, u32[]{:S(2)}) %collective-permute-start.28) | collective-permute-done | bytes 131104 | tf_op jit(solution)/shard_map/ppermute | solution.py:26
  82.7 2.9 %collective-permute-done.29 = bf16[16,4096]{1,0:T(8,128)(2,1)S(1)} collective-permute-done((bf16[16,4096]{1,0:T(8,128)(2,1)S(1)}, bf16[16,4096]{1,0:T(8,128)(2,1)S(1)}, u32[]{:S(2)}, u32[]{:S(2)}) %collective-permute-start.29) | collective-permute-done | bytes 131104 | tf_op jit(solution)/shard_map/ppermute | solution.py:26
  85.6 0.1 fusion.12
  85.8 0.1 collective-permute-start.31
  85.8 1.1 %collective-permute-start.32 = (bf16[4,4096]{1,0:T(4,128)(2,1)S(1)}, bf16[4,4096]{1,0:T(4,128)(2,1)S(1)}, u32[]{:S(2)}, u32[]{:S(2)}) collective-permute-start(bf16[4,4096]{1,0:T(4,128)(2,1)S(1)} %get-tuple-element.48), channel_id=1, source_target_pairs={{0,16},{1,17},{2,18},{3,19},{4,20},{5,21},{6,22},{7,23},{8,24},{9,... | collective-permute-start | bytes 98312 | tf_op jit(solution)/shard_map/ppermute | solution.py:26
  86.9 3.3 %collective-permute-start.33 = (bf16[4,4096]{1,0:T(4,128)(2,1)S(1)}, bf16[4,4096]{1,0:T(4,128)(2,1)S(1)}, u32[]{:S(2)}, u32[]{:S(2)}) collective-permute-start(bf16[4,4096]{1,0:T(4,128)(2,1)S(1)} %get-tuple-element.47), channel_id=1, source_target_pairs={{0,24},{1,25},{2,26},{3,27},{4,28},{5,29},{6,30},{7,31},{8,16},{9,... | collective-permute-start | bytes 98312 | tf_op jit(solution)/shard_map/ppermute | solution.py:26
  90.2 0.8 collective-permute-done.32
  91.0 1.7 %collective-permute-done.33 = bf16[4,4096]{1,0:T(4,128)(2,1)S(1)} collective-permute-done((bf16[4,4096]{1,0:T(4,128)(2,1)S(1)}, bf16[4,4096]{1,0:T(4,128)(2,1)S(1)}, u32[]{:S(2)}, u32[]{:S(2)}) %collective-permute-start.33) | collective-permute-done | bytes 32800 | tf_op jit(solution)/shard_map/ppermute | solution.py:26
  92.6 0.7 fusion.7
  (42 shorter events, 0.3 us)
Async XLA Ops:
  1.7 7.2 %collective-permute-start = (bf16[88,256]{1,0:T(8,128)(2,1)S(1)}, bf16[88,256]{1,0:T(8,128)(2,1)S(1)}, u32[]{:S(2)}, u32[]{:S(2)}) collective-permute-start(bf16[88,256]{1,0:T(8,128)(2,1)S(1)} %get-tuple-element.17), channel_id=1, source_target_pairs={{0,8},{1,9},{2,10},{3,11},{4,12},{5,13},{6,14},{7,15},{8,0},{9,1},... | collective-permute-start | bytes 135176 | tf_op jit(solution)/shard_map/ppermute | solution.py:26
  4.8 5.8 %collective-permute-start.1 = (bf16[88,256]{1,0:T(8,128)(2,1)S(1)}, bf16[88,256]{1,0:T(8,128)(2,1)S(1)}, u32[]{:S(2)}, u32[]{:S(2)}) collective-permute-start(bf16[88,256]{1,0:T(8,128)(2,1)S(1)} %get-tuple-element.18), channel_id=1, source_target_pairs={{0,16},{1,17},{2,18},{3,19},{4,20},{5,21},{6,22},{7,23},{8,24},{9,... | collective-permute-start | bytes 135176 | tf_op jit(solution)/shard_map/ppermute | solution.py:26
  7.4 5.8 %collective-permute-start.2 = (bf16[88,256]{1,0:T(8,128)(2,1)S(1)}, bf16[88,256]{1,0:T(8,128)(2,1)S(1)}, u32[]{:S(2)}, u32[]{:S(2)}) collective-permute-start(bf16[88,256]{1,0:T(8,128)(2,1)S(1)} %get-tuple-element.19), channel_id=1, source_target_pairs={{0,24},{1,25},{2,26},{3,27},{4,28},{5,29},{6,30},{7,31},{8,16},{9,... | collective-permute-start | bytes 135176 | tf_op jit(solution)/shard_map/ppermute | solution.py:26
  13.3 6.4 %collective-permute-start.3 = (bf16[4,72,256]{2,1,0:T(8,128)(2,1)S(1)}, bf16[4,72,256]{2,1,0:T(8,128)(2,1)S(1)}, u32[]{:S(2)}, u32[]{:S(2)}) collective-permute-start(bf16[4,72,256]{2,1,0:T(8,128)(2,1)S(1)} %get-tuple-element.21), channel_id=1, source_target_pairs={{0,2},{1,3},{2,0},{3,1},{4,6},{5,7},{6,4},{7,5},{8,10},{9,11},{10,... | collective-permute-start | bytes 442376 | tf_op jit(solution)/shard_map/ppermute | solution.py:26
  14.9 7.8 %collective-permute-start.4 = (bf16[4,72,256]{2,1,0:T(8,128)(2,1)S(1)}, bf16[4,72,256]{2,1,0:T(8,128)(2,1)}, u32[]{:S(2)}, u32[]{:S(2)}) collective-permute-start(bf16[4,72,256]{2,1,0:T(8,128)(2,1)S(1)} %get-tuple-element.22), channel_id=1, source_target_pairs={{0,4},{1,5},{2,6},{3,7},{4,0},{5,1},{6,2},{7,3},{8,12},{9,13},{10,... | collective-permute-start | bytes 442376 | tf_op jit(solution)/shard_map/ppermute | solution.py:26
  16.4 6.3 %collective-permute-start.5 = (bf16[4,72,256]{2,1,0:T(8,128)(2,1)S(1)}, bf16[4,72,256]{2,1,0:T(8,128)(2,1)}, u32[]{:S(2)}, u32[]{:S(2)}) collective-permute-start(bf16[4,72,256]{2,1,0:T(8,128)(2,1)S(1)} %get-tuple-element.23), channel_id=1, source_target_pairs={{0,6},{1,7},{2,4},{3,5},{4,2},{5,3},{6,0},{7,1},{8,14},{9,15},{10,... | collective-permute-start | bytes 442376 | tf_op jit(solution)/shard_map/ppermute | solution.py:26
  16.9 10.1 %collective-permute-start.6 = (bf16[4,72,256]{2,1,0:T(8,128)(2,1)S(1)}, bf16[4,72,256]{2,1,0:T(8,128)(2,1)}, u32[]{:S(2)}, u32[]{:S(2)}) collective-permute-start(bf16[4,72,256]{2,1,0:T(8,128)(2,1)S(1)} %get-tuple-element.20.refs_0_), channel_id=1, source_target_pairs={{0,1},{1,0},{2,3},{3,2},{4,5},{5,4},{6,7},{7,6},{8,9},{9,8},{10,11... | collective-permute-start | bytes 442376 | tf_op jit(solution)/shard_map/ppermute | solution.py:26
  19.7 7.3 %collective-permute-start.7 = (bf16[4,72,256]{2,1,0:T(8,128)(2,1)S(1)}, bf16[4,72,256]{2,1,0:T(8,128)(2,1)}, u32[]{:S(2)}, u32[]{:S(2)}) collective-permute-start(bf16[4,72,256]{2,1,0:T(8,128)(2,1)S(1)} %collective-permute-done.3.refs_1_), channel_id=1, source_target_pairs={{0,1},{1,0},{2,3},{3,2},{4,5},{5,4},{6,7},{7,6},{8,9},{9,8},{10,11... | collective-permute-start | bytes 442376 | tf_op jit(solution)/shard_map/ppermute | solution.py:26
  22.7 4.4 %collective-permute-start.8 = (bf16[4,72,256]{2,1,0:T(8,128)(2,1)}, bf16[4,72,256]{2,1,0:T(8,128)(2,1)}, u32[]{:S(2)}, u32[]{:S(2)}) collective-permute-start(bf16[4,72,256]{2,1,0:T(8,128)(2,1)} %collective-permute-done.4.refs_2_), channel_id=1, source_target_pairs={{0,1},{1,0},{2,3},{3,2},{4,5},{5,4},{6,7},{7,6},{8,9},{9,8},{10,11... | collective-permute-start | bytes 442376 | tf_op jit(solution)/shard_map/ppermute | solution.py:26
  22.7 4.4 %collective-permute-start.9 = (bf16[4,72,256]{2,1,0:T(8,128)(2,1)}, bf16[4,72,256]{2,1,0:T(8,128)(2,1)}, u32[]{:S(2)}, u32[]{:S(2)}) collective-permute-start(bf16[4,72,256]{2,1,0:T(8,128)(2,1)} %collective-permute-done.5.refs_3_), channel_id=1, source_target_pairs={{0,1},{1,0},{2,3},{3,2},{4,5},{5,4},{6,7},{7,6},{8,9},{9,8},{10,11... | collective-permute-start | bytes 442376 | tf_op jit(solution)/shard_map/ppermute | solution.py:26
  27.0 8.4 %copy-start.2 = (f32[4,8]{1,0:T(4,128)S(1)}, f32[4,8]{1,0:T(4,128)}, u32[]{:S(2)}) copy-start(f32[4,8]{1,0:T(4,128)} %param.27) | copy-start | bytes 388
  27.0 8.4 %copy-start.3 = (s32[4,8]{1,0:T(4,128)S(1)}, s32[4,8]{1,0:T(4,128)}, u32[]{:S(2)}) copy-start(s32[4,8]{1,0:T(4,128)} %param.26) | copy-start | bytes 388
  29.7 18.2 %copy-start = (bf16[4,4096]{1,0:T(4,128)(2,1)S(1)}, bf16[4,4096]{1,0:T(4,128)(2,1)}, u32[]{:S(2)}) copy-start(bf16[4,4096]{1,0:T(4,128)(2,1)} %param.23) | copy-start | bytes 98308
  29.7 18.4 %copy-start.1 = (f32[4096]{0:T(1024)S(1)}, f32[4096]{0:T(1024)}, u32[]{:S(2)}) copy-start(f32[4096]{0:T(1024)} %param.25) | copy-start | bytes 49156
  29.7 2.0 %collective-permute-start.10 = (bf16[64,4096]{1,0:T(8,128)(2,1)S(1)}, bf16[64,4096]{1,0:T(8,128)(2,1)S(1)}, u32[]{:S(2)}, u32[]{:S(2)}) collective-permute-start(bf16[64,4096]{1,0:T(8,128)(2,1)S(1)} %get-tuple-element.26), channel_id=1, source_target_pairs={{0,1},{1,0},{2,3},{3,2},{4,5},{5,4},{6,7},{7,6},{8,9},{9,8},{10,11... | collective-permute-start | bytes 1572872 | tf_op jit(solution)/shard_map/ppermute | solution.py:26
  31.8 6.4 %collective-permute-start.11 = (bf16[16,4096]{1,0:T(8,128)(2,1)S(1)}, bf16[16,4096]{1,0:T(8,128)(2,1)S(1)}, u32[]{:S(2)}, u32[]{:S(2)}) collective-permute-start(bf16[16,4096]{1,0:T(8,128)(2,1)S(1)} %get-tuple-element.43), channel_id=1, source_target_pairs={{0,2},{1,3},{2,0},{3,1},{4,6},{5,7},{6,4},{7,5},{8,10},{9,11},{10,... | collective-permute-start | bytes 393224 | tf_op jit(solution)/shard_map/ppermute | solution.py:26
  31.9 6.3 %collective-permute-start.12 = (bf16[16,4096]{1,0:T(8,128)(2,1)S(1)}, bf16[16,4096]{1,0:T(8,128)(2,1)S(1)}, u32[]{:S(2)}, u32[]{:S(2)}) collective-permute-start(bf16[16,4096]{1,0:T(8,128)(2,1)S(1)} %get-tuple-element.45), channel_id=1, source_target_pairs={{0,4},{1,5},{2,6},{3,7},{4,0},{5,1},{6,2},{7,3},{8,12},{9,13},{10,... | collective-permute-start | bytes 393224 | tf_op jit(solution)/shard_map/ppermute | solution.py:26
  33.2 7.5 %collective-permute-start.13 = (bf16[16,4096]{1,0:T(8,128)(2,1)S(1)}, bf16[16,4096]{1,0:T(8,128)(2,1)S(1)}, u32[]{:S(2)}, u32[]{:S(2)}) collective-permute-start(bf16[16,4096]{1,0:T(8,128)(2,1)S(1)} %get-tuple-element.44), channel_id=1, source_target_pairs={{0,6},{1,7},{2,4},{3,5},{4,2},{5,3},{6,0},{7,1},{8,14},{9,15},{10,... | collective-permute-start | bytes 393224 | tf_op jit(solution)/shard_map/ppermute | solution.py:26
  40.8 4.5 %collective-permute-start.14 = (bf16[4,4096]{1,0:T(4,128)(2,1)S(1)}, bf16[4,4096]{1,0:T(4,128)(2,1)S(1)}, u32[]{:S(2)}, u32[]{:S(2)}) collective-permute-start(bf16[4,4096]{1,0:T(4,128)(2,1)S(1)} %get-tuple-element.49), channel_id=1, source_target_pairs={{0,8},{1,9},{2,10},{3,11},{4,12},{5,13},{6,14},{7,15},{8,0},{9,1},... | collective-permute-start | bytes 98312 | tf_op jit(solution)/shard_map/ppermute | solution.py:26
  40.9 5.1 %collective-permute-start.15 = (bf16[4,4096]{1,0:T(4,128)(2,1)S(1)}, bf16[4,4096]{1,0:T(4,128)(2,1)S(1)}, u32[]{:S(2)}, u32[]{:S(2)}) collective-permute-start(bf16[4,4096]{1,0:T(4,128)(2,1)S(1)} %get-tuple-element.51), channel_id=1, source_target_pairs={{0,16},{1,17},{2,18},{3,19},{4,20},{5,21},{6,22},{7,23},{8,24},{9,... | collective-permute-start | bytes 98312 | tf_op jit(solution)/shard_map/ppermute | solution.py:26
  42.2 5.7 %collective-permute-start.16 = (bf16[4,4096]{1,0:T(4,128)(2,1)S(1)}, bf16[4,4096]{1,0:T(4,128)(2,1)S(1)}, u32[]{:S(2)}, u32[]{:S(2)}) collective-permute-start(bf16[4,4096]{1,0:T(4,128)(2,1)S(1)} %get-tuple-element.50), channel_id=1, source_target_pairs={{0,24},{1,25},{2,26},{3,27},{4,28},{5,29},{6,30},{7,31},{8,16},{9,... | collective-permute-start | bytes 98312 | tf_op jit(solution)/shard_map/ppermute | solution.py:26
  48.3 4.4 %collective-permute-start.17 = (bf16[4,4224]{1,0:T(4,128)(2,1)S(1)}, bf16[4,4224]{1,0:T(4,128)(2,1)S(1)}, u32[]{:S(2)}, u32[]{:S(2)}) collective-permute-start(bf16[4,4224]{1,0:T(4,128)(2,1)S(1)} %concatenate.10.refs_0_), channel_id=1, source_target_pairs={{0,8},{1,9},{2,10},{3,11},{4,12},{5,13},{6,14},{7,15},{8,0},{9,1},... | collective-permute-start | bytes 101384 | tf_op jit(solution)/shard_map/ppermute | solution.py:26
  48.3 6.4 %collective-permute-start.18 = (bf16[4,4224]{1,0:T(4,128)(2,1)S(1)}, bf16[4,4224]{1,0:T(4,128)(2,1)S(1)}, u32[]{:S(2)}, u32[]{:S(2)}) collective-permute-start(bf16[4,4224]{1,0:T(4,128)(2,1)S(1)} %concatenate.10.refs_0_), channel_id=1, source_target_pairs={{0,16},{1,17},{2,18},{3,19},{4,20},{5,21},{6,22},{7,23},{8,24},{9,... | collective-permute-start | bytes 101384 | tf_op jit(solution)/shard_map/ppermute | solution.py:26
  52.3 5.7 %collective-permute-start.19 = (bf16[4,4224]{1,0:T(4,128)(2,1)S(1)}, bf16[4,4224]{1,0:T(4,128)(2,1)S(1)}, u32[]{:S(2)}, u32[]{:S(2)}) collective-permute-start(bf16[4,4224]{1,0:T(4,128)(2,1)S(1)} %concatenate.10.refs_0_), channel_id=1, source_target_pairs={{0,24},{1,25},{2,26},{3,27},{4,28},{5,29},{6,30},{7,31},{8,16},{9,... | collective-permute-start | bytes 101384 | tf_op jit(solution)/shard_map/ppermute | solution.py:26
  58.0 10.9 %copy-start.4 = (f32[1,3,32]{2,0,1:T(1,128)S(1)}, f32[1,3,32]{2,0,1:T(1,128)}, u32[]{:S(2)}) copy-start(f32[1,3,32]{2,0,1:T(1,128)} %param.31) | copy-start | bytes 1156
  58.0 5.1 %collective-permute-start.20 = (bf16[16,4224]{1,0:T(8,128)(2,1)S(1)}, bf16[16,4224]{1,0:T(8,128)(2,1)S(1)}, u32[]{:S(2)}, u32[]{:S(2)}) collective-permute-start(bf16[16,4224]{1,0:T(8,128)(2,1)S(1)} %join.1.refs_0_), channel_id=1, source_target_pairs={{0,2},{1,3},{2,0},{3,1},{4,6},{5,7},{6,4},{7,5},{8,10},{9,11},{10,... | collective-permute-start | bytes 405512 | tf_op jit(solution)/shard_map/ppermute | solution.py:26
  59.2 5.0 %collective-permute-start.21 = (bf16[16,4224]{1,0:T(8,128)(2,1)S(1)}, bf16[16,4224]{1,0:T(8,128)(2,1)S(1)}, u32[]{:S(2)}, u32[]{:S(2)}) collective-permute-start(bf16[16,4224]{1,0:T(8,128)(2,1)S(1)} %join.1.refs_0_), channel_id=1, source_target_pairs={{0,4},{1,5},{2,6},{3,7},{4,0},{5,1},{6,2},{7,3},{8,12},{9,13},{10,... | collective-permute-start | bytes 405512 | tf_op jit(solution)/shard_map/ppermute | solution.py:26
  60.2 5.9 %collective-permute-start.22 = (bf16[16,4224]{1,0:T(8,128)(2,1)S(1)}, bf16[16,4224]{1,0:T(8,128)(2,1)S(1)}, u32[]{:S(2)}, u32[]{:S(2)}) collective-permute-start(bf16[16,4224]{1,0:T(8,128)(2,1)S(1)} %join.1.refs_0_), channel_id=1, source_target_pairs={{0,6},{1,7},{2,4},{3,5},{4,2},{5,3},{6,0},{7,1},{8,14},{9,15},{10,... | collective-permute-start | bytes 405512 | tf_op jit(solution)/shard_map/ppermute | solution.py:26
  61.6 10.2 %collective-permute-start.23 = (bf16[16,4224]{1,0:T(8,128)(2,1)S(1)}, bf16[16,4224]{1,0:T(8,128)(2,1)S(1)}, u32[]{:S(2)}, u32[]{:S(2)}) collective-permute-start(bf16[16,4224]{1,0:T(8,128)(2,1)S(1)} %join.1.refs_0_), channel_id=1, source_target_pairs={{0,1},{1,0},{2,3},{3,2},{4,5},{5,4},{6,7},{7,6},{8,9},{9,8},{10,11... | collective-permute-start | bytes 405512 | tf_op jit(solution)/shard_map/ppermute | solution.py:26
  63.1 8.6 %collective-permute-start.24 = (bf16[16,4224]{1,0:T(8,128)(2,1)S(1)}, bf16[16,4224]{1,0:T(8,128)(2,1)S(1)}, u32[]{:S(2)}, u32[]{:S(2)}) collective-permute-start(bf16[16,4224]{1,0:T(8,128)(2,1)S(1)} %collective-permute-done.20.refs_1_), channel_id=1, source_target_pairs={{0,1},{1,0},{2,3},{3,2},{4,5},{5,4},{6,7},{7,6},{8,9},{9,8},{10,11... | collective-permute-start | bytes 405512 | tf_op jit(solution)/shard_map/ppermute | solution.py:26
  64.2 7.6 %collective-permute-start.25 = (bf16[16,4224]{1,0:T(8,128)(2,1)S(1)}, bf16[16,4224]{1,0:T(8,128)(2,1)S(1)}, u32[]{:S(2)}, u32[]{:S(2)}) collective-permute-start(bf16[16,4224]{1,0:T(8,128)(2,1)S(1)} %collective-permute-done.21.refs_2_), channel_id=1, source_target_pairs={{0,1},{1,0},{2,3},{3,2},{4,5},{5,4},{6,7},{7,6},{8,9},{9,8},{10,11... | collective-permute-start | bytes 405512 | tf_op jit(solution)/shard_map/ppermute | solution.py:26
  66.1 5.7 %collective-permute-start.26 = (bf16[16,4224]{1,0:T(8,128)(2,1)S(1)}, bf16[16,4224]{1,0:T(8,128)(2,1)S(1)}, u32[]{:S(2)}, u32[]{:S(2)}) collective-permute-start(bf16[16,4224]{1,0:T(8,128)(2,1)S(1)} %collective-permute-done.22.refs_3_), channel_id=1, source_target_pairs={{0,1},{1,0},{2,3},{3,2},{4,5},{5,4},{6,7},{7,6},{8,9},{9,8},{10,11... | collective-permute-start | bytes 405512 | tf_op jit(solution)/shard_map/ppermute | solution.py:26
  74.0 2.1 %collective-permute-start.27 = (bf16[64,4096]{1,0:T(8,128)(2,1)S(1)}, bf16[64,4096]{1,0:T(8,128)(2,1)S(1)}, u32[]{:S(2)}, u32[]{:S(2)}) collective-permute-start(bf16[64,4096]{1,0:T(8,128)(2,1)S(1)} %get-tuple-element.29), channel_id=1, source_target_pairs={{0,1},{1,0},{2,3},{3,2},{4,5},{5,4},{6,7},{7,6},{8,9},{9,8},{10,11... | collective-permute-start | bytes 1572872 | tf_op jit(solution)/shard_map/ppermute | solution.py:26
  76.3 6.4 %collective-permute-start.28 = (bf16[16,4096]{1,0:T(8,128)(2,1)S(1)}, bf16[16,4096]{1,0:T(8,128)(2,1)S(1)}, u32[]{:S(2)}, u32[]{:S(2)}) collective-permute-start(bf16[16,4096]{1,0:T(8,128)(2,1)S(1)} %get-tuple-element.40), channel_id=1, source_target_pairs={{0,2},{1,3},{2,0},{3,1},{4,6},{5,7},{6,4},{7,5},{8,10},{9,11},{10,... | collective-permute-start | bytes 393224 | tf_op jit(solution)/shard_map/ppermute | solution.py:26
  77.3 8.3 %collective-permute-start.29 = (bf16[16,4096]{1,0:T(8,128)(2,1)S(1)}, bf16[16,4096]{1,0:T(8,128)(2,1)S(1)}, u32[]{:S(2)}, u32[]{:S(2)}) collective-permute-start(bf16[16,4096]{1,0:T(8,128)(2,1)S(1)} %get-tuple-element.42), channel_id=1, source_target_pairs={{0,4},{1,5},{2,6},{3,7},{4,0},{5,1},{6,2},{7,3},{8,12},{9,13},{10,... | collective-permute-start | bytes 393224 | tf_op jit(solution)/shard_map/ppermute | solution.py:26
  78.3 7.3 %collective-permute-start.30 = (bf16[16,4096]{1,0:T(8,128)(2,1)S(1)}, bf16[16,4096]{1,0:T(8,128)(2,1)S(1)}, u32[]{:S(2)}, u32[]{:S(2)}) collective-permute-start(bf16[16,4096]{1,0:T(8,128)(2,1)S(1)} %get-tuple-element.41), channel_id=1, source_target_pairs={{0,6},{1,7},{2,4},{3,5},{4,2},{5,3},{6,0},{7,1},{8,14},{9,15},{10,... | collective-permute-start | bytes 393224 | tf_op jit(solution)/shard_map/ppermute | solution.py:26
  85.8 4.5 %collective-permute-start.31 = (bf16[4,4096]{1,0:T(4,128)(2,1)S(1)}, bf16[4,4096]{1,0:T(4,128)(2,1)S(1)}, u32[]{:S(2)}, u32[]{:S(2)}) collective-permute-start(bf16[4,4096]{1,0:T(4,128)(2,1)S(1)} %get-tuple-element.46), channel_id=1, source_target_pairs={{0,8},{1,9},{2,10},{3,11},{4,12},{5,13},{6,14},{7,15},{8,0},{9,1},... | collective-permute-start | bytes 98312 | tf_op jit(solution)/shard_map/ppermute | solution.py:26
  85.8 5.1 %collective-permute-start.32 = (bf16[4,4096]{1,0:T(4,128)(2,1)S(1)}, bf16[4,4096]{1,0:T(4,128)(2,1)S(1)}, u32[]{:S(2)}, u32[]{:S(2)}) collective-permute-start(bf16[4,4096]{1,0:T(4,128)(2,1)S(1)} %get-tuple-element.48), channel_id=1, source_target_pairs={{0,16},{1,17},{2,18},{3,19},{4,20},{5,21},{6,22},{7,23},{8,24},{9,... | collective-permute-start | bytes 98312 | tf_op jit(solution)/shard_map/ppermute | solution.py:26
  86.9 5.7 %collective-permute-start.33 = (bf16[4,4096]{1,0:T(4,128)(2,1)S(1)}, bf16[4,4096]{1,0:T(4,128)(2,1)S(1)}, u32[]{:S(2)}, u32[]{:S(2)}) collective-permute-start(bf16[4,4096]{1,0:T(4,128)(2,1)S(1)} %get-tuple-element.47), channel_id=1, source_target_pairs={{0,24},{1,25},{2,26},{3,27},{4,28},{5,29},{6,30},{7,31},{8,16},{9,... | collective-permute-start | bytes 98312 | tf_op jit(solution)/shard_map/ppermute | solution.py:26

commit v3 on v2

--- a/solution.py
+++ b/solution.py
@@ -68,7 +68,7 @@
         out[top : top + rows, HD : 2 * HD] = own_value[:, lanes]
 
 
-def repack_body(after, *refs, kv_rows, rows):
+def repack_body(after, also, *refs, kv_rows, rows):
     outs = refs[-MID:]
     parts = refs[:-MID]
     for zx, part in enumerate(parts):
@@ -82,7 +82,8 @@
 
 def attend_body(info, *refs, ctx_local, kv_rows, rows):
     mine, other = refs[:MID], refs[MID : 2 * MID]
-    w_out, keep, send, att = refs[2 * MID :]
+    w_out, keep = refs[2 * MID : 2 * MID + 2]
+    sends, att = refs[2 * MID + 2 : -1], refs[-1]
     device = lax.axis_index("ctx")
     high = mine[0].shape[0]
     pieces = MID * high
@@ -145,15 +146,18 @@
     attended = att[...].reshape(2 * half, HD).astype(jnp.bfloat16)
     out = jnp.dot(attended, w_out[...], preferred_element_type=jnp.float32)
     keep[...] = out[0:half]
-    send[...] = out[half:].astype(jnp.bfloat16)
+    for i, send in enumerate(sends):
+        count = send.shape[0]
+        send[...] = out[half + i * count : half + (i + 1) * count].astype(jnp.bfloat16)
 
 
 def dequantize_strips(out, codes, scales, first, count, offset):
+    across = codes.shape[1] // BLK
     for i in range(first, first + count):
         rows = slice(i * BLK, (i + 1) * BLK)
         for j in range(codes.shape[1] // BLK):
             lanes = slice(j * BLK, (j + 1) * BLK)
-            out[rows, lanes] = (codes[rows, lanes].astype(jnp.float32) * scales[offset + i, j]).astype(jnp.bfloat16)
+            out[rows, lanes] = (codes[rows, lanes].astype(jnp.float32) * scales[offset + i * across + j]).astype(jnp.bfloat16)
 
 
 def strip_rows(shape):
@@ -166,17 +170,17 @@
 
 def prepare_body(*refs, ranges, fetched):
     count = len(ranges)
-    scales, sources, plain = refs[:count], refs[count : 2 * count], refs[2 * count : 2 * count + fetched]
-    refs = refs[2 * count + fetched :]
+    scales, sources, plain = refs[0], refs[1 : 1 + count], refs[1 + count : 1 + count + fetched]
+    refs = refs[1 + count + fetched :]
     outs, fetch, held, sems = refs[:count], refs[count : count + fetched], refs[count + fetched : -1], refs[-1]
     jobs = []
-    for scale, source, to, out, (start, size) in zip(scales, sources, held, outs, ranges):
+    for source, to, out, (start, size, base) in zip(sources, held, outs, ranges):
         step = strip_rows((size, source.shape[1]))
         for first in range(0, size, step):
             copy = pltpu.make_async_copy(
                 source.at[pl.ds(start + first, step)], to.at[pl.ds(first, step)], sems.at[len(jobs)]
             )
-            jobs.append((copy, (out, to, scale, first // BLK, step // BLK, start // BLK)))
+            jobs.append((copy, (out, to, scales, first // BLK, step // BLK, base)))
     direct = [pltpu.make_async_copy(a, to, sems.at[len(jobs) + i]) for i, (a, to) in enumerate(zip(plain, fetch))]
     for copy, _ in jobs[:DEPTH]:
         copy.start()
@@ -191,23 +195,22 @@
         copy.wait()
 
 
-def prepared(weights, fetch=()):
-    scales = [item[0] for item in weights]
-    codes = [item[1] for item in weights]
-    ranges = tuple(item[2:] for item in weights)
+def prepared(scales, weights, fetch=()):
+    codes = [item[0] for item in weights]
+    ranges = tuple(item[1:] for item in weights)
     fetch = list(fetch)
-    shapes = [(size, a.shape[1]) for a, (_, size) in zip(codes, ranges)]
+    shapes = [(size, a.shape[1]) for a, (_, size, _) in zip(codes, ranges)]
     steps = sum(shape[0] // strip_rows(shape) for shape in shapes)
     return pl.pallas_call(
         functools.partial(prepare_body, ranges=ranges, fetched=len(fetch)),
-        in_specs=[SMEM] * len(codes) + [HBM] * (len(codes) + len(fetch)),
+        in_specs=[SMEM] + [HBM] * (len(codes) + len(fetch)),
         out_specs=[VMEM] * (len(codes) + len(fetch)),
         out_shape=[pltpu.VMEM(shape, jnp.bfloat16) for shape in shapes] + [pltpu.VMEM(a.shape, a.dtype) for a in fetch],
         scratch_shapes=[pltpu.VMEM(shape, jnp.bfloat16) for shape in shapes]
         + [pltpu.SemaphoreType.DMA((steps + len(fetch),))],
         compiler_params=pltpu.CompilerParams(vmem_limit_bytes=2 * sum(math.prod(shape) for shape in shapes) + 2**20),
         name="prepare",
-    )(*scales, *(in_hbm(item) for item in codes + fetch))
+    )(scales, *(in_hbm(item) for item in codes + fetch))
 
 
 def join_body(*refs):
@@ -231,7 +234,8 @@
 
 def expert_body(*refs, width, experts):
     parts = refs[: 2 * MID]
-    gate_first, gate_rest, down, keep, send, x = refs[2 * MID :]
+    gate_first, gate_rest, down, keep = refs[2 * MID : 2 * MID + 4]
+    sends, x = refs[2 * MID + 4 : -1], refs[-1]
     expert = lax.axis_index("ctx") // 2
     some = parts[0].shape[0]
     half = keep.shape[0]
@@ -249,7 +253,9 @@
     active = (gate / (1.0 + jnp.exp(-gate)) * up).astype(jnp.bfloat16)
     out = jnp.dot(active, down[...], preferred_element_type=jnp.float32) * weight
     keep[...] = out[0:half]
-    send[...] = out[half:].astype(jnp.bfloat16)
+    for i, send in enumerate(sends):
+        count = send.shape[0]
+        send[...] = out[half + i * count : half + (i + 1) * count].astype(jnp.bfloat16)
 
 
 VMEM = pl.BlockSpec(memory_space=pltpu.VMEM)
@@ -258,17 +264,36 @@
 ANY = pl.BlockSpec(memory_space=pl.ANY)
 
 
-def scatter_sum(keep, send, mid, high):
+def add_body(keep, got, out, *, first):
+    out[...] = (keep[first : first + out.shape[0], :] + got[...].astype(jnp.float32)).astype(out.dtype)
+
+
+def added(keep, got, first):
+    return pl.pallas_call(
+        functools.partial(add_body, first=first),
+        in_specs=[VMEM] * 2,
+        out_specs=VMEM,
+        out_shape=jax.ShapeDtypeStruct(got.shape, got.dtype),
+        compiler_params=pltpu.CompilerParams(vmem_limit_bytes=keep.size * 4 + got.size * 8 + 2**20),
+        name="add",
+    )(keep, got)
+
+
+def scatter_sum(keep, sends, mid, high):
     width = keep.shape[1]
-    summed = keep + swapped(send, 1).astype(jnp.float32)
-    for offsets in (mid, high):
-        parts = summed.reshape(len(offsets), -1, width)
-        total = parts[0]
-        got = [swapped(parts[i].astype(jnp.bfloat16), offsets[i]) for i in range(1, len(offsets))]
-        for item in got:
-            total = total + item.astype(jnp.float32)
-        summed = total
-    return summed
+    step = sends[0].shape[0]
+    order = (*range(1, len(mid)), 0)
+    came = {i: swapped(sends[i], 1) for i in order}
+    total = keep[:step] + came[0].astype(jnp.float32)
+    got = [swapped(added(keep, came[i], i * step), mid[i]) for i in order[:-1]]
+    for item in got:
+        total = total + item.astype(jnp.float32)
+    parts = total.reshape(len(high), -1, width)
+    total = parts[0]
+    got = [swapped(parts[i].astype(jnp.bfloat16), high[i]) for i in range(1, len(high))]
+    for item in got:
+        total = total + item.astype(jnp.float32)
+    return total
 
 
 def local(
@@ -301,6 +326,7 @@
     feature = w_out.shape[0]
     low, mid, high = stage_offsets(shards)
     info = jnp.concatenate([prefix_of_row[::CAND], context_len])
+    scales = jnp.concatenate([gate_up_scales.reshape(-1), down_scales.reshape(-1)])
 
     inputs = (queries, own_key, own_value, cache_keys, cache_values)
     message = jax.ShapeDtypeStruct((kv_rows + MID * rows + 2 * rows, 2 * HD), jnp.bfloat16)
@@ -317,12 +343,12 @@
     piece = jax.ShapeDtypeStruct((len(high), kv_rows + 2 * rows, 2 * HD), jnp.bfloat16)
     messages = pl.pallas_call(
         functools.partial(repack_body, kv_rows=kv_rows, rows=rows),
-        in_specs=[ANY] + [VMEM] * len(high),
+        in_specs=[ANY] * 2 + [VMEM] * len(high),
         out_specs=[VMEM] * MID,
         out_shape=[piece] * MID,
         compiler_params=pltpu.CompilerParams(vmem_limit_bytes=2 * SMALL_VMEM),
         name="repack",
-    )(info, *got)
+    )(info, scales, *got)
     mine = [messages[0]] + [swapped(messages[i], mid[i]) for i in range(1, MID)]
     other = [swapped(item, low[1]) for item in mine]
 
@@ -332,20 +358,20 @@
         )
     else:
         w_full = w_out
-    codes, scales = gate_up_codes[0], gate_up_scales[0]
+    codes = gate_up_codes[0]
     first = codes.shape[0] // 2
-    gate_first, w_full = prepared([(scales, codes, 0, first)], [w_full])
-    (down,) = prepared([(down_scales[0], down_codes[0], 0, down_codes.shape[1])])
-    (gate_rest,) = prepared([(scales, codes, first, codes.shape[0] - first)])
+    gate_first, w_full = prepared(scales, [(codes, 0, first, 0)], [w_full])
+    (down,) = prepared(scales, [(down_codes[0], 0, down_codes.shape[1], gate_up_scales.size)])
+    (gate_rest,) = prepared(scales, [(codes, first, codes.shape[0] - first, first // BLK * gate_up_scales.shape[2])])
     half = shards * rows // 2
     attend_vmem = 8 * 2**20 + 2 * MID * piece.size * 2 + w_full.size * 2 + half * width * 10
-    keep, send = pl.pallas_call(
+    keep, *sends = pl.pallas_call(
         functools.partial(attend_body, ctx_local=ctx_local, kv_rows=kv_rows, rows=rows),
         in_specs=[SMEM] + [VMEM] * (2 * MID + 1),
-        out_specs=[VMEM] * 2,
+        out_specs=[VMEM] * (1 + MID),
         out_shape=[
             jax.ShapeDtypeStruct((half, width), jnp.float32),
-            jax.ShapeDtypeStruct((half, width), jnp.bfloat16),
+            *[jax.ShapeDtypeStruct((half // MID, width), jnp.bfloat16)] * MID,
         ],
         scratch_shapes=[
             pltpu.VMEM((LOW * MID, len(high) * rows, HD), jnp.float32),
@@ -354,7 +380,7 @@
         name="attend",
     )(info, *mine, *other, w_full)
 
-    projected = scatter_sum(keep, send, mid, high)
+    projected = scatter_sum(keep, sends, mid, high)
     mixed = hidden_in.astype(jnp.float32) + projected
     attention_out = mixed.astype(jnp.bfloat16)
     mean_square = jnp.mean(mixed * mixed, axis=-1, keepdims=True)
@@ -372,13 +398,13 @@
     mine = [held] + [swapped(held, o) for o in mid[1:]]
     other = [swapped(item, low[1]) for item in mine]
     expert_vmem = 4 * 2**20 + 2 * half * width * 15
-    keep, send = pl.pallas_call(
+    keep, *sends = pl.pallas_call(
         functools.partial(expert_body, width=width, experts=experts_all),
         in_specs=[VMEM] * (2 * MID + 3),
-        out_specs=[VMEM] * 2,
+        out_specs=[VMEM] * (1 + MID),
         out_shape=[
             jax.ShapeDtypeStruct((half, width), jnp.float32),
-            jax.ShapeDtypeStruct((half, width), jnp.bfloat16),
+            *[jax.ShapeDtypeStruct((half // MID, width), jnp.bfloat16)] * MID,
         ],
         scratch_shapes=[
             pltpu.VMEM((2 * half, width), jnp.bfloat16),
@@ -386,7 +412,7 @@
         compiler_params=pltpu.CompilerParams(vmem_limit_bytes=expert_vmem),
         name="expert",
     )(*mine, *other, gate_first, gate_rest, down)
-    expert_sum = scatter_sum(keep, send, mid, high)
+    expert_sum = scatter_sum(keep, sends, mid, high)
     layer_out = (mixed + expert_sum).astype(jnp.bfloat16)
     return (attention_out, layer_out)
 

time: 93.6 us -> 91.2 us (0.974)
  waiting for transfers between devices: 39.4 us -> 35.6 us
  starting transfers between devices: 34.4 us -> 36.2 us
  Pallas kernels: 14.6 us -> 13.6 us
    ppermute x34 -> x40, waiting for transfers between devices: 39.4 us -> 35.6 us  [swapped(): lax.ppermute(value, 'ctx', [(i, i ^ offset) for i in range(lax.axis_size(...]
    ppermute x34 -> x40, starting transfers between devices: 34.4 us -> 36.2 us  [swapped(): lax.ppermute(value, 'ctx', [(i, i ^ offset) for i in range(lax.axis_size(...]
  transfers between devices with their start and end apart: 34 -> 40, of which waited for: 19 -> 20; matrix products, arithmetic and copies ran while one was open for 3% -> 4% of each run, Pallas kernels for 9% -> 9%
where the time goes in v3:
time: 91.2 us; the launch traced here: 90.9 us
  starting transfers between devices  36.2 us (40%)
  waiting for transfers between devices  35.6 us (39%)
  Pallas kernels  13.6 us (15%)
  other arithmetic  2.69 us (3%)
  local copies, waits for them, and re-layouts  1.9 us (2%)
    ppermute x40, starting transfers between devices, swapped(): lax.ppermute(value, 'ctx', [(i, i ^ offset) for i in range(lax.axis_size(...  36.2 us
    ppermute x40, waiting for transfers between devices, swapped(): lax.ppermute(value, 'ctx', [(i, i ^ offset) for i in range(lax.axis_size(...  35.6 us
    pallas_call x3, Pallas kernels, prepared(): pl.pallas_call(functools.partial(prepare_body, ranges=ranges, fetched=len...  8.13 us
    pallas_call x1, Pallas kernels, local(): pl.pallas_call(functools.partial(expert_body, width=width, experts=expert...  2.22 us
    pallas_call x1, Pallas kernels, local(): pl.pallas_call(functools.partial(attend_body, ctx_local=ctx_local, kv_row...  1.92 us
  transfers between devices with their start and end apart: 40, of which 20 were waited for; matrix products, arithmetic and copies ran while one was open for 4% of the time, Pallas kernels for 9%

profile of v3, /device:TPU:0, one launch (start us, length us, event | category | flops | bytes accessed | tf_op | source)
XLA Modules:
  0.0 90.9 jit_solution(9788010062052521220)
XLA Ops:
  0.6 1.1 %pack.1 = (bf16[88,256]{1,0:T(8,128)(2,1)S(1)}, bf16[88,256]{1,0:T(8,128)(2,1)S(1)}, bf16[88,256]{1,0:T(8,128)(2,1)S(1)}, bf16[88,256]{1,0:T(8,128)(2,1)S(1)}) custom-call(bf16[4,4096]{1,0:T(4,128)(2,1)} %refs_0_.1, bf16[4,256]{1,0:T(4,128)(2,1)} %refs_1_.1, bf16[4,256]{1,0:T(4,128)(2,1)} %refs_2_.2, bf16[2,32,256]{2,1,0:T(8,128)(2,1)} %refs_3_.1, ...), custom_call_target="tpu_custom_call" | custom-call | tf_op jit(solution)/shard_map/pack/pallas_call | solution.py:333
  1.7 3.1 %collective-permute-start = (bf16[88,256]{1,0:T(8,128)(2,1)S(1)}, bf16[88,256]{1,0:T(8,128)(2,1)S(1)}, u32[]{:S(2)}, u32[]{:S(2)}) collective-permute-start(bf16[88,256]{1,0:T(8,128)(2,1)S(1)} %get-tuple-element.23), channel_id=1, source_target_pairs={{0,8},{1,9},{2,10},{3,11},{4,12},{5,13},{6,14},{7,15},{8,0},{9,1},... | collective-permute-start | bytes 135176 | tf_op jit(solution)/shard_map/ppermute | solution.py:26
  4.8 2.6 %collective-permute-start.1 = (bf16[88,256]{1,0:T(8,128)(2,1)S(1)}, bf16[88,256]{1,0:T(8,128)(2,1)S(1)}, u32[]{:S(2)}, u32[]{:S(2)}) collective-permute-start(bf16[88,256]{1,0:T(8,128)(2,1)S(1)} %get-tuple-element.24), channel_id=1, source_target_pairs={{0,16},{1,17},{2,18},{3,19},{4,20},{5,21},{6,22},{7,23},{8,24},{9,... | collective-permute-start | bytes 135176 | tf_op jit(solution)/shard_map/ppermute | solution.py:26
  7.4 0.8 copy.19
  8.2 0.1 reshape.39
  8.3 0.7 reduce
  9.0 0.1 reshape.40
  9.1 0.7 slice.47
  9.9 0.7 pad_add_fusion.after.info
  10.6 2.6 %collective-permute-done.2.refs_3_ = bf16[88,256]{1,0:T(8,128)(2,1)S(1)} collective-permute-done((bf16[88,256]{1,0:T(8,128)(2,1)S(1)}, bf16[88,256]{1,0:T(8,128)(2,1)S(1)}, u32[]{:S(2)}, u32[]{:S(2)}) %collective-permute-start.2) | collective-permute-done | bytes 45088 | tf_op jit(solution)/shard_map/ppermute | solution.py:26
  13.3 1.6 %collective-permute-start.3 = (bf16[4,72,256]{2,1,0:T(8,128)(2,1)S(1)}, bf16[4,72,256]{2,1,0:T(8,128)(2,1)S(1)}, u32[]{:S(2)}, u32[]{:S(2)}) collective-permute-start(bf16[4,72,256]{2,1,0:T(8,128)(2,1)S(1)} %get-tuple-element.27), channel_id=1, source_target_pairs={{0,2},{1,3},{2,0},{3,1},{4,6},{5,7},{6,4},{7,5},{8,10},{9,11},{10,... | collective-permute-start | bytes 442376 | tf_op jit(solution)/shard_map/ppermute | solution.py:26
  14.9 1.5 %collective-permute-start.4 = (bf16[4,72,256]{2,1,0:T(8,128)(2,1)S(1)}, bf16[4,72,256]{2,1,0:T(8,128)(2,1)S(1)}, u32[]{:S(2)}, u32[]{:S(2)}) collective-permute-start(bf16[4,72,256]{2,1,0:T(8,128)(2,1)S(1)} %get-tuple-element.28), channel_id=1, source_target_pairs={{0,4},{1,5},{2,6},{3,7},{4,0},{5,1},{6,2},{7,3},{8,12},{9,13},{10,... | collective-permute-start | bytes 442376 | tf_op jit(solution)/shard_map/ppermute | solution.py:26
  16.4 0.5 collective-permute-start.5
  16.9 2.9 %collective-permute-done.3.refs_1_ = bf16[4,72,256]{2,1,0:T(8,128)(2,1)S(1)} collective-permute-done((bf16[4,72,256]{2,1,0:T(8,128)(2,1)S(1)}, bf16[4,72,256]{2,1,0:T(8,128)(2,1)S(1)}, u32[]{:S(2)}, u32[]{:S(2)}) %collective-permute-start.3) | collective-permute-done | bytes 147488 | tf_op jit(solution)/shard_map/ppermute | solution.py:26
  19.8 2.8 %collective-permute-done.4.refs_2_ = bf16[4,72,256]{2,1,0:T(8,128)(2,1)S(1)} collective-permute-done((bf16[4,72,256]{2,1,0:T(8,128)(2,1)S(1)}, bf16[4,72,256]{2,1,0:T(8,128)(2,1)S(1)}, u32[]{:S(2)}, u32[]{:S(2)}) %collective-permute-start.4) | collective-permute-done | bytes 147488 | tf_op jit(solution)/shard_map/ppermute | solution.py:26
  22.6 0.5 collective-permute-start.9
  23.1 2.8 %prepare.3 = (bf16[2048,768]{1,0:T(8,128)(2,1)S(1)}, bf16[128,4096]{1,0:T(8,128)(2,1)S(1)}) custom-call(f32[288]{0:T(512)S(1)} %pad_maximum_fusion.also.refs_0_, bf16[4096,768]{1,0:T(8,128)(2,1)} %bitcast.2, bf16[128,4096]{1,0:T(8,128)(2,1)} %refs_2_.3), custom_call_target="tpu_custom_call" | custom-call | tf_op jit(solution)/shard_map/prepare/pallas_call | solution.py:204
  25.9 1.9 %attend.1 = (f32[64,4096]{1,0:T(8,128)S(1)}, bf16[16,4096]{1,0:T(8,128)(2,1)S(1)}, bf16[16,4096]{1,0:T(8,128)(2,1)S(1)}, bf16[16,4096]{1,0:T(8,128)(2,1)S(1)}, bf16[16,4096]{1,0:T(8,128)(2,1)S(1)}) custom-call(s32[4]{0:T(128)S(1)} %pad_add_fusion.after.info, bf16[4,72,256]{2,1,0:T(8,128)(2,1)S(1)} %get-tuple-element.26.refs_0_, ...), custom_call_target="tpu_custom_call" | custom-call | tf_op jit(solution)/shard_map/attend/pallas_call | solution.py:368
  27.9 0.5 collective-permute-start.13
  28.4 0.1 collective-permute-start.15
  28.5 0.4 collective-permute-start.10
  29.0 0.3 collective-permute-done.11.got
  29.3 0.1 collective-permute-start.12
  29.5 1.2 %collective-permute-start.14 = (bf16[16,4096]{1,0:T(8,128)(2,1)S(1)}, bf16[16,4096]{1,0:T(8,128)(2,1)S(1)}, u32[]{:S(2)}, u32[]{:S(2)}) collective-permute-start(bf16[16,4096]{1,0:T(8,128)(2,1)S(1)} %add.144), channel_id=1, source_target_pairs={{0,4},{1,5},{2,6},{3,7},{4,0},{5,1},{6,2},{7,3},{8,12},{9,13},{10,... | collective-permute-start | bytes 393224 | tf_op jit(solution)/shard_map/ppermute | solution.py:26
  30.8 2.3 %collective-permute-start.16 = (bf16[16,4096]{1,0:T(8,128)(2,1)S(1)}, bf16[16,4096]{1,0:T(8,128)(2,1)S(1)}, u32[]{:S(2)}, u32[]{:S(2)}) collective-permute-start(bf16[16,4096]{1,0:T(8,128)(2,1)S(1)} %add.145), channel_id=1, source_target_pairs={{0,6},{1,7},{2,4},{3,5},{4,2},{5,3},{6,0},{7,1},{8,14},{9,15},{10,... | collective-permute-start | bytes 393224 | tf_op jit(solution)/shard_map/ppermute | solution.py:26
  33.1 0.1 select_reduce_fusion
  33.2 2.6 %collective-permute-done.12 = bf16[16,4096]{1,0:T(8,128)(2,1)S(1)} collective-permute-done((bf16[16,4096]{1,0:T(8,128)(2,1)S(1)}, bf16[16,4096]{1,0:T(8,128)(2,1)S(1)}, u32[]{:S(2)}, u32[]{:S(2)}) %collective-permute-start.12) | collective-permute-done | bytes 131104 | tf_op jit(solution)/shard_map/ppermute | solution.py:26
  35.8 0.3 collective-permute-done.14
  36.0 2.2 %collective-permute-done.16 = bf16[16,4096]{1,0:T(8,128)(2,1)S(1)} collective-permute-done((bf16[16,4096]{1,0:T(8,128)(2,1)S(1)}, bf16[16,4096]{1,0:T(8,128)(2,1)S(1)}, u32[]{:S(2)}, u32[]{:S(2)}) %collective-permute-start.16) | collective-permute-done | bytes 131104 | tf_op jit(solution)/shard_map/ppermute | solution.py:26
  38.4 2.3 %collective-permute-start.18 = (bf16[4,4096]{1,0:T(4,128)(2,1)S(1)}, bf16[4,4096]{1,0:T(4,128)(2,1)S(1)}, u32[]{:S(2)}, u32[]{:S(2)}) collective-permute-start(bf16[4,4096]{1,0:T(4,128)(2,1)S(1)} %get-tuple-element.53), channel_id=1, source_target_pairs={{0,16},{1,17},{2,18},{3,19},{4,20},{5,21},{6,22},{7,23},{8,24},{9,... | collective-permute-start | bytes 98312 | tf_op jit(solution)/shard_map/ppermute | solution.py:26
  40.7 2.1 %collective-permute-start.19 = (bf16[4,4096]{1,0:T(4,128)(2,1)S(1)}, bf16[4,4096]{1,0:T(4,128)(2,1)S(1)}, u32[]{:S(2)}, u32[]{:S(2)}) collective-permute-start(bf16[4,4096]{1,0:T(4,128)(2,1)S(1)} %get-tuple-element.52), channel_id=1, source_target_pairs={{0,24},{1,25},{2,26},{3,27},{4,28},{5,29},{6,30},{7,31},{8,16},{9,... | collective-permute-start | bytes 98312 | tf_op jit(solution)/shard_map/ppermute | solution.py:26
  42.8 0.5 collective-permute-done.18
  43.3 3.2 %collective-permute-done.19 = bf16[4,4096]{1,0:T(4,128)(2,1)S(1)} collective-permute-done((bf16[4,4096]{1,0:T(4,128)(2,1)S(1)}, bf16[4,4096]{1,0:T(4,128)(2,1)S(1)}, u32[]{:S(2)}, u32[]{:S(2)}) %collective-permute-start.19) | collective-permute-done | bytes 32800 | tf_op jit(solution)/shard_map/ppermute | solution.py:26
  46.4 0.2 multiply_reduce_fusion
  46.6 0.1 multiply_convert_fusion
  46.7 0.1 concatenate.14.refs_0_
  46.9 2.6 %collective-permute-start.21 = (bf16[4,4224]{1,0:T(4,128)(2,1)S(1)}, bf16[4,4224]{1,0:T(4,128)(2,1)S(1)}, u32[]{:S(2)}, u32[]{:S(2)}) collective-permute-start(bf16[4,4224]{1,0:T(4,128)(2,1)S(1)} %concatenate.14.refs_0_), channel_id=1, source_target_pairs={{0,16},{1,17},{2,18},{3,19},{4,20},{5,21},{6,22},{7,23},{8,24},{9,... | collective-permute-start | bytes 101384 | tf_op jit(solution)/shard_map/ppermute | solution.py:26
  49.5 1.8 %collective-permute-start.22 = (bf16[4,4224]{1,0:T(4,128)(2,1)S(1)}, bf16[4,4224]{1,0:T(4,128)(2,1)S(1)}, u32[]{:S(2)}, u32[]{:S(2)}) collective-permute-start(bf16[4,4224]{1,0:T(4,128)(2,1)S(1)} %concatenate.14.refs_0_), channel_id=1, source_target_pairs={{0,24},{1,25},{2,26},{3,27},{4,28},{5,29},{6,30},{7,31},{8,16},{9,... | collective-permute-start | bytes 101384 | tf_op jit(solution)/shard_map/ppermute | solution.py:26
  51.2 0.6 collective-permute-done.21.refs_2_
  51.9 3.3 %collective-permute-done.22.refs_3_ = bf16[4,4224]{1,0:T(4,128)(2,1)S(1)} collective-permute-done((bf16[4,4224]{1,0:T(4,128)(2,1)S(1)}, bf16[4,4224]{1,0:T(4,128)(2,1)S(1)}, u32[]{:S(2)}, u32[]{:S(2)}) %collective-permute-start.22) | collective-permute-done | bytes 33824 | tf_op jit(solution)/shard_map/ppermute | solution.py:26
  55.2 1.5 %collective-permute-start.23 = (bf16[16,4224]{1,0:T(8,128)(2,1)S(1)}, bf16[16,4224]{1,0:T(8,128)(2,1)S(1)}, u32[]{:S(2)}, u32[]{:S(2)}) collective-permute-start(bf16[16,4224]{1,0:T(8,128)(2,1)S(1)} %join.1.refs_0_), channel_id=1, source_target_pairs={{0,2},{1,3},{2,0},{3,1},{4,6},{5,7},{6,4},{7,5},{8,10},{9,11},{10,... | collective-permute-start | bytes 405512 | tf_op jit(solution)/shard_map/ppermute | solution.py:26
  56.7 1.1 %collective-permute-start.24 = (bf16[16,4224]{1,0:T(8,128)(2,1)S(1)}, bf16[16,4224]{1,0:T(8,128)(2,1)S(1)}, u32[]{:S(2)}, u32[]{:S(2)}) collective-permute-start(bf16[16,4224]{1,0:T(8,128)(2,1)S(1)} %join.1.refs_0_), channel_id=1, source_target_pairs={{0,4},{1,5},{2,6},{3,7},{4,0},{5,1},{6,2},{7,3},{8,12},{9,13},{10,... | collective-permute-start | bytes 405512 | tf_op jit(solution)/shard_map/ppermute | solution.py:26
  57.8 1.0 %collective-permute-start.25 = (bf16[16,4224]{1,0:T(8,128)(2,1)S(1)}, bf16[16,4224]{1,0:T(8,128)(2,1)S(1)}, u32[]{:S(2)}, u32[]{:S(2)}) collective-permute-start(bf16[16,4224]{1,0:T(8,128)(2,1)S(1)} %join.1.refs_0_), channel_id=1, source_target_pairs={{0,6},{1,7},{2,4},{3,5},{4,2},{5,3},{6,0},{7,1},{8,14},{9,15},{10,... | collective-permute-start | bytes 405512 | tf_op jit(solution)/shard_map/ppermute | solution.py:26
  58.8 1.5 %collective-permute-done.23.refs_1_ = bf16[16,4224]{1,0:T(8,128)(2,1)S(1)} collective-permute-done((bf16[16,4224]{1,0:T(8,128)(2,1)S(1)}, bf16[16,4224]{1,0:T(8,128)(2,1)S(1)}, u32[]{:S(2)}, u32[]{:S(2)}) %collective-permute-start.23) | collective-permute-done | bytes 135200 | tf_op jit(solution)/shard_map/ppermute | solution.py:26
  60.3 1.4 %collective-permute-done.24.refs_2_ = bf16[16,4224]{1,0:T(8,128)(2,1)S(1)} collective-permute-done((bf16[16,4224]{1,0:T(8,128)(2,1)S(1)}, bf16[16,4224]{1,0:T(8,128)(2,1)S(1)}, u32[]{:S(2)}, u32[]{:S(2)}) %collective-permute-start.24) | collective-permute-done | bytes 135200 | tf_op jit(solution)/shard_map/ppermute | solution.py:26
  61.7 2.0 %collective-permute-done.25.refs_3_ = bf16[16,4224]{1,0:T(8,128)(2,1)S(1)} collective-permute-done((bf16[16,4224]{1,0:T(8,128)(2,1)S(1)}, bf16[16,4224]{1,0:T(8,128)(2,1)S(1)}, u32[]{:S(2)}, u32[]{:S(2)}) %collective-permute-start.25) | collective-permute-done | bytes 135200 | tf_op jit(solution)/shard_map/ppermute | solution.py:26
  63.7 2.6 %prepare.4.refs_9_ = bf16[2048,768]{1,0:T(8,128)(2,1)S(1)} custom-call(f32[288]{0:T(512)S(1)} %pad_maximum_fusion.also.refs_0_, bf16[4096,768]{1,0:T(8,128)(2,1)} %bitcast.3), custom_call_target="tpu_custom_call" | custom-call | tf_op jit(solution)/shard_map/prepare/pallas_call | solution.py:204
  66.3 2.8 %prepare.5.refs_10_ = bf16[384,4096]{1,0:T(8,128)(2,1)S(1)} custom-call(f32[288]{0:T(512)S(1)} %pad_maximum_fusion.also.refs_0_, bf16[384,4096]{1,0:T(8,128)(2,1)} %bitcast.4), custom_call_target="tpu_custom_call" | custom-call | tf_op jit(solution)/shard_map/prepare/pallas_call | solution.py:204
  69.1 2.2 %expert.1 = (f32[64,4096]{1,0:T(8,128)S(1)}, bf16[16,4096]{1,0:T(8,128)(2,1)S(1)}, bf16[16,4096]{1,0:T(8,128)(2,1)S(1)}, bf16[16,4096]{1,0:T(8,128)(2,1)S(1)}, bf16[16,4096]{1,0:T(8,128)(2,1)S(1)}) custom-call(bf16[16,4224]{1,0:T(8,128)(2,1)S(1)} %join.1.refs_0_, bf16[16,4224]{1,0:T(8,128)(2,1)S(1)} %collective-permute-done.23.refs_1_, ...), custom_call_target="tpu_custom_call" | custom-call | tf_op jit(solution)/shard_map/expert/pallas_call | solution.py:401
  71.3 0.6 collective-permute-start.31
  72.0 0.4 collective-permute-start.35
  72.5 0.4 collective-permute-done.31.got
  72.9 0.6 collective-permute-start.32
  73.6 1.1 %collective-permute-start.34 = (bf16[16,4096]{1,0:T(8,128)(2,1)S(1)}, bf16[16,4096]{1,0:T(8,128)(2,1)S(1)}, u32[]{:S(2)}, u32[]{:S(2)}) collective-permute-start(bf16[16,4096]{1,0:T(8,128)(2,1)S(1)} %add.147), channel_id=1, source_target_pairs={{0,4},{1,5},{2,6},{3,7},{4,0},{5,1},{6,2},{7,3},{8,12},{9,13},{10,... | collective-permute-start | bytes 393224 | tf_op jit(solution)/shard_map/ppermute | solution.py:26
  74.7 2.0 %collective-permute-start.36 = (bf16[16,4096]{1,0:T(8,128)(2,1)S(1)}, bf16[16,4096]{1,0:T(8,128)(2,1)S(1)}, u32[]{:S(2)}, u32[]{:S(2)}) collective-permute-start(bf16[16,4096]{1,0:T(8,128)(2,1)S(1)} %add.148), channel_id=1, source_target_pairs={{0,6},{1,7},{2,4},{3,5},{4,2},{5,3},{6,0},{7,1},{8,14},{9,15},{10,... | collective-permute-start | bytes 393224 | tf_op jit(solution)/shard_map/ppermute | solution.py:26
  76.7 2.7 %collective-permute-done.32 = bf16[16,4096]{1,0:T(8,128)(2,1)S(1)} collective-permute-done((bf16[16,4096]{1,0:T(8,128)(2,1)S(1)}, bf16[16,4096]{1,0:T(8,128)(2,1)S(1)}, u32[]{:S(2)}, u32[]{:S(2)}) %collective-permute-start.32) | collective-permute-done | bytes 131104 | tf_op jit(solution)/shard_map/ppermute | solution.py:26
  79.3 0.4 collective-permute-done.34
  79.7 2.2 %collective-permute-done.36 = bf16[16,4096]{1,0:T(8,128)(2,1)S(1)} collective-permute-done((bf16[16,4096]{1,0:T(8,128)(2,1)S(1)}, bf16[16,4096]{1,0:T(8,128)(2,1)S(1)}, u32[]{:S(2)}, u32[]{:S(2)}) %collective-permute-start.36) | collective-permute-done | bytes 131104 | tf_op jit(solution)/shard_map/ppermute | solution.py:26
  81.9 0.1 fusion.8
  82.2 2.4 %collective-permute-start.38 = (bf16[4,4096]{1,0:T(4,128)(2,1)S(1)}, bf16[4,4096]{1,0:T(4,128)(2,1)S(1)}, u32[]{:S(2)}, u32[]{:S(2)}) collective-permute-start(bf16[4,4096]{1,0:T(4,128)(2,1)S(1)} %get-tuple-element.50), channel_id=1, source_target_pairs={{0,16},{1,17},{2,18},{3,19},{4,20},{5,21},{6,22},{7,23},{8,24},{9,... | collective-permute-start | bytes 98312 | tf_op jit(solution)/shard_map/ppermute | solution.py:26
  84.5 2.0 %collective-permute-start.39 = (bf16[4,4096]{1,0:T(4,128)(2,1)S(1)}, bf16[4,4096]{1,0:T(4,128)(2,1)S(1)}, u32[]{:S(2)}, u32[]{:S(2)}) collective-permute-start(bf16[4,4096]{1,0:T(4,128)(2,1)S(1)} %get-tuple-element.49), channel_id=1, source_target_pairs={{0,24},{1,25},{2,26},{3,27},{4,28},{5,29},{6,30},{7,31},{8,16},{9,... | collective-permute-start | bytes 98312 | tf_op jit(solution)/shard_map/ppermute | solution.py:26
  86.5 0.5 collective-permute-done.38
  87.0 3.2 %collective-permute-done.39 = bf16[4,4096]{1,0:T(4,128)(2,1)S(1)} collective-permute-done((bf16[4,4096]{1,0:T(4,128)(2,1)S(1)}, bf16[4,4096]{1,0:T(4,128)(2,1)S(1)}, u32[]{:S(2)}, u32[]{:S(2)}) %collective-permute-start.39) | collective-permute-done | bytes 32800 | tf_op jit(solution)/shard_map/ppermute | solution.py:26
  90.3 0.7 fusion.3
  (57 shorter events, 1.0 us)
Async XLA Ops:
  1.7 8.9 %collective-permute-start = (bf16[88,256]{1,0:T(8,128)(2,1)S(1)}, bf16[88,256]{1,0:T(8,128)(2,1)S(1)}, u32[]{:S(2)}, u32[]{:S(2)}) collective-permute-start(bf16[88,256]{1,0:T(8,128)(2,1)S(1)} %get-tuple-element.23), channel_id=1, source_target_pairs={{0,8},{1,9},{2,10},{3,11},{4,12},{5,13},{6,14},{7,15},{8,0},{9,1},... | collective-permute-start | bytes 135176 | tf_op jit(solution)/shard_map/ppermute | solution.py:26
  4.8 5.8 %collective-permute-start.1 = (bf16[88,256]{1,0:T(8,128)(2,1)S(1)}, bf16[88,256]{1,0:T(8,128)(2,1)S(1)}, u32[]{:S(2)}, u32[]{:S(2)}) collective-permute-start(bf16[88,256]{1,0:T(8,128)(2,1)S(1)} %get-tuple-element.24), channel_id=1, source_target_pairs={{0,16},{1,17},{2,18},{3,19},{4,20},{5,21},{6,22},{7,23},{8,24},{9,... | collective-permute-start | bytes 135176 | tf_op jit(solution)/shard_map/ppermute | solution.py:26
  7.4 5.8 %collective-permute-start.2 = (bf16[88,256]{1,0:T(8,128)(2,1)S(1)}, bf16[88,256]{1,0:T(8,128)(2,1)S(1)}, u32[]{:S(2)}, u32[]{:S(2)}) collective-permute-start(bf16[88,256]{1,0:T(8,128)(2,1)S(1)} %get-tuple-element.25), channel_id=1, source_target_pairs={{0,24},{1,25},{2,26},{3,27},{4,28},{5,29},{6,30},{7,31},{8,16},{9,... | collective-permute-start | bytes 135176 | tf_op jit(solution)/shard_map/ppermute | solution.py:26
  13.3 6.4 %collective-permute-start.3 = (bf16[4,72,256]{2,1,0:T(8,128)(2,1)S(1)}, bf16[4,72,256]{2,1,0:T(8,128)(2,1)S(1)}, u32[]{:S(2)}, u32[]{:S(2)}) collective-permute-start(bf16[4,72,256]{2,1,0:T(8,128)(2,1)S(1)} %get-tuple-element.27), channel_id=1, source_target_pairs={{0,2},{1,3},{2,0},{3,1},{4,6},{5,7},{6,4},{7,5},{8,10},{9,11},{10,... | collective-permute-start | bytes 442376 | tf_op jit(solution)/shard_map/ppermute | solution.py:26
  14.9 7.7 %collective-permute-start.4 = (bf16[4,72,256]{2,1,0:T(8,128)(2,1)S(1)}, bf16[4,72,256]{2,1,0:T(8,128)(2,1)S(1)}, u32[]{:S(2)}, u32[]{:S(2)}) collective-permute-start(bf16[4,72,256]{2,1,0:T(8,128)(2,1)S(1)} %get-tuple-element.28), channel_id=1, source_target_pairs={{0,4},{1,5},{2,6},{3,7},{4,0},{5,1},{6,2},{7,3},{8,12},{9,13},{10,... | collective-permute-start | bytes 442376 | tf_op jit(solution)/shard_map/ppermute | solution.py:26
  16.4 6.2 %collective-permute-start.5 = (bf16[4,72,256]{2,1,0:T(8,128)(2,1)S(1)}, bf16[4,72,256]{2,1,0:T(8,128)(2,1)S(1)}, u32[]{:S(2)}, u32[]{:S(2)}) collective-permute-start(bf16[4,72,256]{2,1,0:T(8,128)(2,1)S(1)} %get-tuple-element.29), channel_id=1, source_target_pairs={{0,6},{1,7},{2,4},{3,5},{4,2},{5,3},{6,0},{7,1},{8,14},{9,15},{10,... | collective-permute-start | bytes 442376 | tf_op jit(solution)/shard_map/ppermute | solution.py:26
  16.9 9.0 %collective-permute-start.6 = (bf16[4,72,256]{2,1,0:T(8,128)(2,1)S(1)}, bf16[4,72,256]{2,1,0:T(8,128)(2,1)S(1)}, u32[]{:S(2)}, u32[]{:S(2)}) collective-permute-start(bf16[4,72,256]{2,1,0:T(8,128)(2,1)S(1)} %get-tuple-element.26.refs_0_), channel_id=1, source_target_pairs={{0,1},{1,0},{2,3},{3,2},{4,5},{5,4},{6,7},{7,6},{8,9},{9,8},{10,11... | collective-permute-start | bytes 442376 | tf_op jit(solution)/shard_map/ppermute | solution.py:26
  19.7 6.1 %collective-permute-start.7 = (bf16[4,72,256]{2,1,0:T(8,128)(2,1)S(1)}, bf16[4,72,256]{2,1,0:T(8,128)(2,1)S(1)}, u32[]{:S(2)}, u32[]{:S(2)}) collective-permute-start(bf16[4,72,256]{2,1,0:T(8,128)(2,1)S(1)} %collective-permute-done.3.refs_1_), channel_id=1, source_target_pairs={{0,1},{1,0},{2,3},{3,2},{4,5},{5,4},{6,7},{7,6},{8,9},{9,8},{10,11... | collective-permute-start | bytes 442376 | tf_op jit(solution)/shard_map/ppermute | solution.py:26
  22.6 3.3 %collective-permute-start.8 = (bf16[4,72,256]{2,1,0:T(8,128)(2,1)S(1)}, bf16[4,72,256]{2,1,0:T(8,128)(2,1)S(1)}, u32[]{:S(2)}, u32[]{:S(2)}) collective-permute-start(bf16[4,72,256]{2,1,0:T(8,128)(2,1)S(1)} %collective-permute-done.4.refs_2_), channel_id=1, source_target_pairs={{0,1},{1,0},{2,3},{3,2},{4,5},{5,4},{6,7},{7,6},{8,9},{9,8},{10,11... | collective-permute-start | bytes 442376 | tf_op jit(solution)/shard_map/ppermute | solution.py:26
  22.6 3.3 %collective-permute-start.9 = (bf16[4,72,256]{2,1,0:T(8,128)(2,1)S(1)}, bf16[4,72,256]{2,1,0:T(8,128)(2,1)S(1)}, u32[]{:S(2)}, u32[]{:S(2)}) collective-permute-start(bf16[4,72,256]{2,1,0:T(8,128)(2,1)S(1)} %collective-permute-done.5.refs_3_), channel_id=1, source_target_pairs={{0,1},{1,0},{2,3},{3,2},{4,5},{5,4},{6,7},{7,6},{8,9},{9,8},{10,11... | collective-permute-start | bytes 442376 | tf_op jit(solution)/shard_map/ppermute | solution.py:26
  25.9 7.2 %copy-start.2 = (f32[4,8]{1,0:T(4,128)S(1)}, f32[4,8]{1,0:T(4,128)}, u32[]{:S(2)}) copy-start(f32[4,8]{1,0:T(4,128)} %param.27) | copy-start | bytes 388
  25.9 7.2 %copy-start.3 = (s32[4,8]{1,0:T(4,128)S(1)}, s32[4,8]{1,0:T(4,128)}, u32[]{:S(2)}) copy-start(s32[4,8]{1,0:T(4,128)} %param.26) | copy-start | bytes 388
  27.8 18.6 %copy-start = (bf16[4,4096]{1,0:T(4,128)(2,1)S(1)}, bf16[4,4096]{1,0:T(4,128)(2,1)}, u32[]{:S(2)}) copy-start(bf16[4,4096]{1,0:T(4,128)(2,1)} %param.23) | copy-start | bytes 98308
  27.9 18.8 %copy-start.1 = (f32[4096]{0:T(1024)S(1)}, f32[4096]{0:T(1024)}, u32[]{:S(2)}) copy-start(f32[4096]{0:T(1024)} %param.25) | copy-start | bytes 49156
  27.9 1.4 %collective-permute-start.11 = (bf16[16,4096]{1,0:T(8,128)(2,1)S(1)}, bf16[16,4096]{1,0:T(8,128)(2,1)S(1)}, u32[]{:S(2)}, u32[]{:S(2)}) collective-permute-start(bf16[16,4096]{1,0:T(8,128)(2,1)S(1)} %get-tuple-element.33), channel_id=1, source_target_pairs={{0,1},{1,0},{2,3},{3,2},{4,5},{5,4},{6,7},{7,6},{8,9},{9,8},{10,11... | collective-permute-start | bytes 393224 | tf_op jit(solution)/shard_map/ppermute | solution.py:26
  27.9 1.5 %collective-permute-start.13 = (bf16[16,4096]{1,0:T(8,128)(2,1)S(1)}, bf16[16,4096]{1,0:T(8,128)(2,1)S(1)}, u32[]{:S(2)}, u32[]{:S(2)}) collective-permute-start(bf16[16,4096]{1,0:T(8,128)(2,1)S(1)} %get-tuple-element.34), channel_id=1, source_target_pairs={{0,1},{1,0},{2,3},{3,2},{4,5},{5,4},{6,7},{7,6},{8,9},{9,8},{10,11... | collective-permute-start | bytes 393224 | tf_op jit(solution)/shard_map/ppermute | solution.py:26
  28.4 2.3 %collective-permute-start.15 = (bf16[16,4096]{1,0:T(8,128)(2,1)S(1)}, bf16[16,4096]{1,0:T(8,128)(2,1)S(1)}, u32[]{:S(2)}, u32[]{:S(2)}) collective-permute-start(bf16[16,4096]{1,0:T(8,128)(2,1)S(1)} %get-tuple-element.35), channel_id=1, source_target_pairs={{0,1},{1,0},{2,3},{3,2},{4,5},{5,4},{6,7},{7,6},{8,9},{9,8},{10,11... | collective-permute-start | bytes 393224 | tf_op jit(solution)/shard_map/ppermute | solution.py:26
  28.5 4.7 %collective-permute-start.10 = (bf16[16,4096]{1,0:T(8,128)(2,1)S(1)}, bf16[16,4096]{1,0:T(8,128)(2,1)S(1)}, u32[]{:S(2)}, u32[]{:S(2)}) collective-permute-start(bf16[16,4096]{1,0:T(8,128)(2,1)S(1)} %get-tuple-element.32), channel_id=1, source_target_pairs={{0,1},{1,0},{2,3},{3,2},{4,5},{5,4},{6,7},{7,6},{8,9},{9,8},{10,11... | collective-permute-start | bytes 393224 | tf_op jit(solution)/shard_map/ppermute | solution.py:26
  29.3 6.4 %collective-permute-start.12 = (bf16[16,4096]{1,0:T(8,128)(2,1)S(1)}, bf16[16,4096]{1,0:T(8,128)(2,1)S(1)}, u32[]{:S(2)}, u32[]{:S(2)}) collective-permute-start(bf16[16,4096]{1,0:T(8,128)(2,1)S(1)} %add.143), channel_id=1, source_target_pairs={{0,2},{1,3},{2,0},{3,1},{4,6},{5,7},{6,4},{7,5},{8,10},{9,11},{10,... | collective-permute-start | bytes 393224 | tf_op jit(solution)/shard_map/ppermute | solution.py:26
  29.5 6.5 %collective-permute-start.14 = (bf16[16,4096]{1,0:T(8,128)(2,1)S(1)}, bf16[16,4096]{1,0:T(8,128)(2,1)S(1)}, u32[]{:S(2)}, u32[]{:S(2)}) collective-permute-start(bf16[16,4096]{1,0:T(8,128)(2,1)S(1)} %add.144), channel_id=1, source_target_pairs={{0,4},{1,5},{2,6},{3,7},{4,0},{5,1},{6,2},{7,3},{8,12},{9,13},{10,... | collective-permute-start | bytes 393224 | tf_op jit(solution)/shard_map/ppermute | solution.py:26
  30.8 7.4 %collective-permute-start.16 = (bf16[16,4096]{1,0:T(8,128)(2,1)S(1)}, bf16[16,4096]{1,0:T(8,128)(2,1)S(1)}, u32[]{:S(2)}, u32[]{:S(2)}) collective-permute-start(bf16[16,4096]{1,0:T(8,128)(2,1)S(1)} %add.145), channel_id=1, source_target_pairs={{0,6},{1,7},{2,4},{3,5},{4,2},{5,3},{6,0},{7,1},{8,14},{9,15},{10,... | collective-permute-start | bytes 393224 | tf_op jit(solution)/shard_map/ppermute | solution.py:26
  38.3 4.5 %collective-permute-start.17 = (bf16[4,4096]{1,0:T(4,128)(2,1)S(1)}, bf16[4,4096]{1,0:T(4,128)(2,1)S(1)}, u32[]{:S(2)}, u32[]{:S(2)}) collective-permute-start(bf16[4,4096]{1,0:T(4,128)(2,1)S(1)} %get-tuple-element.51), channel_id=1, source_target_pairs={{0,8},{1,9},{2,10},{3,11},{4,12},{5,13},{6,14},{7,15},{8,0},{9,1},... | collective-permute-start | bytes 98312 | tf_op jit(solution)/shard_map/ppermute | solution.py:26
  38.4 4.9 %collective-permute-start.18 = (bf16[4,4096]{1,0:T(4,128)(2,1)S(1)}, bf16[4,4096]{1,0:T(4,128)(2,1)S(1)}, u32[]{:S(2)}, u32[]{:S(2)}) collective-permute-start(bf16[4,4096]{1,0:T(4,128)(2,1)S(1)} %get-tuple-element.53), channel_id=1, source_target_pairs={{0,16},{1,17},{2,18},{3,19},{4,20},{5,21},{6,22},{7,23},{8,24},{9,... | collective-permute-start | bytes 98312 | tf_op jit(solution)/shard_map/ppermute | solution.py:26
  40.7 5.7 %collective-permute-start.19 = (bf16[4,4096]{1,0:T(4,128)(2,1)S(1)}, bf16[4,4096]{1,0:T(4,128)(2,1)S(1)}, u32[]{:S(2)}, u32[]{:S(2)}) collective-permute-start(bf16[4,4096]{1,0:T(4,128)(2,1)S(1)} %get-tuple-element.52), channel_id=1, source_target_pairs={{0,24},{1,25},{2,26},{3,27},{4,28},{5,29},{6,30},{7,31},{8,16},{9,... | collective-permute-start | bytes 98312 | tf_op jit(solution)/shard_map/ppermute | solution.py:26
  46.8 4.4 %collective-permute-start.20 = (bf16[4,4224]{1,0:T(4,128)(2,1)S(1)}, bf16[4,4224]{1,0:T(4,128)(2,1)S(1)}, u32[]{:S(2)}, u32[]{:S(2)}) collective-permute-start(bf16[4,4224]{1,0:T(4,128)(2,1)S(1)} %concatenate.14.refs_0_), channel_id=1, source_target_pairs={{0,8},{1,9},{2,10},{3,11},{4,12},{5,13},{6,14},{7,15},{8,0},{9,1},... | collective-permute-start | bytes 101384 | tf_op jit(solution)/shard_map/ppermute | solution.py:26
  46.9 5.0 %collective-permute-start.21 = (bf16[4,4224]{1,0:T(4,128)(2,1)S(1)}, bf16[4,4224]{1,0:T(4,128)(2,1)S(1)}, u32[]{:S(2)}, u32[]{:S(2)}) collective-permute-start(bf16[4,4224]{1,0:T(4,128)(2,1)S(1)} %concatenate.14.refs_0_), channel_id=1, source_target_pairs={{0,16},{1,17},{2,18},{3,19},{4,20},{5,21},{6,22},{7,23},{8,24},{9,... | collective-permute-start | bytes 101384 | tf_op jit(solution)/shard_map/ppermute | solution.py:26
  49.5 5.7 %collective-permute-start.22 = (bf16[4,4224]{1,0:T(4,128)(2,1)S(1)}, bf16[4,4224]{1,0:T(4,128)(2,1)S(1)}, u32[]{:S(2)}, u32[]{:S(2)}) collective-permute-start(bf16[4,4224]{1,0:T(4,128)(2,1)S(1)} %concatenate.14.refs_0_), channel_id=1, source_target_pairs={{0,24},{1,25},{2,26},{3,27},{4,28},{5,29},{6,30},{7,31},{8,16},{9,... | collective-permute-start | bytes 101384 | tf_op jit(solution)/shard_map/ppermute | solution.py:26
  55.2 5.1 %collective-permute-start.23 = (bf16[16,4224]{1,0:T(8,128)(2,1)S(1)}, bf16[16,4224]{1,0:T(8,128)(2,1)S(1)}, u32[]{:S(2)}, u32[]{:S(2)}) collective-permute-start(bf16[16,4224]{1,0:T(8,128)(2,1)S(1)} %join.1.refs_0_), channel_id=1, source_target_pairs={{0,2},{1,3},{2,0},{3,1},{4,6},{5,7},{6,4},{7,5},{8,10},{9,11},{10,... | collective-permute-start | bytes 405512 | tf_op jit(solution)/shard_map/ppermute | solution.py:26
  56.7 5.0 %collective-permute-start.24 = (bf16[16,4224]{1,0:T(8,128)(2,1)S(1)}, bf16[16,4224]{1,0:T(8,128)(2,1)S(1)}, u32[]{:S(2)}, u32[]{:S(2)}) collective-permute-start(bf16[16,4224]{1,0:T(8,128)(2,1)S(1)} %join.1.refs_0_), channel_id=1, source_target_pairs={{0,4},{1,5},{2,6},{3,7},{4,0},{5,1},{6,2},{7,3},{8,12},{9,13},{10,... | collective-permute-start | bytes 405512 | tf_op jit(solution)/shard_map/ppermute | solution.py:26
  57.8 5.9 %collective-permute-start.25 = (bf16[16,4224]{1,0:T(8,128)(2,1)S(1)}, bf16[16,4224]{1,0:T(8,128)(2,1)S(1)}, u32[]{:S(2)}, u32[]{:S(2)}) collective-permute-start(bf16[16,4224]{1,0:T(8,128)(2,1)S(1)} %join.1.refs_0_), channel_id=1, source_target_pairs={{0,6},{1,7},{2,4},{3,5},{4,2},{5,3},{6,0},{7,1},{8,14},{9,15},{10,... | collective-permute-start | bytes 405512 | tf_op jit(solution)/shard_map/ppermute | solution.py:26
  58.8 10.3 %collective-permute-start.26 = (bf16[16,4224]{1,0:T(8,128)(2,1)S(1)}, bf16[16,4224]{1,0:T(8,128)(2,1)S(1)}, u32[]{:S(2)}, u32[]{:S(2)}) collective-permute-start(bf16[16,4224]{1,0:T(8,128)(2,1)S(1)} %join.1.refs_0_), channel_id=1, source_target_pairs={{0,1},{1,0},{2,3},{3,2},{4,5},{5,4},{6,7},{7,6},{8,9},{9,8},{10,11... | collective-permute-start | bytes 405512 | tf_op jit(solution)/shard_map/ppermute | solution.py:26
  60.3 8.8 %collective-permute-start.27 = (bf16[16,4224]{1,0:T(8,128)(2,1)S(1)}, bf16[16,4224]{1,0:T(8,128)(2,1)S(1)}, u32[]{:S(2)}, u32[]{:S(2)}) collective-permute-start(bf16[16,4224]{1,0:T(8,128)(2,1)S(1)} %collective-permute-done.23.refs_1_), channel_id=1, source_target_pairs={{0,1},{1,0},{2,3},{3,2},{4,5},{5,4},{6,7},{7,6},{8,9},{9,8},{10,11... | collective-permute-start | bytes 405512 | tf_op jit(solution)/shard_map/ppermute | solution.py:26
  61.7 7.4 %collective-permute-start.28 = (bf16[16,4224]{1,0:T(8,128)(2,1)S(1)}, bf16[16,4224]{1,0:T(8,128)(2,1)S(1)}, u32[]{:S(2)}, u32[]{:S(2)}) collective-permute-start(bf16[16,4224]{1,0:T(8,128)(2,1)S(1)} %collective-permute-done.24.refs_2_), channel_id=1, source_target_pairs={{0,1},{1,0},{2,3},{3,2},{4,5},{5,4},{6,7},{7,6},{8,9},{9,8},{10,11... | collective-permute-start | bytes 405512 | tf_op jit(solution)/shard_map/ppermute | solution.py:26
  63.7 5.4 %collective-permute-start.29 = (bf16[16,4224]{1,0:T(8,128)(2,1)S(1)}, bf16[16,4224]{1,0:T(8,128)(2,1)S(1)}, u32[]{:S(2)}, u32[]{:S(2)}) collective-permute-start(bf16[16,4224]{1,0:T(8,128)(2,1)S(1)} %collective-permute-done.25.refs_3_), channel_id=1, source_target_pairs={{0,1},{1,0},{2,3},{3,2},{4,5},{5,4},{6,7},{7,6},{8,9},{9,8},{10,11... | collective-permute-start | bytes 405512 | tf_op jit(solution)/shard_map/ppermute | solution.py:26
  71.3 1.6 %collective-permute-start.31 = (bf16[16,4096]{1,0:T(8,128)(2,1)S(1)}, bf16[16,4096]{1,0:T(8,128)(2,1)S(1)}, u32[]{:S(2)}, u32[]{:S(2)}) collective-permute-start(bf16[16,4096]{1,0:T(8,128)(2,1)S(1)} %get-tuple-element.39), channel_id=1, source_target_pairs={{0,1},{1,0},{2,3},{3,2},{4,5},{5,4},{6,7},{7,6},{8,9},{9,8},{10,11... | collective-permute-start | bytes 393224 | tf_op jit(solution)/shard_map/ppermute | solution.py:26
  71.9 1.6 %collective-permute-start.33 = (bf16[16,4096]{1,0:T(8,128)(2,1)S(1)}, bf16[16,4096]{1,0:T(8,128)(2,1)S(1)}, u32[]{:S(2)}, u32[]{:S(2)}) collective-permute-start(bf16[16,4096]{1,0:T(8,128)(2,1)S(1)} %get-tuple-element.40), channel_id=1, source_target_pairs={{0,1},{1,0},{2,3},{3,2},{4,5},{5,4},{6,7},{7,6},{8,9},{9,8},{10,11... | collective-permute-start | bytes 393224 | tf_op jit(solution)/shard_map/ppermute | solution.py:26
  72.0 2.7 %collective-permute-start.35 = (bf16[16,4096]{1,0:T(8,128)(2,1)S(1)}, bf16[16,4096]{1,0:T(8,128)(2,1)S(1)}, u32[]{:S(2)}, u32[]{:S(2)}) collective-permute-start(bf16[16,4096]{1,0:T(8,128)(2,1)S(1)} %get-tuple-element.41), channel_id=1, source_target_pairs={{0,1},{1,0},{2,3},{3,2},{4,5},{5,4},{6,7},{7,6},{8,9},{9,8},{10,11... | collective-permute-start | bytes 393224 | tf_op jit(solution)/shard_map/ppermute | solution.py:26
  72.4 4.3 %collective-permute-start.30 = (bf16[16,4096]{1,0:T(8,128)(2,1)S(1)}, bf16[16,4096]{1,0:T(8,128)(2,1)S(1)}, u32[]{:S(2)}, u32[]{:S(2)}) collective-permute-start(bf16[16,4096]{1,0:T(8,128)(2,1)S(1)} %get-tuple-element.38), channel_id=1, source_target_pairs={{0,1},{1,0},{2,3},{3,2},{4,5},{5,4},{6,7},{7,6},{8,9},{9,8},{10,11... | collective-permute-start | bytes 393224 | tf_op jit(solution)/shard_map/ppermute | solution.py:26
  72.9 6.4 %collective-permute-start.32 = (bf16[16,4096]{1,0:T(8,128)(2,1)S(1)}, bf16[16,4096]{1,0:T(8,128)(2,1)S(1)}, u32[]{:S(2)}, u32[]{:S(2)}) collective-permute-start(bf16[16,4096]{1,0:T(8,128)(2,1)S(1)} %add.146), channel_id=1, source_target_pairs={{0,2},{1,3},{2,0},{3,1},{4,6},{5,7},{6,4},{7,5},{8,10},{9,11},{10,... | collective-permute-start | bytes 393224 | tf_op jit(solution)/shard_map/ppermute | solution.py:26
  73.6 6.1 %collective-permute-start.34 = (bf16[16,4096]{1,0:T(8,128)(2,1)S(1)}, bf16[16,4096]{1,0:T(8,128)(2,1)S(1)}, u32[]{:S(2)}, u32[]{:S(2)}) collective-permute-start(bf16[16,4096]{1,0:T(8,128)(2,1)S(1)} %add.147), channel_id=1, source_target_pairs={{0,4},{1,5},{2,6},{3,7},{4,0},{5,1},{6,2},{7,3},{8,12},{9,13},{10,... | collective-permute-start | bytes 393224 | tf_op jit(solution)/shard_map/ppermute | solution.py:26
  74.7 7.3 %collective-permute-start.36 = (bf16[16,4096]{1,0:T(8,128)(2,1)S(1)}, bf16[16,4096]{1,0:T(8,128)(2,1)S(1)}, u32[]{:S(2)}, u32[]{:S(2)}) collective-permute-start(bf16[16,4096]{1,0:T(8,128)(2,1)S(1)} %add.148), channel_id=1, source_target_pairs={{0,6},{1,7},{2,4},{3,5},{4,2},{5,3},{6,0},{7,1},{8,14},{9,15},{10,... | collective-permute-start | bytes 393224 | tf_op jit(solution)/shard_map/ppermute | solution.py:26
  82.1 4.5 %collective-permute-start.37 = (bf16[4,4096]{1,0:T(4,128)(2,1)S(1)}, bf16[4,4096]{1,0:T(4,128)(2,1)S(1)}, u32[]{:S(2)}, u32[]{:S(2)}) collective-permute-start(bf16[4,4096]{1,0:T(4,128)(2,1)S(1)} %get-tuple-element.48), channel_id=1, source_target_pairs={{0,8},{1,9},{2,10},{3,11},{4,12},{5,13},{6,14},{7,15},{8,0},{9,1},... | collective-permute-start | bytes 98312 | tf_op jit(solution)/shard_map/ppermute | solution.py:26
  82.2 4.9 %collective-permute-start.38 = (bf16[4,4096]{1,0:T(4,128)(2,1)S(1)}, bf16[4,4096]{1,0:T(4,128)(2,1)S(1)}, u32[]{:S(2)}, u32[]{:S(2)}) collective-permute-start(bf16[4,4096]{1,0:T(4,128)(2,1)S(1)} %get-tuple-element.50), channel_id=1, source_target_pairs={{0,16},{1,17},{2,18},{3,19},{4,20},{5,21},{6,22},{7,23},{8,24},{9,... | collective-permute-start | bytes 98312 | tf_op jit(solution)/shard_map/ppermute | solution.py:26
  84.5 5.7 %collective-permute-start.39 = (bf16[4,4096]{1,0:T(4,128)(2,1)S(1)}, bf16[4,4096]{1,0:T(4,128)(2,1)S(1)}, u32[]{:S(2)}, u32[]{:S(2)}) collective-permute-start(bf16[4,4096]{1,0:T(4,128)(2,1)S(1)} %get-tuple-element.49), channel_id=1, source_target_pairs={{0,24},{1,25},{2,26},{3,27},{4,28},{5,29},{6,30},{7,31},{8,16},{9,... | collective-permute-start | bytes 98312 | tf_op jit(solution)/shard_map/ppermute | solution.py:26

commit v4 on v3

--- a/solution.py
+++ b/solution.py
@@ -37,9 +37,11 @@
     return low, mid, high
 
 
-def pack_body(*refs, feature, per_group, count):
-    sources, outs, held, sems = refs[:5], refs[5 : 5 + count], refs[5 + count : 10 + count], refs[10 + count]
-    copies = [pltpu.make_async_copy(source, to, sems.at[i]) for i, (source, to) in enumerate(zip(sources, held))]
+def pack_body(*refs, feature, per_group, count, tables):
+    sources, refs = refs[: 5 + tables], refs[5 + tables :]
+    outs, kept, held, sems = refs[:count], refs[count : count + tables], refs[count + tables : -1], refs[-1]
+    goals = (*held, *kept)
+    copies = [pltpu.make_async_copy(source, to, sems.at[i]) for i, (source, to) in enumerate(zip(sources, goals))]
     for copy in copies:
         copy.start()
     for copy in copies:
@@ -68,7 +70,7 @@
         out[top : top + rows, HD : 2 * HD] = own_value[:, lanes]
 
 
-def repack_body(after, also, *refs, kv_rows, rows):
+def repack_body(*refs, kv_rows, rows):
     outs = refs[-MID:]
     parts = refs[:-MID]
     for zx, part in enumerate(parts):
@@ -80,7 +82,7 @@
             out[zx, kv_rows + rows : kv_rows + 2 * rows, :] = part[own : own + rows, :]
 
 
-def attend_body(info, *refs, ctx_local, kv_rows, rows):
+def attend_body(prefix_of, lengths, *refs, ctx_local, kv_rows, rows):
     mine, other = refs[:MID], refs[MID : 2 * MID]
     w_out, keep = refs[2 * MID : 2 * MID + 2]
     sends, att = refs[2 * MID + 2 : -1], refs[-1]
@@ -105,8 +107,8 @@
         return jnp.concatenate([part[zs, at, lanes].reshape(depth, -1) for part in parts], axis=0)
 
     for zg in range(high // span):
-        prefix = info[own_group ^ zg]
-        length = info[high // span + prefix]
+        prefix = prefix_of[(own_group ^ zg) * CAND]
+        length = lengths[prefix]
         zs = slice(zg * span, (zg + 1) * span)
         tails = slice(kv_rows, kv_rows + tile)
         at = pl.ds(pl.multiple_of(prefix * ctx_local, ctx_local), ctx_local)
@@ -151,13 +153,13 @@
         send[...] = out[half + i * count : half + (i + 1) * count].astype(jnp.bfloat16)
 
 
-def dequantize_strips(out, codes, scales, first, count, offset):
-    across = codes.shape[1] // BLK
+def dequantize_strips(out, codes, scales, across, first, count, offset):
     for i in range(first, first + count):
         rows = slice(i * BLK, (i + 1) * BLK)
         for j in range(codes.shape[1] // BLK):
             lanes = slice(j * BLK, (j + 1) * BLK)
-            out[rows, lanes] = (codes[rows, lanes].astype(jnp.float32) * scales[offset + i * across + j]).astype(jnp.bfloat16)
+            scale = scales[j, 0, offset + i] if across else scales[offset + i, 0, j]
+            out[rows, lanes] = (codes[rows, lanes].astype(jnp.float32) * scale).astype(jnp.bfloat16)
 
 
 def strip_rows(shape):
@@ -168,19 +170,19 @@
     return count * BLK
 
 
-def prepare_body(*refs, ranges, fetched):
+def prepare_body(*refs, ranges, fetched, across):
     count = len(ranges)
     scales, sources, plain = refs[0], refs[1 : 1 + count], refs[1 + count : 1 + count + fetched]
     refs = refs[1 + count + fetched :]
     outs, fetch, held, sems = refs[:count], refs[count : count + fetched], refs[count + fetched : -1], refs[-1]
     jobs = []
-    for source, to, out, (start, size, base) in zip(sources, held, outs, ranges):
+    for source, to, out, (start, size) in zip(sources, held, outs, ranges):
         step = strip_rows((size, source.shape[1]))
         for first in range(0, size, step):
             copy = pltpu.make_async_copy(
                 source.at[pl.ds(start + first, step)], to.at[pl.ds(first, step)], sems.at[len(jobs)]
             )
-            jobs.append((copy, (out, to, scales, first // BLK, step // BLK, base)))
+            jobs.append((copy, (out, to, scales, across, first // BLK, step // BLK, start // BLK)))
     direct = [pltpu.make_async_copy(a, to, sems.at[len(jobs) + i]) for i, (a, to) in enumerate(zip(plain, fetch))]
     for copy, _ in jobs[:DEPTH]:
         copy.start()
@@ -195,14 +197,14 @@
         copy.wait()
 
 
-def prepared(scales, weights, fetch=()):
+def prepared(scales, across, weights, fetch=()):
     codes = [item[0] for item in weights]
     ranges = tuple(item[1:] for item in weights)
     fetch = list(fetch)
-    shapes = [(size, a.shape[1]) for a, (_, size, _) in zip(codes, ranges)]
+    shapes = [(size, a.shape[1]) for a, (_, size) in zip(codes, ranges)]
     steps = sum(shape[0] // strip_rows(shape) for shape in shapes)
     return pl.pallas_call(
-        functools.partial(prepare_body, ranges=ranges, fetched=len(fetch)),
+        functools.partial(prepare_body, ranges=ranges, fetched=len(fetch), across=across),
         in_specs=[SMEM] + [HBM] * (len(codes) + len(fetch)),
         out_specs=[VMEM] * (len(codes) + len(fetch)),
         out_shape=[pltpu.VMEM(shape, jnp.bfloat16) for shape in shapes] + [pltpu.VMEM(a.shape, a.dtype) for a in fetch],
@@ -325,30 +327,31 @@
     kv_rows = prefixes * ctx_local
     feature = w_out.shape[0]
     low, mid, high = stage_offsets(shards)
-    info = jnp.concatenate([prefix_of_row[::CAND], context_len])
-    scales = jnp.concatenate([gate_up_scales.reshape(-1), down_scales.reshape(-1)])
+    tables = (prefix_of_row, context_len, gate_up_scales.transpose(2, 0, 1), down_scales.transpose(1, 0, 2))
 
     inputs = (queries, own_key, own_value, cache_keys, cache_values)
     message = jax.ShapeDtypeStruct((kv_rows + MID * rows + 2 * rows, 2 * HD), jnp.bfloat16)
-    messages = pl.pallas_call(
-        functools.partial(pack_body, feature=feature, per_group=per_group, count=len(high)),
-        in_specs=[HBM] * len(inputs),
-        out_specs=[VMEM] * len(high),
-        out_shape=[message] * len(high),
-        scratch_shapes=[pltpu.VMEM(a.shape, a.dtype) for a in inputs] + [pltpu.SemaphoreType.DMA((len(inputs),))],
+    steps = len(inputs) + len(tables)
+    packed = pl.pallas_call(
+        functools.partial(pack_body, feature=feature, per_group=per_group, count=len(high), tables=len(tables)),
+        in_specs=[HBM] * steps,
+        out_specs=[VMEM] * (len(high) + len(tables)),
+        out_shape=[message] * len(high) + [jax.ShapeDtypeStruct(a.shape, a.dtype) for a in tables],
+        scratch_shapes=[pltpu.VMEM(a.shape, a.dtype) for a in inputs] + [pltpu.SemaphoreType.DMA((steps,))],
         compiler_params=pltpu.CompilerParams(vmem_limit_bytes=SMALL_VMEM),
         name="pack",
-    )(*(in_hbm(item) for item in inputs))
+    )(*(in_hbm(item) for item in inputs + tables))
+    messages, (prefix_of, lengths, gate_scales, low_scales) = packed[: len(high)], packed[len(high) :]
     got = [messages[0]] + [swapped(messages[i], high[i]) for i in range(1, len(high))]
     piece = jax.ShapeDtypeStruct((len(high), kv_rows + 2 * rows, 2 * HD), jnp.bfloat16)
     messages = pl.pallas_call(
         functools.partial(repack_body, kv_rows=kv_rows, rows=rows),
-        in_specs=[ANY] * 2 + [VMEM] * len(high),
+        in_specs=[VMEM] * len(high),
         out_specs=[VMEM] * MID,
         out_shape=[piece] * MID,
         compiler_params=pltpu.CompilerParams(vmem_limit_bytes=2 * SMALL_VMEM),
         name="repack",
-    )(info, scales, *got)
+    )(*got)
     mine = [messages[0]] + [swapped(messages[i], mid[i]) for i in range(1, MID)]
     other = [swapped(item, low[1]) for item in mine]
 
@@ -360,14 +363,14 @@
         w_full = w_out
     codes = gate_up_codes[0]
     first = codes.shape[0] // 2
-    gate_first, w_full = prepared(scales, [(codes, 0, first, 0)], [w_full])
-    (down,) = prepared(scales, [(down_codes[0], 0, down_codes.shape[1], gate_up_scales.size)])
-    (gate_rest,) = prepared(scales, [(codes, first, codes.shape[0] - first, first // BLK * gate_up_scales.shape[2])])
+    gate_first, w_full = prepared(gate_scales, True, [(codes, 0, first)], [w_full])
+    (down,) = prepared(low_scales, False, [(down_codes[0], 0, down_codes.shape[1])])
+    (gate_rest,) = prepared(gate_scales, True, [(codes, first, codes.shape[0] - first)])
     half = shards * rows // 2
     attend_vmem = 8 * 2**20 + 2 * MID * piece.size * 2 + w_full.size * 2 + half * width * 10
     keep, *sends = pl.pallas_call(
         functools.partial(attend_body, ctx_local=ctx_local, kv_rows=kv_rows, rows=rows),
-        in_specs=[SMEM] + [VMEM] * (2 * MID + 1),
+        in_specs=[SMEM] * 2 + [VMEM] * (2 * MID + 1),
         out_specs=[VMEM] * (1 + MID),
         out_shape=[
             jax.ShapeDtypeStruct((half, width), jnp.float32),
@@ -378,7 +381,7 @@
         ],
         compiler_params=pltpu.CompilerParams(vmem_limit_bytes=attend_vmem),
         name="attend",
-    )(info, *mine, *other, w_full)
+    )(prefix_of, lengths, *mine, *other, w_full)
 
     projected = scatter_sum(keep, sends, mid, high)
     mixed = hidden_in.astype(jnp.float32) + projected

time: 91.2 us -> 90.3 us (level)
  waiting for transfers between devices: 35.6 us -> 37.8 us
  local copies, waits for them, and re-layouts: 1.9 us -> 0.21 us
  other arithmetic: 2.69 us -> 1.19 us
    ppermute x40, waiting for transfers between devices: 35.6 us -> 37.8 us  [swapped(): lax.ppermute(value, 'ctx', [(i, i ^ offset) for i in range(lax.axis_size(...]
  transfers between devices with their start and end apart: 40 -> 40, of which waited for: 20 -> 20; matrix products, arithmetic and copies ran while one was open for 4% -> 0% of each run, Pallas kernels for 9% -> 9%
where the time goes in v4:
time: 90.3 us; the launch traced here: 90 us
  waiting for transfers between devices  37.8 us (42%)
  starting transfers between devices  36.2 us (40%)
  Pallas kernels  13.7 us (15%)
  other arithmetic  1.19 us (1%)
  between operations  0.91 us (1%)
    ppermute x40, waiting for transfers between devices, swapped(): lax.ppermute(value, 'ctx', [(i, i ^ offset) for i in range(lax.axis_size(...  37.8 us
    ppermute x40, starting transfers between devices, swapped(): lax.ppermute(value, 'ctx', [(i, i ^ offset) for i in range(lax.axis_size(...  36.2 us
    pallas_call x3, Pallas kernels, prepared(): pl.pallas_call(functools.partial(prepare_body, ranges=ranges, fetched=len...  8.18 us
    pallas_call x1, Pallas kernels, local(): pl.pallas_call(functools.partial(expert_body, width=width, experts=expert...  2.22 us
    pallas_call x1, Pallas kernels, local(): pl.pallas_call(functools.partial(attend_body, ctx_local=ctx_local, kv_row...  1.92 us
  transfers between devices with their start and end apart: 40, of which 20 were waited for; matrix products, arithmetic and copies ran while one was open for 0% of the time, Pallas kernels for 9%

profile of v4, /device:TPU:0, one launch (start us, length us, event | category | flops | bytes accessed | tf_op | source)
XLA Modules:
  0.0 90.0 jit_solution(5365422704875197554)
XLA Ops:
  0.6 1.1 %pack.1 = (bf16[88,256]{1,0:T(8,128)(2,1)S(1)}, bf16[88,256]{1,0:T(8,128)(2,1)S(1)}, bf16[88,256]{1,0:T(8,128)(2,1)S(1)}, bf16[88,256]{1,0:T(8,128)(2,1)S(1)}, s...) custom-call(bf16[4,4096]{1,0:T(4,128)(2,1)} %refs_0_.1, ...), custom_call_target="tpu_custom_call" | custom-call | tf_op jit(solution)/shard_map/pack/pallas_call | solution.py:335
  1.8 3.1 %collective-permute-start = (bf16[88,256]{1,0:T(8,128)(2,1)S(1)}, bf16[88,256]{1,0:T(8,128)(2,1)S(1)}, u32[]{:S(2)}, u32[]{:S(2)}) collective-permute-start(bf16[88,256]{1,0:T(8,128)(2,1)S(1)} %get-tuple-element.29), channel_id=1, source_target_pairs={{0,8},{1,9},{2,10},{3,11},{4,12},{5,13},{6,14},{7,15},{8,0},{9,1},... | collective-permute-start | bytes 135176 | tf_op jit(solution)/shard_map/ppermute | solution.py:26
  4.9 2.6 %collective-permute-start.1 = (bf16[88,256]{1,0:T(8,128)(2,1)S(1)}, bf16[88,256]{1,0:T(8,128)(2,1)S(1)}, u32[]{:S(2)}, u32[]{:S(2)}) collective-permute-start(bf16[88,256]{1,0:T(8,128)(2,1)S(1)} %get-tuple-element.30), channel_id=1, source_target_pairs={{0,16},{1,17},{2,18},{3,19},{4,20},{5,21},{6,22},{7,23},{8,24},{9,... | collective-permute-start | bytes 135176 | tf_op jit(solution)/shard_map/ppermute | solution.py:26
  7.5 3.2 %collective-permute-done.1.refs_2_ = bf16[88,256]{1,0:T(8,128)(2,1)S(1)} collective-permute-done((bf16[88,256]{1,0:T(8,128)(2,1)S(1)}, bf16[88,256]{1,0:T(8,128)(2,1)S(1)}, u32[]{:S(2)}, u32[]{:S(2)}) %collective-permute-start.1) | collective-permute-done | bytes 45088 | tf_op jit(solution)/shard_map/ppermute | solution.py:26
  10.7 2.6 %collective-permute-done.2.refs_3_ = bf16[88,256]{1,0:T(8,128)(2,1)S(1)} collective-permute-done((bf16[88,256]{1,0:T(8,128)(2,1)S(1)}, bf16[88,256]{1,0:T(8,128)(2,1)S(1)}, u32[]{:S(2)}, u32[]{:S(2)}) %collective-permute-start.2) | collective-permute-done | bytes 45088 | tf_op jit(solution)/shard_map/ppermute | solution.py:26
  13.4 1.6 %collective-permute-start.3 = (bf16[4,72,256]{2,1,0:T(8,128)(2,1)S(1)}, bf16[4,72,256]{2,1,0:T(8,128)(2,1)S(1)}, u32[]{:S(2)}, u32[]{:S(2)}) collective-permute-start(bf16[4,72,256]{2,1,0:T(8,128)(2,1)S(1)} %get-tuple-element.33), channel_id=1, source_target_pairs={{0,2},{1,3},{2,0},{3,1},{4,6},{5,7},{6,4},{7,5},{8,10},{9,11},{10,... | collective-permute-start | bytes 442376 | tf_op jit(solution)/shard_map/ppermute | solution.py:26
  14.9 1.5 %collective-permute-start.4 = (bf16[4,72,256]{2,1,0:T(8,128)(2,1)S(1)}, bf16[4,72,256]{2,1,0:T(8,128)(2,1)S(1)}, u32[]{:S(2)}, u32[]{:S(2)}) collective-permute-start(bf16[4,72,256]{2,1,0:T(8,128)(2,1)S(1)} %get-tuple-element.34), channel_id=1, source_target_pairs={{0,4},{1,5},{2,6},{3,7},{4,0},{5,1},{6,2},{7,3},{8,12},{9,13},{10,... | collective-permute-start | bytes 442376 | tf_op jit(solution)/shard_map/ppermute | solution.py:26
  16.4 0.5 collective-permute-start.5
  16.9 2.9 %collective-permute-done.3.refs_1_ = bf16[4,72,256]{2,1,0:T(8,128)(2,1)S(1)} collective-permute-done((bf16[4,72,256]{2,1,0:T(8,128)(2,1)S(1)}, bf16[4,72,256]{2,1,0:T(8,128)(2,1)S(1)}, u32[]{:S(2)}, u32[]{:S(2)}) %collective-permute-start.3) | collective-permute-done | bytes 147488 | tf_op jit(solution)/shard_map/ppermute | solution.py:26
  19.8 2.8 %collective-permute-done.4.refs_2_ = bf16[4,72,256]{2,1,0:T(8,128)(2,1)S(1)} collective-permute-done((bf16[4,72,256]{2,1,0:T(8,128)(2,1)S(1)}, bf16[4,72,256]{2,1,0:T(8,128)(2,1)S(1)}, u32[]{:S(2)}, u32[]{:S(2)}) %collective-permute-start.4) | collective-permute-done | bytes 147488 | tf_op jit(solution)/shard_map/ppermute | solution.py:26
  22.6 0.5 collective-permute-start.9
  23.1 2.8 %prepare.3 = (bf16[2048,768]{1,0:T(8,128)(2,1)S(1)}, bf16[128,4096]{1,0:T(8,128)(2,1)S(1)}) custom-call(f32[6,1,32]{2,1,0:T(1,128)S(1)} %get-tuple-element.36.refs_0_, bf16[4096,768]{1,0:T(8,128)(2,1)} %bitcast.4, bf16[128,4096]{1,0:T(8,128)(2,1)} %refs_2_.3), custom_call_target="tpu_custom_call" | custom-call | tf_op jit(solution)/shard_map/prepare/pallas_call | solution.py:206
  26.0 1.9 %attend.1 = (f32[64,4096]{1,0:T(8,128)S(1)}, bf16[16,4096]{1,0:T(8,128)(2,1)S(1)}, bf16[16,4096]{1,0:T(8,128)(2,1)S(1)}, bf16[16,4096]{1,0:T(8,128)(2,1)S(1)}, bf16[16,4096]{1,0:T(8,128)(2,1)S(1)}) custom-call(s32[128]{0:T(128)S(1)} %get-tuple-element.26.prefix_of, s32[2]{0:T(128)S(1)} %get-tuple-element.27.lengths, ...), custom_call_target="tpu_custom_call" | custom-call | tf_op jit(solution)/shard_map/attend/pallas_call | solution.py:371
  27.9 0.1 collective-permute-start.11
  28.0 0.5 collective-permute-start.13
  28.5 0.1 collective-permute-start.15
  28.6 0.4 collective-permute-start.10
  29.0 0.3 collective-permute-done.11.got
  29.4 0.1 collective-permute-start.12
  29.6 1.2 %collective-permute-start.14 = (bf16[16,4096]{1,0:T(8,128)(2,1)S(1)}, bf16[16,4096]{1,0:T(8,128)(2,1)S(1)}, u32[]{:S(2)}, u32[]{:S(2)}) collective-permute-start(bf16[16,4096]{1,0:T(8,128)(2,1)S(1)} %add.141), channel_id=1, source_target_pairs={{0,4},{1,5},{2,6},{3,7},{4,0},{5,1},{6,2},{7,3},{8,12},{9,13},{10,... | collective-permute-start | bytes 393224 | tf_op jit(solution)/shard_map/ppermute | solution.py:26
  30.9 2.3 %collective-permute-start.16 = (bf16[16,4096]{1,0:T(8,128)(2,1)S(1)}, bf16[16,4096]{1,0:T(8,128)(2,1)S(1)}, u32[]{:S(2)}, u32[]{:S(2)}) collective-permute-start(bf16[16,4096]{1,0:T(8,128)(2,1)S(1)} %add.142), channel_id=1, source_target_pairs={{0,6},{1,7},{2,4},{3,5},{4,2},{5,3},{6,0},{7,1},{8,14},{9,15},{10,... | collective-permute-start | bytes 393224 | tf_op jit(solution)/shard_map/ppermute | solution.py:26
  33.2 0.1 select_reduce_fusion
  33.3 2.6 %collective-permute-done.12 = bf16[16,4096]{1,0:T(8,128)(2,1)S(1)} collective-permute-done((bf16[16,4096]{1,0:T(8,128)(2,1)S(1)}, bf16[16,4096]{1,0:T(8,128)(2,1)S(1)}, u32[]{:S(2)}, u32[]{:S(2)}) %collective-permute-start.12) | collective-permute-done | bytes 131104 | tf_op jit(solution)/shard_map/ppermute | solution.py:26
  35.8 0.3 collective-permute-done.14
  36.1 2.2 %collective-permute-done.16 = bf16[16,4096]{1,0:T(8,128)(2,1)S(1)} collective-permute-done((bf16[16,4096]{1,0:T(8,128)(2,1)S(1)}, bf16[16,4096]{1,0:T(8,128)(2,1)S(1)}, u32[]{:S(2)}, u32[]{:S(2)}) %collective-permute-start.16) | collective-permute-done | bytes 131104 | tf_op jit(solution)/shard_map/ppermute | solution.py:26
  38.3 0.1 fusion.10
  38.4 0.1 collective-permute-start.17
  38.5 1.3 %collective-permute-start.18 = (bf16[4,4096]{1,0:T(4,128)(2,1)S(1)}, bf16[4,4096]{1,0:T(4,128)(2,1)S(1)}, u32[]{:S(2)}, u32[]{:S(2)}) collective-permute-start(bf16[4,4096]{1,0:T(4,128)(2,1)S(1)} %get-tuple-element.61), channel_id=1, source_target_pairs={{0,16},{1,17},{2,18},{3,19},{4,20},{5,21},{6,22},{7,23},{8,24},{9,... | collective-permute-start | bytes 98312 | tf_op jit(solution)/shard_map/ppermute | solution.py:26
  39.8 3.1 %collective-permute-start.19 = (bf16[4,4096]{1,0:T(4,128)(2,1)S(1)}, bf16[4,4096]{1,0:T(4,128)(2,1)S(1)}, u32[]{:S(2)}, u32[]{:S(2)}) collective-permute-start(bf16[4,4096]{1,0:T(4,128)(2,1)S(1)} %get-tuple-element.60), channel_id=1, source_target_pairs={{0,24},{1,25},{2,26},{3,27},{4,28},{5,29},{6,30},{7,31},{8,16},{9,... | collective-permute-start | bytes 98312 | tf_op jit(solution)/shard_map/ppermute | solution.py:26
  42.9 0.7 collective-permute-done.18
  43.6 1.9 %collective-permute-done.19 = bf16[4,4096]{1,0:T(4,128)(2,1)S(1)} collective-permute-done((bf16[4,4096]{1,0:T(4,128)(2,1)S(1)}, bf16[4,4096]{1,0:T(4,128)(2,1)S(1)}, u32[]{:S(2)}, u32[]{:S(2)}) %collective-permute-start.19) | collective-permute-done | bytes 32800 | tf_op jit(solution)/shard_map/ppermute | solution.py:26
  45.5 0.2 multiply_reduce_fusion
  45.7 0.1 multiply_convert_fusion
  45.8 0.1 concatenate.6.refs_0_
  45.9 4.0 %collective-permute-start.21 = (bf16[4,4224]{1,0:T(4,128)(2,1)S(1)}, bf16[4,4224]{1,0:T(4,128)(2,1)S(1)}, u32[]{:S(2)}, u32[]{:S(2)}) collective-permute-start(bf16[4,4224]{1,0:T(4,128)(2,1)S(1)} %concatenate.6.refs_0_), channel_id=1, source_target_pairs={{0,16},{1,17},{2,18},{3,19},{4,20},{5,21},{6,22},{7,23},{8,24},{9,... | collective-permute-start | bytes 101384 | tf_op jit(solution)/shard_map/ppermute | solution.py:26
  49.9 0.4 collective-permute-start.22
  50.3 2.0 %collective-permute-done.21.refs_2_ = bf16[4,4224]{1,0:T(4,128)(2,1)S(1)} collective-permute-done((bf16[4,4224]{1,0:T(4,128)(2,1)S(1)}, bf16[4,4224]{1,0:T(4,128)(2,1)S(1)}, u32[]{:S(2)}, u32[]{:S(2)}) %collective-permute-start.21) | collective-permute-done | bytes 33824 | tf_op jit(solution)/shard_map/ppermute | solution.py:26
  52.3 3.3 %collective-permute-done.22.refs_3_ = bf16[4,4224]{1,0:T(4,128)(2,1)S(1)} collective-permute-done((bf16[4,4224]{1,0:T(4,128)(2,1)S(1)}, bf16[4,4224]{1,0:T(4,128)(2,1)S(1)}, u32[]{:S(2)}, u32[]{:S(2)}) %collective-permute-start.22) | collective-permute-done | bytes 33824 | tf_op jit(solution)/shard_map/ppermute | solution.py:26
  55.6 1.2 %collective-permute-start.23 = (bf16[16,4224]{1,0:T(8,128)(2,1)S(1)}, bf16[16,4224]{1,0:T(8,128)(2,1)S(1)}, u32[]{:S(2)}, u32[]{:S(2)}) collective-permute-start(bf16[16,4224]{1,0:T(8,128)(2,1)S(1)} %join.1.refs_0_), channel_id=1, source_target_pairs={{0,2},{1,3},{2,0},{3,1},{4,6},{5,7},{6,4},{7,5},{8,10},{9,11},{10,... | collective-permute-start | bytes 405512 | tf_op jit(solution)/shard_map/ppermute | solution.py:26
  56.8 1.0 %collective-permute-start.24 = (bf16[16,4224]{1,0:T(8,128)(2,1)S(1)}, bf16[16,4224]{1,0:T(8,128)(2,1)S(1)}, u32[]{:S(2)}, u32[]{:S(2)}) collective-permute-start(bf16[16,4224]{1,0:T(8,128)(2,1)S(1)} %join.1.refs_0_), channel_id=1, source_target_pairs={{0,4},{1,5},{2,6},{3,7},{4,0},{5,1},{6,2},{7,3},{8,12},{9,13},{10,... | collective-permute-start | bytes 405512 | tf_op jit(solution)/shard_map/ppermute | solution.py:26
  57.8 1.4 %collective-permute-start.25 = (bf16[16,4224]{1,0:T(8,128)(2,1)S(1)}, bf16[16,4224]{1,0:T(8,128)(2,1)S(1)}, u32[]{:S(2)}, u32[]{:S(2)}) collective-permute-start(bf16[16,4224]{1,0:T(8,128)(2,1)S(1)} %join.1.refs_0_), channel_id=1, source_target_pairs={{0,6},{1,7},{2,4},{3,5},{4,2},{5,3},{6,0},{7,1},{8,14},{9,15},{10,... | collective-permute-start | bytes 405512 | tf_op jit(solution)/shard_map/ppermute | solution.py:26
  59.2 1.5 %collective-permute-done.23.refs_1_ = bf16[16,4224]{1,0:T(8,128)(2,1)S(1)} collective-permute-done((bf16[16,4224]{1,0:T(8,128)(2,1)S(1)}, bf16[16,4224]{1,0:T(8,128)(2,1)S(1)}, u32[]{:S(2)}, u32[]{:S(2)}) %collective-permute-start.23) | collective-permute-done | bytes 135200 | tf_op jit(solution)/shard_map/ppermute | solution.py:26
  60.7 1.1 %collective-permute-done.24.refs_2_ = bf16[16,4224]{1,0:T(8,128)(2,1)S(1)} collective-permute-done((bf16[16,4224]{1,0:T(8,128)(2,1)S(1)}, bf16[16,4224]{1,0:T(8,128)(2,1)S(1)}, u32[]{:S(2)}, u32[]{:S(2)}) %collective-permute-start.24) | collective-permute-done | bytes 135200 | tf_op jit(solution)/shard_map/ppermute | solution.py:26
  61.8 1.9 %collective-permute-done.25.refs_3_ = bf16[16,4224]{1,0:T(8,128)(2,1)S(1)} collective-permute-done((bf16[16,4224]{1,0:T(8,128)(2,1)S(1)}, bf16[16,4224]{1,0:T(8,128)(2,1)S(1)}, u32[]{:S(2)}, u32[]{:S(2)}) %collective-permute-start.25) | collective-permute-done | bytes 135200 | tf_op jit(solution)/shard_map/ppermute | solution.py:26
  63.7 2.6 %prepare.4.refs_9_ = bf16[2048,768]{1,0:T(8,128)(2,1)S(1)} custom-call(f32[6,1,32]{2,1,0:T(1,128)S(1)} %get-tuple-element.36.refs_0_, bf16[4096,768]{1,0:T(8,128)(2,1)} %bitcast.5), custom_call_target="tpu_custom_call" | custom-call | tf_op jit(solution)/shard_map/prepare/pallas_call | solution.py:206
  66.3 2.8 %prepare.5.refs_10_ = bf16[384,4096]{1,0:T(8,128)(2,1)S(1)} custom-call(f32[3,1,32]{2,1,0:T(1,128)S(1)} %get-tuple-element.44.refs_0_, bf16[384,4096]{1,0:T(8,128)(2,1)} %bitcast.6), custom_call_target="tpu_custom_call" | custom-call | tf_op jit(solution)/shard_map/prepare/pallas_call | solution.py:206
  69.2 2.2 %expert.1 = (f32[64,4096]{1,0:T(8,128)S(1)}, bf16[16,4096]{1,0:T(8,128)(2,1)S(1)}, bf16[16,4096]{1,0:T(8,128)(2,1)S(1)}, bf16[16,4096]{1,0:T(8,128)(2,1)S(1)}, bf16[16,4096]{1,0:T(8,128)(2,1)S(1)}) custom-call(bf16[16,4224]{1,0:T(8,128)(2,1)S(1)} %join.1.refs_0_, bf16[16,4224]{1,0:T(8,128)(2,1)S(1)} %collective-permute-done.23.refs_1_, ...), custom_call_target="tpu_custom_call" | custom-call | tf_op jit(solution)/shard_map/expert/pallas_call | solution.py:404
  71.4 0.6 collective-permute-start.31
  72.0 0.1 collective-permute-start.33
  72.0 0.4 collective-permute-start.35
  72.5 0.1 collective-permute-start.30
  72.5 0.4 collective-permute-done.31.got
  73.0 1.0 %collective-permute-start.32 = (bf16[16,4096]{1,0:T(8,128)(2,1)S(1)}, bf16[16,4096]{1,0:T(8,128)(2,1)S(1)}, u32[]{:S(2)}, u32[]{:S(2)}) collective-permute-start(bf16[16,4096]{1,0:T(8,128)(2,1)S(1)} %add.143), channel_id=1, source_target_pairs={{0,2},{1,3},{2,0},{3,1},{4,6},{5,7},{6,4},{7,5},{8,10},{9,11},{10,... | collective-permute-start | bytes 393224 | tf_op jit(solution)/shard_map/ppermute | solution.py:26
  74.0 1.1 %collective-permute-start.34 = (bf16[16,4096]{1,0:T(8,128)(2,1)S(1)}, bf16[16,4096]{1,0:T(8,128)(2,1)S(1)}, u32[]{:S(2)}, u32[]{:S(2)}) collective-permute-start(bf16[16,4096]{1,0:T(8,128)(2,1)S(1)} %add.144), channel_id=1, source_target_pairs={{0,4},{1,5},{2,6},{3,7},{4,0},{5,1},{6,2},{7,3},{8,12},{9,13},{10,... | collective-permute-start | bytes 393224 | tf_op jit(solution)/shard_map/ppermute | solution.py:26
  75.1 1.6 %collective-permute-start.36 = (bf16[16,4096]{1,0:T(8,128)(2,1)S(1)}, bf16[16,4096]{1,0:T(8,128)(2,1)S(1)}, u32[]{:S(2)}, u32[]{:S(2)}) collective-permute-start(bf16[16,4096]{1,0:T(8,128)(2,1)S(1)} %add.145), channel_id=1, source_target_pairs={{0,6},{1,7},{2,4},{3,5},{4,2},{5,3},{6,0},{7,1},{8,14},{9,15},{10,... | collective-permute-start | bytes 393224 | tf_op jit(solution)/shard_map/ppermute | solution.py:26
  76.7 2.7 %collective-permute-done.32 = bf16[16,4096]{1,0:T(8,128)(2,1)S(1)} collective-permute-done((bf16[16,4096]{1,0:T(8,128)(2,1)S(1)}, bf16[16,4096]{1,0:T(8,128)(2,1)S(1)}, u32[]{:S(2)}, u32[]{:S(2)}) %collective-permute-start.32) | collective-permute-done | bytes 131104 | tf_op jit(solution)/shard_map/ppermute | solution.py:26
  79.4 2.9 %collective-permute-done.34 = bf16[16,4096]{1,0:T(8,128)(2,1)S(1)} collective-permute-done((bf16[16,4096]{1,0:T(8,128)(2,1)S(1)}, bf16[16,4096]{1,0:T(8,128)(2,1)S(1)}, u32[]{:S(2)}, u32[]{:S(2)}) %collective-permute-start.34) | collective-permute-done | bytes 131104 | tf_op jit(solution)/shard_map/ppermute | solution.py:26
  82.3 0.1 fusion.8
  82.5 0.1 collective-permute-start.37
  82.6 1.1 %collective-permute-start.38 = (bf16[4,4096]{1,0:T(4,128)(2,1)S(1)}, bf16[4,4096]{1,0:T(4,128)(2,1)S(1)}, u32[]{:S(2)}, u32[]{:S(2)}) collective-permute-start(bf16[4,4096]{1,0:T(4,128)(2,1)S(1)} %get-tuple-element.58), channel_id=1, source_target_pairs={{0,16},{1,17},{2,18},{3,19},{4,20},{5,21},{6,22},{7,23},{8,24},{9,... | collective-permute-start | bytes 98312 | tf_op jit(solution)/shard_map/ppermute | solution.py:26
  83.7 3.3 %collective-permute-start.39 = (bf16[4,4096]{1,0:T(4,128)(2,1)S(1)}, bf16[4,4096]{1,0:T(4,128)(2,1)S(1)}, u32[]{:S(2)}, u32[]{:S(2)}) collective-permute-start(bf16[4,4096]{1,0:T(4,128)(2,1)S(1)} %get-tuple-element.57), channel_id=1, source_target_pairs={{0,24},{1,25},{2,26},{3,27},{4,28},{5,29},{6,30},{7,31},{8,16},{9,... | collective-permute-start | bytes 98312 | tf_op jit(solution)/shard_map/ppermute | solution.py:26
  86.9 0.8 collective-permute-done.38
  87.7 1.7 %collective-permute-done.39 = bf16[4,4096]{1,0:T(4,128)(2,1)S(1)} collective-permute-done((bf16[4,4096]{1,0:T(4,128)(2,1)S(1)}, bf16[4,4096]{1,0:T(4,128)(2,1)S(1)}, u32[]{:S(2)}, u32[]{:S(2)}) %collective-permute-start.39) | collective-permute-done | bytes 32800 | tf_op jit(solution)/shard_map/ppermute | solution.py:26
  89.4 0.7 fusion.3
  (50 shorter events, 0.5 us)
Async XLA Ops:
  1.8 5.7 %collective-permute-start = (bf16[88,256]{1,0:T(8,128)(2,1)S(1)}, bf16[88,256]{1,0:T(8,128)(2,1)S(1)}, u32[]{:S(2)}, u32[]{:S(2)}) collective-permute-start(bf16[88,256]{1,0:T(8,128)(2,1)S(1)} %get-tuple-element.29), channel_id=1, source_target_pairs={{0,8},{1,9},{2,10},{3,11},{4,12},{5,13},{6,14},{7,15},{8,0},{9,1},... | collective-permute-start | bytes 135176 | tf_op jit(solution)/shard_map/ppermute | solution.py:26
  4.9 5.8 %collective-permute-start.1 = (bf16[88,256]{1,0:T(8,128)(2,1)S(1)}, bf16[88,256]{1,0:T(8,128)(2,1)S(1)}, u32[]{:S(2)}, u32[]{:S(2)}) collective-permute-start(bf16[88,256]{1,0:T(8,128)(2,1)S(1)} %get-tuple-element.30), channel_id=1, source_target_pairs={{0,16},{1,17},{2,18},{3,19},{4,20},{5,21},{6,22},{7,23},{8,24},{9,... | collective-permute-start | bytes 135176 | tf_op jit(solution)/shard_map/ppermute | solution.py:26
  7.5 5.8 %collective-permute-start.2 = (bf16[88,256]{1,0:T(8,128)(2,1)S(1)}, bf16[88,256]{1,0:T(8,128)(2,1)S(1)}, u32[]{:S(2)}, u32[]{:S(2)}) collective-permute-start(bf16[88,256]{1,0:T(8,128)(2,1)S(1)} %get-tuple-element.31), channel_id=1, source_target_pairs={{0,24},{1,25},{2,26},{3,27},{4,28},{5,29},{6,30},{7,31},{8,16},{9,... | collective-permute-start | bytes 135176 | tf_op jit(solution)/shard_map/ppermute | solution.py:26
  13.4 6.4 %collective-permute-start.3 = (bf16[4,72,256]{2,1,0:T(8,128)(2,1)S(1)}, bf16[4,72,256]{2,1,0:T(8,128)(2,1)S(1)}, u32[]{:S(2)}, u32[]{:S(2)}) collective-permute-start(bf16[4,72,256]{2,1,0:T(8,128)(2,1)S(1)} %get-tuple-element.33), channel_id=1, source_target_pairs={{0,2},{1,3},{2,0},{3,1},{4,6},{5,7},{6,4},{7,5},{8,10},{9,11},{10,... | collective-permute-start | bytes 442376 | tf_op jit(solution)/shard_map/ppermute | solution.py:26
  14.9 7.7 %collective-permute-start.4 = (bf16[4,72,256]{2,1,0:T(8,128)(2,1)S(1)}, bf16[4,72,256]{2,1,0:T(8,128)(2,1)S(1)}, u32[]{:S(2)}, u32[]{:S(2)}) collective-permute-start(bf16[4,72,256]{2,1,0:T(8,128)(2,1)S(1)} %get-tuple-element.34), channel_id=1, source_target_pairs={{0,4},{1,5},{2,6},{3,7},{4,0},{5,1},{6,2},{7,3},{8,12},{9,13},{10,... | collective-permute-start | bytes 442376 | tf_op jit(solution)/shard_map/ppermute | solution.py:26
  16.4 6.2 %collective-permute-start.5 = (bf16[4,72,256]{2,1,0:T(8,128)(2,1)S(1)}, bf16[4,72,256]{2,1,0:T(8,128)(2,1)S(1)}, u32[]{:S(2)}, u32[]{:S(2)}) collective-permute-start(bf16[4,72,256]{2,1,0:T(8,128)(2,1)S(1)} %get-tuple-element.35), channel_id=1, source_target_pairs={{0,6},{1,7},{2,4},{3,5},{4,2},{5,3},{6,0},{7,1},{8,14},{9,15},{10,... | collective-permute-start | bytes 442376 | tf_op jit(solution)/shard_map/ppermute | solution.py:26
  16.9 9.0 %collective-permute-start.6 = (bf16[4,72,256]{2,1,0:T(8,128)(2,1)S(1)}, bf16[4,72,256]{2,1,0:T(8,128)(2,1)S(1)}, u32[]{:S(2)}, u32[]{:S(2)}) collective-permute-start(bf16[4,72,256]{2,1,0:T(8,128)(2,1)S(1)} %get-tuple-element.32.refs_0_), channel_id=1, source_target_pairs={{0,1},{1,0},{2,3},{3,2},{4,5},{5,4},{6,7},{7,6},{8,9},{9,8},{10,11... | collective-permute-start | bytes 442376 | tf_op jit(solution)/shard_map/ppermute | solution.py:26
  19.8 6.2 %collective-permute-start.7 = (bf16[4,72,256]{2,1,0:T(8,128)(2,1)S(1)}, bf16[4,72,256]{2,1,0:T(8,128)(2,1)S(1)}, u32[]{:S(2)}, u32[]{:S(2)}) collective-permute-start(bf16[4,72,256]{2,1,0:T(8,128)(2,1)S(1)} %collective-permute-done.3.refs_1_), channel_id=1, source_target_pairs={{0,1},{1,0},{2,3},{3,2},{4,5},{5,4},{6,7},{7,6},{8,9},{9,8},{10,11... | collective-permute-start | bytes 442376 | tf_op jit(solution)/shard_map/ppermute | solution.py:26
  22.6 3.4 %collective-permute-start.8 = (bf16[4,72,256]{2,1,0:T(8,128)(2,1)S(1)}, bf16[4,72,256]{2,1,0:T(8,128)(2,1)S(1)}, u32[]{:S(2)}, u32[]{:S(2)}) collective-permute-start(bf16[4,72,256]{2,1,0:T(8,128)(2,1)S(1)} %collective-permute-done.4.refs_2_), channel_id=1, source_target_pairs={{0,1},{1,0},{2,3},{3,2},{4,5},{5,4},{6,7},{7,6},{8,9},{9,8},{10,11... | collective-permute-start | bytes 442376 | tf_op jit(solution)/shard_map/ppermute | solution.py:26
  22.6 3.4 %collective-permute-start.9 = (bf16[4,72,256]{2,1,0:T(8,128)(2,1)S(1)}, bf16[4,72,256]{2,1,0:T(8,128)(2,1)S(1)}, u32[]{:S(2)}, u32[]{:S(2)}) collective-permute-start(bf16[4,72,256]{2,1,0:T(8,128)(2,1)S(1)} %collective-permute-done.5.refs_3_), channel_id=1, source_target_pairs={{0,1},{1,0},{2,3},{3,2},{4,5},{5,4},{6,7},{7,6},{8,9},{9,8},{10,11... | collective-permute-start | bytes 442376 | tf_op jit(solution)/shard_map/ppermute | solution.py:26
  25.9 7.2 %copy-start.2 = (f32[4,8]{1,0:T(4,128)S(1)}, f32[4,8]{1,0:T(4,128)}, u32[]{:S(2)}) copy-start(f32[4,8]{1,0:T(4,128)} %param.27) | copy-start | bytes 388
  25.9 7.2 %copy-start.3 = (s32[4,8]{1,0:T(4,128)S(1)}, s32[4,8]{1,0:T(4,128)}, u32[]{:S(2)}) copy-start(s32[4,8]{1,0:T(4,128)} %param.26) | copy-start | bytes 388
  27.9 17.6 %copy-start = (bf16[4,4096]{1,0:T(4,128)(2,1)S(1)}, bf16[4,4096]{1,0:T(4,128)(2,1)}, u32[]{:S(2)}) copy-start(bf16[4,4096]{1,0:T(4,128)(2,1)} %param.23) | copy-start | bytes 98308
  27.9 17.7 %copy-start.1 = (f32[4096]{0:T(1024)S(1)}, f32[4096]{0:T(1024)}, u32[]{:S(2)}) copy-start(f32[4096]{0:T(1024)} %param.25) | copy-start | bytes 49156
  27.9 1.4 %collective-permute-start.11 = (bf16[16,4096]{1,0:T(8,128)(2,1)S(1)}, bf16[16,4096]{1,0:T(8,128)(2,1)S(1)}, u32[]{:S(2)}, u32[]{:S(2)}) collective-permute-start(bf16[16,4096]{1,0:T(8,128)(2,1)S(1)} %get-tuple-element.40), channel_id=1, source_target_pairs={{0,1},{1,0},{2,3},{3,2},{4,5},{5,4},{6,7},{7,6},{8,9},{9,8},{10,11... | collective-permute-start | bytes 393224 | tf_op jit(solution)/shard_map/ppermute | solution.py:26
  28.0 1.5 %collective-permute-start.13 = (bf16[16,4096]{1,0:T(8,128)(2,1)S(1)}, bf16[16,4096]{1,0:T(8,128)(2,1)S(1)}, u32[]{:S(2)}, u32[]{:S(2)}) collective-permute-start(bf16[16,4096]{1,0:T(8,128)(2,1)S(1)} %get-tuple-element.41), channel_id=1, source_target_pairs={{0,1},{1,0},{2,3},{3,2},{4,5},{5,4},{6,7},{7,6},{8,9},{9,8},{10,11... | collective-permute-start | bytes 393224 | tf_op jit(solution)/shard_map/ppermute | solution.py:26
  28.5 2.3 %collective-permute-start.15 = (bf16[16,4096]{1,0:T(8,128)(2,1)S(1)}, bf16[16,4096]{1,0:T(8,128)(2,1)S(1)}, u32[]{:S(2)}, u32[]{:S(2)}) collective-permute-start(bf16[16,4096]{1,0:T(8,128)(2,1)S(1)} %get-tuple-element.42), channel_id=1, source_target_pairs={{0,1},{1,0},{2,3},{3,2},{4,5},{5,4},{6,7},{7,6},{8,9},{9,8},{10,11... | collective-permute-start | bytes 393224 | tf_op jit(solution)/shard_map/ppermute | solution.py:26
  28.6 4.7 %collective-permute-start.10 = (bf16[16,4096]{1,0:T(8,128)(2,1)S(1)}, bf16[16,4096]{1,0:T(8,128)(2,1)S(1)}, u32[]{:S(2)}, u32[]{:S(2)}) collective-permute-start(bf16[16,4096]{1,0:T(8,128)(2,1)S(1)} %get-tuple-element.39), channel_id=1, source_target_pairs={{0,1},{1,0},{2,3},{3,2},{4,5},{5,4},{6,7},{7,6},{8,9},{9,8},{10,11... | collective-permute-start | bytes 393224 | tf_op jit(solution)/shard_map/ppermute | solution.py:26
  29.4 6.4 %collective-permute-start.12 = (bf16[16,4096]{1,0:T(8,128)(2,1)S(1)}, bf16[16,4096]{1,0:T(8,128)(2,1)S(1)}, u32[]{:S(2)}, u32[]{:S(2)}) collective-permute-start(bf16[16,4096]{1,0:T(8,128)(2,1)S(1)} %add.140), channel_id=1, source_target_pairs={{0,2},{1,3},{2,0},{3,1},{4,6},{5,7},{6,4},{7,5},{8,10},{9,11},{10,... | collective-permute-start | bytes 393224 | tf_op jit(solution)/shard_map/ppermute | solution.py:26
  29.6 6.5 %collective-permute-start.14 = (bf16[16,4096]{1,0:T(8,128)(2,1)S(1)}, bf16[16,4096]{1,0:T(8,128)(2,1)S(1)}, u32[]{:S(2)}, u32[]{:S(2)}) collective-permute-start(bf16[16,4096]{1,0:T(8,128)(2,1)S(1)} %add.141), channel_id=1, source_target_pairs={{0,4},{1,5},{2,6},{3,7},{4,0},{5,1},{6,2},{7,3},{8,12},{9,13},{10,... | collective-permute-start | bytes 393224 | tf_op jit(solution)/shard_map/ppermute | solution.py:26
  30.9 7.4 %collective-permute-start.16 = (bf16[16,4096]{1,0:T(8,128)(2,1)S(1)}, bf16[16,4096]{1,0:T(8,128)(2,1)S(1)}, u32[]{:S(2)}, u32[]{:S(2)}) collective-permute-start(bf16[16,4096]{1,0:T(8,128)(2,1)S(1)} %add.142), channel_id=1, source_target_pairs={{0,6},{1,7},{2,4},{3,5},{4,2},{5,3},{6,0},{7,1},{8,14},{9,15},{10,... | collective-permute-start | bytes 393224 | tf_op jit(solution)/shard_map/ppermute | solution.py:26
  38.4 4.5 %collective-permute-start.17 = (bf16[4,4096]{1,0:T(4,128)(2,1)S(1)}, bf16[4,4096]{1,0:T(4,128)(2,1)S(1)}, u32[]{:S(2)}, u32[]{:S(2)}) collective-permute-start(bf16[4,4096]{1,0:T(4,128)(2,1)S(1)} %get-tuple-element.59), channel_id=1, source_target_pairs={{0,8},{1,9},{2,10},{3,11},{4,12},{5,13},{6,14},{7,15},{8,0},{9,1},... | collective-permute-start | bytes 98312 | tf_op jit(solution)/shard_map/ppermute | solution.py:26
  38.5 5.1 %collective-permute-start.18 = (bf16[4,4096]{1,0:T(4,128)(2,1)S(1)}, bf16[4,4096]{1,0:T(4,128)(2,1)S(1)}, u32[]{:S(2)}, u32[]{:S(2)}) collective-permute-start(bf16[4,4096]{1,0:T(4,128)(2,1)S(1)} %get-tuple-element.61), channel_id=1, source_target_pairs={{0,16},{1,17},{2,18},{3,19},{4,20},{5,21},{6,22},{7,23},{8,24},{9,... | collective-permute-start | bytes 98312 | tf_op jit(solution)/shard_map/ppermute | solution.py:26
  39.8 5.7 %collective-permute-start.19 = (bf16[4,4096]{1,0:T(4,128)(2,1)S(1)}, bf16[4,4096]{1,0:T(4,128)(2,1)S(1)}, u32[]{:S(2)}, u32[]{:S(2)}) collective-permute-start(bf16[4,4096]{1,0:T(4,128)(2,1)S(1)} %get-tuple-element.60), channel_id=1, source_target_pairs={{0,24},{1,25},{2,26},{3,27},{4,28},{5,29},{6,30},{7,31},{8,16},{9,... | collective-permute-start | bytes 98312 | tf_op jit(solution)/shard_map/ppermute | solution.py:26
  45.9 4.4 %collective-permute-start.20 = (bf16[4,4224]{1,0:T(4,128)(2,1)S(1)}, bf16[4,4224]{1,0:T(4,128)(2,1)S(1)}, u32[]{:S(2)}, u32[]{:S(2)}) collective-permute-start(bf16[4,4224]{1,0:T(4,128)(2,1)S(1)} %concatenate.6.refs_0_), channel_id=1, source_target_pairs={{0,8},{1,9},{2,10},{3,11},{4,12},{5,13},{6,14},{7,15},{8,0},{9,1},... | collective-permute-start | bytes 101384 | tf_op jit(solution)/shard_map/ppermute | solution.py:26
  45.9 6.4 %collective-permute-start.21 = (bf16[4,4224]{1,0:T(4,128)(2,1)S(1)}, bf16[4,4224]{1,0:T(4,128)(2,1)S(1)}, u32[]{:S(2)}, u32[]{:S(2)}) collective-permute-start(bf16[4,4224]{1,0:T(4,128)(2,1)S(1)} %concatenate.6.refs_0_), channel_id=1, source_target_pairs={{0,16},{1,17},{2,18},{3,19},{4,20},{5,21},{6,22},{7,23},{8,24},{9,... | collective-permute-start | bytes 101384 | tf_op jit(solution)/shard_map/ppermute | solution.py:26
  49.9 5.7 %collective-permute-start.22 = (bf16[4,4224]{1,0:T(4,128)(2,1)S(1)}, bf16[4,4224]{1,0:T(4,128)(2,1)S(1)}, u32[]{:S(2)}, u32[]{:S(2)}) collective-permute-start(bf16[4,4224]{1,0:T(4,128)(2,1)S(1)} %concatenate.6.refs_0_), channel_id=1, source_target_pairs={{0,24},{1,25},{2,26},{3,27},{4,28},{5,29},{6,30},{7,31},{8,16},{9,... | collective-permute-start | bytes 101384 | tf_op jit(solution)/shard_map/ppermute | solution.py:26
  55.6 5.1 %collective-permute-start.23 = (bf16[16,4224]{1,0:T(8,128)(2,1)S(1)}, bf16[16,4224]{1,0:T(8,128)(2,1)S(1)}, u32[]{:S(2)}, u32[]{:S(2)}) collective-permute-start(bf16[16,4224]{1,0:T(8,128)(2,1)S(1)} %join.1.refs_0_), channel_id=1, source_target_pairs={{0,2},{1,3},{2,0},{3,1},{4,6},{5,7},{6,4},{7,5},{8,10},{9,11},{10,... | collective-permute-start | bytes 405512 | tf_op jit(solution)/shard_map/ppermute | solution.py:26
  56.8 5.0 %collective-permute-start.24 = (bf16[16,4224]{1,0:T(8,128)(2,1)S(1)}, bf16[16,4224]{1,0:T(8,128)(2,1)S(1)}, u32[]{:S(2)}, u32[]{:S(2)}) collective-permute-start(bf16[16,4224]{1,0:T(8,128)(2,1)S(1)} %join.1.refs_0_), channel_id=1, source_target_pairs={{0,4},{1,5},{2,6},{3,7},{4,0},{5,1},{6,2},{7,3},{8,12},{9,13},{10,... | collective-permute-start | bytes 405512 | tf_op jit(solution)/shard_map/ppermute | solution.py:26
  57.8 5.9 %collective-permute-start.25 = (bf16[16,4224]{1,0:T(8,128)(2,1)S(1)}, bf16[16,4224]{1,0:T(8,128)(2,1)S(1)}, u32[]{:S(2)}, u32[]{:S(2)}) collective-permute-start(bf16[16,4224]{1,0:T(8,128)(2,1)S(1)} %join.1.refs_0_), channel_id=1, source_target_pairs={{0,6},{1,7},{2,4},{3,5},{4,2},{5,3},{6,0},{7,1},{8,14},{9,15},{10,... | collective-permute-start | bytes 405512 | tf_op jit(solution)/shard_map/ppermute | solution.py:26
  59.2 9.9 %collective-permute-start.26 = (bf16[16,4224]{1,0:T(8,128)(2,1)S(1)}, bf16[16,4224]{1,0:T(8,128)(2,1)S(1)}, u32[]{:S(2)}, u32[]{:S(2)}) collective-permute-start(bf16[16,4224]{1,0:T(8,128)(2,1)S(1)} %join.1.refs_0_), channel_id=1, source_target_pairs={{0,1},{1,0},{2,3},{3,2},{4,5},{5,4},{6,7},{7,6},{8,9},{9,8},{10,11... | collective-permute-start | bytes 405512 | tf_op jit(solution)/shard_map/ppermute | solution.py:26
  60.7 8.4 %collective-permute-start.27 = (bf16[16,4224]{1,0:T(8,128)(2,1)S(1)}, bf16[16,4224]{1,0:T(8,128)(2,1)S(1)}, u32[]{:S(2)}, u32[]{:S(2)}) collective-permute-start(bf16[16,4224]{1,0:T(8,128)(2,1)S(1)} %collective-permute-done.23.refs_1_), channel_id=1, source_target_pairs={{0,1},{1,0},{2,3},{3,2},{4,5},{5,4},{6,7},{7,6},{8,9},{9,8},{10,11... | collective-permute-start | bytes 405512 | tf_op jit(solution)/shard_map/ppermute | solution.py:26
  61.8 7.3 %collective-permute-start.28 = (bf16[16,4224]{1,0:T(8,128)(2,1)S(1)}, bf16[16,4224]{1,0:T(8,128)(2,1)S(1)}, u32[]{:S(2)}, u32[]{:S(2)}) collective-permute-start(bf16[16,4224]{1,0:T(8,128)(2,1)S(1)} %collective-permute-done.24.refs_2_), channel_id=1, source_target_pairs={{0,1},{1,0},{2,3},{3,2},{4,5},{5,4},{6,7},{7,6},{8,9},{9,8},{10,11... | collective-permute-start | bytes 405512 | tf_op jit(solution)/shard_map/ppermute | solution.py:26
  63.7 5.4 %collective-permute-start.29 = (bf16[16,4224]{1,0:T(8,128)(2,1)S(1)}, bf16[16,4224]{1,0:T(8,128)(2,1)S(1)}, u32[]{:S(2)}, u32[]{:S(2)}) collective-permute-start(bf16[16,4224]{1,0:T(8,128)(2,1)S(1)} %collective-permute-done.25.refs_3_), channel_id=1, source_target_pairs={{0,1},{1,0},{2,3},{3,2},{4,5},{5,4},{6,7},{7,6},{8,9},{9,8},{10,11... | collective-permute-start | bytes 405512 | tf_op jit(solution)/shard_map/ppermute | solution.py:26
  71.4 1.6 %collective-permute-start.31 = (bf16[16,4096]{1,0:T(8,128)(2,1)S(1)}, bf16[16,4096]{1,0:T(8,128)(2,1)S(1)}, u32[]{:S(2)}, u32[]{:S(2)}) collective-permute-start(bf16[16,4096]{1,0:T(8,128)(2,1)S(1)} %get-tuple-element.47), channel_id=1, source_target_pairs={{0,1},{1,0},{2,3},{3,2},{4,5},{5,4},{6,7},{7,6},{8,9},{9,8},{10,11... | collective-permute-start | bytes 393224 | tf_op jit(solution)/shard_map/ppermute | solution.py:26
  72.0 2.0 %collective-permute-start.33 = (bf16[16,4096]{1,0:T(8,128)(2,1)S(1)}, bf16[16,4096]{1,0:T(8,128)(2,1)S(1)}, u32[]{:S(2)}, u32[]{:S(2)}) collective-permute-start(bf16[16,4096]{1,0:T(8,128)(2,1)S(1)} %get-tuple-element.48), channel_id=1, source_target_pairs={{0,1},{1,0},{2,3},{3,2},{4,5},{5,4},{6,7},{7,6},{8,9},{9,8},{10,11... | collective-permute-start | bytes 393224 | tf_op jit(solution)/shard_map/ppermute | solution.py:26
  72.0 3.0 %collective-permute-start.35 = (bf16[16,4096]{1,0:T(8,128)(2,1)S(1)}, bf16[16,4096]{1,0:T(8,128)(2,1)S(1)}, u32[]{:S(2)}, u32[]{:S(2)}) collective-permute-start(bf16[16,4096]{1,0:T(8,128)(2,1)S(1)} %get-tuple-element.49), channel_id=1, source_target_pairs={{0,1},{1,0},{2,3},{3,2},{4,5},{5,4},{6,7},{7,6},{8,9},{9,8},{10,11... | collective-permute-start | bytes 393224 | tf_op jit(solution)/shard_map/ppermute | solution.py:26
  72.5 4.3 %collective-permute-start.30 = (bf16[16,4096]{1,0:T(8,128)(2,1)S(1)}, bf16[16,4096]{1,0:T(8,128)(2,1)S(1)}, u32[]{:S(2)}, u32[]{:S(2)}) collective-permute-start(bf16[16,4096]{1,0:T(8,128)(2,1)S(1)} %get-tuple-element.46), channel_id=1, source_target_pairs={{0,1},{1,0},{2,3},{3,2},{4,5},{5,4},{6,7},{7,6},{8,9},{9,8},{10,11... | collective-permute-start | bytes 393224 | tf_op jit(solution)/shard_map/ppermute | solution.py:26
  73.0 6.4 %collective-permute-start.32 = (bf16[16,4096]{1,0:T(8,128)(2,1)S(1)}, bf16[16,4096]{1,0:T(8,128)(2,1)S(1)}, u32[]{:S(2)}, u32[]{:S(2)}) collective-permute-start(bf16[16,4096]{1,0:T(8,128)(2,1)S(1)} %add.143), channel_id=1, source_target_pairs={{0,2},{1,3},{2,0},{3,1},{4,6},{5,7},{6,4},{7,5},{8,10},{9,11},{10,... | collective-permute-start | bytes 393224 | tf_op jit(solution)/shard_map/ppermute | solution.py:26
  74.0 8.4 %collective-permute-start.34 = (bf16[16,4096]{1,0:T(8,128)(2,1)S(1)}, bf16[16,4096]{1,0:T(8,128)(2,1)S(1)}, u32[]{:S(2)}, u32[]{:S(2)}) collective-permute-start(bf16[16,4096]{1,0:T(8,128)(2,1)S(1)} %add.144), channel_id=1, source_target_pairs={{0,4},{1,5},{2,6},{3,7},{4,0},{5,1},{6,2},{7,3},{8,12},{9,13},{10,... | collective-permute-start | bytes 393224 | tf_op jit(solution)/shard_map/ppermute | solution.py:26
  75.1 7.2 %collective-permute-start.36 = (bf16[16,4096]{1,0:T(8,128)(2,1)S(1)}, bf16[16,4096]{1,0:T(8,128)(2,1)S(1)}, u32[]{:S(2)}, u32[]{:S(2)}) collective-permute-start(bf16[16,4096]{1,0:T(8,128)(2,1)S(1)} %add.145), channel_id=1, source_target_pairs={{0,6},{1,7},{2,4},{3,5},{4,2},{5,3},{6,0},{7,1},{8,14},{9,15},{10,... | collective-permute-start | bytes 393224 | tf_op jit(solution)/shard_map/ppermute | solution.py:26
  82.5 4.5 %collective-permute-start.37 = (bf16[4,4096]{1,0:T(4,128)(2,1)S(1)}, bf16[4,4096]{1,0:T(4,128)(2,1)S(1)}, u32[]{:S(2)}, u32[]{:S(2)}) collective-permute-start(bf16[4,4096]{1,0:T(4,128)(2,1)S(1)} %get-tuple-element.56), channel_id=1, source_target_pairs={{0,8},{1,9},{2,10},{3,11},{4,12},{5,13},{6,14},{7,15},{8,0},{9,1},... | collective-permute-start | bytes 98312 | tf_op jit(solution)/shard_map/ppermute | solution.py:26
  82.6 5.1 %collective-permute-start.38 = (bf16[4,4096]{1,0:T(4,128)(2,1)S(1)}, bf16[4,4096]{1,0:T(4,128)(2,1)S(1)}, u32[]{:S(2)}, u32[]{:S(2)}) collective-permute-start(bf16[4,4096]{1,0:T(4,128)(2,1)S(1)} %get-tuple-element.58), channel_id=1, source_target_pairs={{0,16},{1,17},{2,18},{3,19},{4,20},{5,21},{6,22},{7,23},{8,24},{9,... | collective-permute-start | bytes 98312 | tf_op jit(solution)/shard_map/ppermute | solution.py:26
  83.7 5.7 %collective-permute-start.39 = (bf16[4,4096]{1,0:T(4,128)(2,1)S(1)}, bf16[4,4096]{1,0:T(4,128)(2,1)S(1)}, u32[]{:S(2)}, u32[]{:S(2)}) collective-permute-start(bf16[4,4096]{1,0:T(4,128)(2,1)S(1)} %get-tuple-element.57), channel_id=1, source_target_pairs={{0,24},{1,25},{2,26},{3,27},{4,28},{5,29},{6,30},{7,31},{8,16},{9,... | collective-permute-start | bytes 98312 | tf_op jit(solution)/shard_map/ppermute | solution.py:26

commit v5 on v4

--- a/solution.py
+++ b/solution.py
@@ -55,19 +55,23 @@
     def head_of(target):
         return (target * feature) // HD
 
-    for zx, out in enumerate(outs):
+    def fill(out, zx, middle, own):
         group = head_of(device ^ (zx * LOW * MID)) // per_group
         lanes = pl.ds(pl.multiple_of(group * HD, HD), HD)
         out[0:kv_rows, 0:HD] = keys[:, :, lanes].reshape(kv_rows, HD)
         out[0:kv_rows, HD : 2 * HD] = values[:, :, lanes].reshape(kv_rows, HD)
-        for mx in range(MID):
-            top = kv_rows + mx * rows
+        for i, mx in enumerate(middle):
+            top = kv_rows + i * rows
             for cx in range(LOW):
                 head = head_of(device ^ (zx * LOW * MID + mx * LOW + cx))
                 out[top : top + rows, cx * HD : (cx + 1) * HD] = q[:, pl.ds(pl.multiple_of(head * HD, HD), HD)]
-        top = kv_rows + MID * rows
-        out[top : top + rows, 0:HD] = own_key[:, lanes]
-        out[top : top + rows, HD : 2 * HD] = own_value[:, lanes]
+        out[own : own + rows, 0:HD] = own_key[:, lanes]
+        out[own : own + rows, HD : 2 * HD] = own_value[:, lanes]
+
+    for mx in range(MID):
+        fill(outs[mx], 0, [mx], kv_rows + rows)
+    for zx, out in enumerate(outs[MID:], 1):
+        fill(out, zx, range(MID), kv_rows + MID * rows)
 
 
 def repack_body(*refs, kv_rows, rows):
@@ -83,11 +87,11 @@
 
 
 def attend_body(prefix_of, lengths, *refs, ctx_local, kv_rows, rows):
-    mine, other = refs[:MID], refs[MID : 2 * MID]
-    w_out, keep = refs[2 * MID : 2 * MID + 2]
-    sends, att = refs[2 * MID + 2 : -1], refs[-1]
+    mine, other = (list(zip(part[:MID], part[MID:])) for part in (refs[: 2 * MID], refs[2 * MID : 4 * MID]))
+    w_out, keep = refs[4 * MID : 4 * MID + 2]
+    sends, att = refs[4 * MID + 2 : -1], refs[-1]
     device = lax.axis_index("ctx")
-    high = mine[0].shape[0]
+    high = mine[0][1].shape[0] + 1
     pieces = MID * high
     span = CAND // (LOW * MID * rows)
     scale = 1.0 / math.sqrt(HD)
@@ -103,8 +107,16 @@
     relative = (piece % high) * (LOW * MID) + (piece // high) * LOW
     own_group = device // (LOW * MID * span)
 
-    def joined(parts, zs, at, lanes, depth):
-        return jnp.concatenate([part[zs, at, lanes].reshape(depth, -1) for part in parts], axis=0)
+    def joined(parts, zs, at, lanes):
+        taken = []
+        for near, rest in parts:
+            first, last = zs.start, zs.stop
+            if first == 0:
+                taken.append(near[at, lanes])
+                first = 1
+            block = rest[first - 1 : last - 1, at, lanes]
+            taken.append(block.reshape(-1, block.shape[-1]))
+        return jnp.concatenate(taken, axis=0)
 
     for zg in range(high // span):
         prefix = prefix_of[(own_group ^ zg) * CAND]
@@ -113,8 +125,8 @@
         tails = slice(kv_rows, kv_rows + tile)
         at = pl.ds(pl.multiple_of(prefix * ctx_local, ctx_local), ctx_local)
         every = slice(0, high)
-        tail_mine = joined(mine, zs, tails, slice(0, 2 * HD), span * tile)
-        tail_other = joined(other, zs, tails, slice(0, 2 * HD), span * tile)
+        tail_mine = joined(mine, zs, tails, slice(0, 2 * HD))
+        tail_other = joined(other, zs, tails, slice(0, 2 * HD))
         padded = jnp.concatenate([tail_mine[:, 0:HD], tail_other[:, HD : 2 * HD]], axis=0)
         query = jnp.dot(pick_query, padded, preferred_element_type=jnp.float32)
         own = jnp.dot(
@@ -125,7 +137,7 @@
         top = own_score
         all_scores = []
         for cx, source in enumerate((mine, other)):
-            key = joined(source, every, at, slice(0, HD), high * ctx_local)
+            key = joined(source, every, at, slice(0, HD))
             scores = (
                 lax.dot_general(query, key, (((1,), (1,)), ((), ())), preferred_element_type=jnp.float32) * scale
             )
@@ -137,7 +149,7 @@
         numer = own_weight * own[:, HD : 2 * HD]
         denom = own_weight
         for scores, source in zip(all_scores, (mine, other)):
-            value = joined(source, every, at, slice(HD, 2 * HD), high * ctx_local)
+            value = joined(source, every, at, slice(HD, 2 * HD))
             weights = jnp.exp(scores - top)
             denom = denom + jnp.sum(weights, axis=1, keepdims=True)
             numer = numer + jnp.dot(weights.astype(jnp.bfloat16), value, preferred_element_type=jnp.float32)
@@ -331,28 +343,32 @@
 
     inputs = (queries, own_key, own_value, cache_keys, cache_values)
     message = jax.ShapeDtypeStruct((kv_rows + MID * rows + 2 * rows, 2 * HD), jnp.bfloat16)
+    near = jax.ShapeDtypeStruct((kv_rows + 2 * rows, 2 * HD), jnp.bfloat16)
+    count = MID + len(high) - 1
     steps = len(inputs) + len(tables)
     packed = pl.pallas_call(
-        functools.partial(pack_body, feature=feature, per_group=per_group, count=len(high), tables=len(tables)),
+        functools.partial(pack_body, feature=feature, per_group=per_group, count=count, tables=len(tables)),
         in_specs=[HBM] * steps,
-        out_specs=[VMEM] * (len(high) + len(tables)),
-        out_shape=[message] * len(high) + [jax.ShapeDtypeStruct(a.shape, a.dtype) for a in tables],
+        out_specs=[VMEM] * (count + len(tables)),
+        out_shape=[near] * MID + [message] * (len(high) - 1) + [jax.ShapeDtypeStruct(a.shape, a.dtype) for a in tables],
         scratch_shapes=[pltpu.VMEM(a.shape, a.dtype) for a in inputs] + [pltpu.SemaphoreType.DMA((steps,))],
         compiler_params=pltpu.CompilerParams(vmem_limit_bytes=SMALL_VMEM),
         name="pack",
     )(*(in_hbm(item) for item in inputs + tables))
-    messages, (prefix_of, lengths, gate_scales, low_scales) = packed[: len(high)], packed[len(high) :]
-    got = [messages[0]] + [swapped(messages[i], high[i]) for i in range(1, len(high))]
-    piece = jax.ShapeDtypeStruct((len(high), kv_rows + 2 * rows, 2 * HD), jnp.bfloat16)
+    prefix_of, lengths, gate_scales, low_scales = packed[count:]
+    got = [swapped(item, offset) for item, offset in zip(packed[MID:count], high[1:])]
+    mine_near = [packed[0]] + [swapped(packed[i], mid[i]) for i in range(1, MID)]
+    piece = jax.ShapeDtypeStruct((len(high) - 1, kv_rows + 2 * rows, 2 * HD), jnp.bfloat16)
     messages = pl.pallas_call(
         functools.partial(repack_body, kv_rows=kv_rows, rows=rows),
-        in_specs=[VMEM] * len(high),
+        in_specs=[VMEM] * len(got),
         out_specs=[VMEM] * MID,
         out_shape=[piece] * MID,
         compiler_params=pltpu.CompilerParams(vmem_limit_bytes=2 * SMALL_VMEM),
         name="repack",
     )(*got)
     mine = [messages[0]] + [swapped(messages[i], mid[i]) for i in range(1, MID)]
+    other_near = [swapped(item, low[1]) for item in mine_near]
     other = [swapped(item, low[1]) for item in mine]
 
     if feature < HD:
@@ -367,10 +383,10 @@
     (down,) = prepared(low_scales, False, [(down_codes[0], 0, down_codes.shape[1])])
     (gate_rest,) = prepared(gate_scales, True, [(codes, first, codes.shape[0] - first)])
     half = shards * rows // 2
-    attend_vmem = 8 * 2**20 + 2 * MID * piece.size * 2 + w_full.size * 2 + half * width * 10
+    attend_vmem = 8 * 2**20 + 2 * MID * (piece.size + near.size) * 2 + w_full.size * 2 + half * width * 10
     keep, *sends = pl.pallas_call(
         functools.partial(attend_body, ctx_local=ctx_local, kv_rows=kv_rows, rows=rows),
-        in_specs=[SMEM] * 2 + [VMEM] * (2 * MID + 1),
+        in_specs=[SMEM] * 2 + [VMEM] * (4 * MID + 1),
         out_specs=[VMEM] * (1 + MID),
         out_shape=[
             jax.ShapeDtypeStruct((half, width), jnp.float32),
@@ -381,7 +397,7 @@
         ],
         compiler_params=pltpu.CompilerParams(vmem_limit_bytes=attend_vmem),
         name="attend",
-    )(prefix_of, lengths, *mine, *other, w_full)
+    )(prefix_of, lengths, *mine_near, *mine, *other_near, *other, w_full)
 
     projected = scatter_sum(keep, sends, mid, high)
     mixed = hidden_in.astype(jnp.float32) + projected

time: 90.3 us -> 96.8 us (1.072)
  starting transfers between devices: 36.2 us -> 42.3 us
    ppermute x40 -> x47, starting transfers between devices: 36.2 us -> 42.3 us  [swapped(): lax.ppermute(value, 'ctx', [(i, i ^ offset) for i in range(lax.axis_size(...]
    ppermute x40 -> x47, waiting for transfers between devices: 37.8 us -> 38.2 us  [swapped(): lax.ppermute(value, 'ctx', [(i, i ^ offset) for i in range(lax.axis_size(...]
  transfers between devices with their start and end apart: 40 -> 47, of which waited for: 20 -> 22; matrix products, arithmetic and copies ran while one was open for 0% -> 0% of each run, Pallas kernels for 9% -> 9%
where the time goes in v5:
time: 96.8 us; the launch traced here: 96.5 us
  starting transfers between devices  42.3 us (44%)
  waiting for transfers between devices  38.2 us (39%)
  Pallas kernels  13.7 us (14%)
  other arithmetic  1.19 us (1%)
    ppermute x47, starting transfers between devices, swapped(): lax.ppermute(value, 'ctx', [(i, i ^ offset) for i in range(lax.axis_size(...  42.3 us
    ppermute x47, waiting for transfers between devices, swapped(): lax.ppermute(value, 'ctx', [(i, i ^ offset) for i in range(lax.axis_size(...  38.2 us
    pallas_call x3, Pallas kernels, prepared(): pl.pallas_call(functools.partial(prepare_body, ranges=ranges, fetched=len...  8.18 us
    pallas_call x1, Pallas kernels, local(): pl.pallas_call(functools.partial(expert_body, width=width, experts=expert...  2.21 us
    pallas_call x1, Pallas kernels, local(): pl.pallas_call(functools.partial(attend_body, ctx_local=ctx_local, kv_row...  1.94 us
  transfers between devices with their start and end apart: 47, of which 22 were waited for; matrix products, arithmetic and copies ran while one was open for 0% of the time, Pallas kernels for 9%

profile of v5, /device:TPU:0, one launch (start us, length us, event | category | flops | bytes accessed | tf_op | source)
XLA Modules:
  0.0 96.5 jit_solution(6823451280042277641)
XLA Ops:
  0.6 1.1 %pack.1 = (bf16[72,256]{1,0:T(8,128)(2,1)S(1)}, bf16[72,256]{1,0:T(8,128)(2,1)S(1)}, bf16[72,256]{1,0:T(8,128)(2,1)S(1)}, bf16[72,256]{1,0:T(8,128)(2,1)S(1)}, b...) custom-call(bf16[4,4096]{1,0:T(4,128)(2,1)} %refs_0_.1, ...), custom_call_target="tpu_custom_call" | custom-call | tf_op jit(solution)/shard_map/pack/pallas_call | solution.py:349
  1.8 3.1 %collective-permute-start.3 = (bf16[88,256]{1,0:T(8,128)(2,1)S(1)}, bf16[88,256]{1,0:T(8,128)(2,1)S(1)}, u32[]{:S(2)}, u32[]{:S(2)}) collective-permute-start(bf16[88,256]{1,0:T(8,128)(2,1)S(1)} %get-tuple-element.35), channel_id=1, source_target_pairs={{0,8},{1,9},{2,10},{3,11},{4,12},{5,13},{6,14},{7,15},{8,0},{9,1},... | collective-permute-start | bytes 135176 | tf_op jit(solution)/shard_map/ppermute | solution.py:26
  4.9 2.6 %collective-permute-start.4 = (bf16[88,256]{1,0:T(8,128)(2,1)S(1)}, bf16[88,256]{1,0:T(8,128)(2,1)S(1)}, u32[]{:S(2)}, u32[]{:S(2)}) collective-permute-start(bf16[88,256]{1,0:T(8,128)(2,1)S(1)} %get-tuple-element.36), channel_id=1, source_target_pairs={{0,16},{1,17},{2,18},{3,19},{4,20},{5,21},{6,22},{7,23},{8,24},{9,... | collective-permute-start | bytes 135176 | tf_op jit(solution)/shard_map/ppermute | solution.py:26
  7.5 3.2 %collective-permute-done.4.refs_1_ = bf16[88,256]{1,0:T(8,128)(2,1)S(1)} collective-permute-done((bf16[88,256]{1,0:T(8,128)(2,1)S(1)}, bf16[88,256]{1,0:T(8,128)(2,1)S(1)}, u32[]{:S(2)}, u32[]{:S(2)}) %collective-permute-start.4) | collective-permute-done | bytes 45088 | tf_op jit(solution)/shard_map/ppermute | solution.py:26
  10.7 2.6 %collective-permute-done.5.refs_2_ = bf16[88,256]{1,0:T(8,128)(2,1)S(1)} collective-permute-done((bf16[88,256]{1,0:T(8,128)(2,1)S(1)}, bf16[88,256]{1,0:T(8,128)(2,1)S(1)}, u32[]{:S(2)}, u32[]{:S(2)}) %collective-permute-start.5) | collective-permute-done | bytes 45088 | tf_op jit(solution)/shard_map/ppermute | solution.py:26
  13.4 1.6 %collective-permute-start.6 = (bf16[3,72,256]{2,1,0:T(8,128)(2,1)S(1)}, bf16[3,72,256]{2,1,0:T(8,128)(2,1)S(1)}, u32[]{:S(2)}, u32[]{:S(2)}) collective-permute-start(bf16[3,72,256]{2,1,0:T(8,128)(2,1)S(1)} %get-tuple-element.39), channel_id=1, source_target_pairs={{0,2},{1,3},{2,0},{3,1},{4,6},{5,7},{6,4},{7,5},{8,10},{9,11},{10,... | collective-permute-start | bytes 331784 | tf_op jit(solution)/shard_map/ppermute | solution.py:26
  14.9 1.5 %collective-permute-start.7 = (bf16[3,72,256]{2,1,0:T(8,128)(2,1)S(1)}, bf16[3,72,256]{2,1,0:T(8,128)(2,1)S(1)}, u32[]{:S(2)}, u32[]{:S(2)}) collective-permute-start(bf16[3,72,256]{2,1,0:T(8,128)(2,1)S(1)} %get-tuple-element.40), channel_id=1, source_target_pairs={{0,4},{1,5},{2,6},{3,7},{4,0},{5,1},{6,2},{7,3},{8,12},{9,13},{10,... | collective-permute-start | bytes 331784 | tf_op jit(solution)/shard_map/ppermute | solution.py:26
  16.4 0.5 collective-permute-start.8
  16.9 1.5 %collective-permute-start = (bf16[72,256]{1,0:T(8,128)(2,1)S(1)}, bf16[72,256]{1,0:T(8,128)(2,1)S(1)}, u32[]{:S(2)}, u32[]{:S(2)}) collective-permute-start(bf16[72,256]{1,0:T(8,128)(2,1)S(1)} %get-tuple-element.32), channel_id=1, source_target_pairs={{0,2},{1,3},{2,0},{3,1},{4,6},{5,7},{6,4},{7,5},{8,10},{9,11},{10,... | collective-permute-start | bytes 110600 | tf_op jit(solution)/shard_map/ppermute | solution.py:26
  18.4 1.5 %collective-permute-start.1 = (bf16[72,256]{1,0:T(8,128)(2,1)S(1)}, bf16[72,256]{1,0:T(8,128)(2,1)S(1)}, u32[]{:S(2)}, u32[]{:S(2)}) collective-permute-start(bf16[72,256]{1,0:T(8,128)(2,1)S(1)} %get-tuple-element.33), channel_id=1, source_target_pairs={{0,4},{1,5},{2,6},{3,7},{4,0},{5,1},{6,2},{7,3},{8,12},{9,13},{10,... | collective-permute-start | bytes 110600 | tf_op jit(solution)/shard_map/ppermute | solution.py:26
  19.9 1.6 %collective-permute-done.refs_1_ = bf16[72,256]{1,0:T(8,128)(2,1)S(1)} collective-permute-done((bf16[72,256]{1,0:T(8,128)(2,1)S(1)}, bf16[72,256]{1,0:T(8,128)(2,1)S(1)}, u32[]{:S(2)}, u32[]{:S(2)}) %collective-permute-start) | collective-permute-done | bytes 36896 | tf_op jit(solution)/shard_map/ppermute | solution.py:26
  21.5 1.8 %collective-permute-start.2 = (bf16[72,256]{1,0:T(8,128)(2,1)S(1)}, bf16[72,256]{1,0:T(8,128)(2,1)S(1)}, u32[]{:S(2)}, u32[]{:S(2)}) collective-permute-start(bf16[72,256]{1,0:T(8,128)(2,1)S(1)} %get-tuple-element.34), channel_id=1, source_target_pairs={{0,6},{1,7},{2,4},{3,5},{4,2},{5,3},{6,0},{7,1},{8,14},{9,15},{10,... | collective-permute-start | bytes 110600 | tf_op jit(solution)/shard_map/ppermute | solution.py:26
  23.3 3.1 %collective-permute-done.2.refs_3_ = bf16[72,256]{1,0:T(8,128)(2,1)S(1)} collective-permute-done((bf16[72,256]{1,0:T(8,128)(2,1)S(1)}, bf16[72,256]{1,0:T(8,128)(2,1)S(1)}, u32[]{:S(2)}, u32[]{:S(2)}) %collective-permute-start.2) | collective-permute-done | bytes 36896 | tf_op jit(solution)/shard_map/ppermute | solution.py:26
  26.4 0.5 collective-permute-start.13
  27.0 0.4 collective-permute-start.15
  27.5 0.1 collective-permute-done.10.refs_9_
  27.6 0.3 collective-permute-start.11
  27.9 0.9 collective-permute-done.11.refs_10_
  28.8 0.3 collective-permute-start.12
  29.1 2.8 %prepare.3 = (bf16[2048,768]{1,0:T(8,128)(2,1)S(1)}, bf16[128,4096]{1,0:T(8,128)(2,1)S(1)}) custom-call(f32[6,1,32]{2,1,0:T(1,128)S(1)} %get-tuple-element.42.refs_0_, bf16[4096,768]{1,0:T(8,128)(2,1)} %bitcast.4, bf16[128,4096]{1,0:T(8,128)(2,1)} %refs_2_.3), custom_call_target="tpu_custom_call" | custom-call | tf_op jit(solution)/shard_map/prepare/pallas_call | solution.py:218
  32.0 1.9 %attend.1 = (f32[64,4096]{1,0:T(8,128)S(1)}, bf16[16,4096]{1,0:T(8,128)(2,1)S(1)}, bf16[16,4096]{1,0:T(8,128)(2,1)S(1)}, bf16[16,4096]{1,0:T(8,128)(2,1)S(1)}, bf16[16,4096]{1,0:T(8,128)(2,1)S(1)}) custom-call(s32[128]{0:T(128)S(1)} %get-tuple-element.29.prefix_of, s32[2]{0:T(128)S(1)} %get-tuple-element.30.lengths, ...), custom_call_target="tpu_custom_call" | custom-call | tf_op jit(solution)/shard_map/attend/pallas_call | solution.py:387
  34.0 0.2 collective-permute-start.18
  34.2 0.3 collective-permute-start.20
  34.6 0.2 collective-permute-start.22
  34.8 0.3 collective-permute-start.17
  35.1 0.3 collective-permute-done.18.got
  35.5 0.9 collective-permute-start.19
  36.4 1.6 %collective-permute-start.21 = (bf16[16,4096]{1,0:T(8,128)(2,1)S(1)}, bf16[16,4096]{1,0:T(8,128)(2,1)S(1)}, u32[]{:S(2)}, u32[]{:S(2)}) collective-permute-start(bf16[16,4096]{1,0:T(8,128)(2,1)S(1)} %add.141), channel_id=1, source_target_pairs={{0,4},{1,5},{2,6},{3,7},{4,0},{5,1},{6,2},{7,3},{8,12},{9,13},{10,... | collective-permute-start | bytes 393224 | tf_op jit(solution)/shard_map/ppermute | solution.py:26
  38.0 1.2 %collective-permute-start.23 = (bf16[16,4096]{1,0:T(8,128)(2,1)S(1)}, bf16[16,4096]{1,0:T(8,128)(2,1)S(1)}, u32[]{:S(2)}, u32[]{:S(2)}) collective-permute-start(bf16[16,4096]{1,0:T(8,128)(2,1)S(1)} %add.142), channel_id=1, source_target_pairs={{0,6},{1,7},{2,4},{3,5},{4,2},{5,3},{6,0},{7,1},{8,14},{9,15},{10,... | collective-permute-start | bytes 393224 | tf_op jit(solution)/shard_map/ppermute | solution.py:26
  39.3 2.6 %collective-permute-done.19 = bf16[16,4096]{1,0:T(8,128)(2,1)S(1)} collective-permute-done((bf16[16,4096]{1,0:T(8,128)(2,1)S(1)}, bf16[16,4096]{1,0:T(8,128)(2,1)S(1)}, u32[]{:S(2)}, u32[]{:S(2)}) %collective-permute-start.19) | collective-permute-done | bytes 131104 | tf_op jit(solution)/shard_map/ppermute | solution.py:26
  41.9 1.7 %collective-permute-done.21 = bf16[16,4096]{1,0:T(8,128)(2,1)S(1)} collective-permute-done((bf16[16,4096]{1,0:T(8,128)(2,1)S(1)}, bf16[16,4096]{1,0:T(8,128)(2,1)S(1)}, u32[]{:S(2)}, u32[]{:S(2)}) %collective-permute-start.21) | collective-permute-done | bytes 131104 | tf_op jit(solution)/shard_map/ppermute | solution.py:26
  43.6 1.3 %collective-permute-done.23 = bf16[16,4096]{1,0:T(8,128)(2,1)S(1)} collective-permute-done((bf16[16,4096]{1,0:T(8,128)(2,1)S(1)}, bf16[16,4096]{1,0:T(8,128)(2,1)S(1)}, u32[]{:S(2)}, u32[]{:S(2)}) %collective-permute-start.23) | collective-permute-done | bytes 131104 | tf_op jit(solution)/shard_map/ppermute | solution.py:26
  45.1 1.1 %collective-permute-start.25 = (bf16[4,4096]{1,0:T(4,128)(2,1)S(1)}, bf16[4,4096]{1,0:T(4,128)(2,1)S(1)}, u32[]{:S(2)}, u32[]{:S(2)}) collective-permute-start(bf16[4,4096]{1,0:T(4,128)(2,1)S(1)} %get-tuple-element.67), channel_id=1, source_target_pairs={{0,16},{1,17},{2,18},{3,19},{4,20},{5,21},{6,22},{7,23},{8,24},{9,... | collective-permute-start | bytes 98312 | tf_op jit(solution)/shard_map/ppermute | solution.py:26
  46.2 3.3 %collective-permute-start.26 = (bf16[4,4096]{1,0:T(4,128)(2,1)S(1)}, bf16[4,4096]{1,0:T(4,128)(2,1)S(1)}, u32[]{:S(2)}, u32[]{:S(2)}) collective-permute-start(bf16[4,4096]{1,0:T(4,128)(2,1)S(1)} %get-tuple-element.66), channel_id=1, source_target_pairs={{0,24},{1,25},{2,26},{3,27},{4,28},{5,29},{6,30},{7,31},{8,16},{9,... | collective-permute-start | bytes 98312 | tf_op jit(solution)/shard_map/ppermute | solution.py:26
  49.5 0.6 collective-permute-done.25
  50.1 1.7 %collective-permute-done.26 = bf16[4,4096]{1,0:T(4,128)(2,1)S(1)} collective-permute-done((bf16[4,4096]{1,0:T(4,128)(2,1)S(1)}, bf16[4,4096]{1,0:T(4,128)(2,1)S(1)}, u32[]{:S(2)}, u32[]{:S(2)}) %collective-permute-start.26) | collective-permute-done | bytes 32800 | tf_op jit(solution)/shard_map/ppermute | solution.py:26
  51.9 0.2 multiply_reduce_fusion
  52.2 0.1 concatenate.6.refs_0_
  52.3 4.0 %collective-permute-start.28 = (bf16[4,4224]{1,0:T(4,128)(2,1)S(1)}, bf16[4,4224]{1,0:T(4,128)(2,1)S(1)}, u32[]{:S(2)}, u32[]{:S(2)}) collective-permute-start(bf16[4,4224]{1,0:T(4,128)(2,1)S(1)} %concatenate.6.refs_0_), channel_id=1, source_target_pairs={{0,16},{1,17},{2,18},{3,19},{4,20},{5,21},{6,22},{7,23},{8,24},{9,... | collective-permute-start | bytes 101384 | tf_op jit(solution)/shard_map/ppermute | solution.py:26
  56.4 0.3 collective-permute-start.29
  56.7 2.1 %collective-permute-done.28.refs_2_ = bf16[4,4224]{1,0:T(4,128)(2,1)S(1)} collective-permute-done((bf16[4,4224]{1,0:T(4,128)(2,1)S(1)}, bf16[4,4224]{1,0:T(4,128)(2,1)S(1)}, u32[]{:S(2)}, u32[]{:S(2)}) %collective-permute-start.28) | collective-permute-done | bytes 33824 | tf_op jit(solution)/shard_map/ppermute | solution.py:26
  58.8 3.3 %collective-permute-done.29.refs_3_ = bf16[4,4224]{1,0:T(4,128)(2,1)S(1)} collective-permute-done((bf16[4,4224]{1,0:T(4,128)(2,1)S(1)}, bf16[4,4224]{1,0:T(4,128)(2,1)S(1)}, u32[]{:S(2)}, u32[]{:S(2)}) %collective-permute-start.29) | collective-permute-done | bytes 33824 | tf_op jit(solution)/shard_map/ppermute | solution.py:26
  62.1 0.8 collective-permute-start.30
  63.0 1.4 %collective-permute-start.31 = (bf16[16,4224]{1,0:T(8,128)(2,1)S(1)}, bf16[16,4224]{1,0:T(8,128)(2,1)S(1)}, u32[]{:S(2)}, u32[]{:S(2)}) collective-permute-start(bf16[16,4224]{1,0:T(8,128)(2,1)S(1)} %join.1.refs_0_), channel_id=1, source_target_pairs={{0,4},{1,5},{2,6},{3,7},{4,0},{5,1},{6,2},{7,3},{8,12},{9,13},{10,... | collective-permute-start | bytes 405512 | tf_op jit(solution)/shard_map/ppermute | solution.py:26
  64.4 1.3 %collective-permute-start.32 = (bf16[16,4224]{1,0:T(8,128)(2,1)S(1)}, bf16[16,4224]{1,0:T(8,128)(2,1)S(1)}, u32[]{:S(2)}, u32[]{:S(2)}) collective-permute-start(bf16[16,4224]{1,0:T(8,128)(2,1)S(1)} %join.1.refs_0_), channel_id=1, source_target_pairs={{0,6},{1,7},{2,4},{3,5},{4,2},{5,3},{6,0},{7,1},{8,14},{9,15},{10,... | collective-permute-start | bytes 405512 | tf_op jit(solution)/shard_map/ppermute | solution.py:26
  65.7 1.5 %collective-permute-done.30.refs_1_ = bf16[16,4224]{1,0:T(8,128)(2,1)S(1)} collective-permute-done((bf16[16,4224]{1,0:T(8,128)(2,1)S(1)}, bf16[16,4224]{1,0:T(8,128)(2,1)S(1)}, u32[]{:S(2)}, u32[]{:S(2)}) %collective-permute-start.30) | collective-permute-done | bytes 135200 | tf_op jit(solution)/shard_map/ppermute | solution.py:26
  67.2 0.8 collective-permute-done.31.refs_2_
  68.0 2.3 %collective-permute-done.32.refs_3_ = bf16[16,4224]{1,0:T(8,128)(2,1)S(1)} collective-permute-done((bf16[16,4224]{1,0:T(8,128)(2,1)S(1)}, bf16[16,4224]{1,0:T(8,128)(2,1)S(1)}, u32[]{:S(2)}, u32[]{:S(2)}) %collective-permute-start.32) | collective-permute-done | bytes 135200 | tf_op jit(solution)/shard_map/ppermute | solution.py:26
  70.3 2.6 %prepare.4.refs_9_ = bf16[2048,768]{1,0:T(8,128)(2,1)S(1)} custom-call(f32[6,1,32]{2,1,0:T(1,128)S(1)} %get-tuple-element.42.refs_0_, bf16[4096,768]{1,0:T(8,128)(2,1)} %bitcast.5), custom_call_target="tpu_custom_call" | custom-call | tf_op jit(solution)/shard_map/prepare/pallas_call | solution.py:218
  72.9 2.8 %prepare.5.refs_10_ = bf16[384,4096]{1,0:T(8,128)(2,1)S(1)} custom-call(f32[3,1,32]{2,1,0:T(1,128)S(1)} %get-tuple-element.50.refs_0_, bf16[384,4096]{1,0:T(8,128)(2,1)} %bitcast.6), custom_call_target="tpu_custom_call" | custom-call | tf_op jit(solution)/shard_map/prepare/pallas_call | solution.py:218
  75.8 2.2 %expert.1 = (f32[64,4096]{1,0:T(8,128)S(1)}, bf16[16,4096]{1,0:T(8,128)(2,1)S(1)}, bf16[16,4096]{1,0:T(8,128)(2,1)S(1)}, bf16[16,4096]{1,0:T(8,128)(2,1)S(1)}, bf16[16,4096]{1,0:T(8,128)(2,1)S(1)}) custom-call(bf16[16,4224]{1,0:T(8,128)(2,1)S(1)} %join.1.refs_0_, bf16[16,4224]{1,0:T(8,128)(2,1)S(1)} %collective-permute-done.30.refs_1_, ...), custom_call_target="tpu_custom_call" | custom-call | tf_op jit(solution)/shard_map/expert/pallas_call | solution.py:420
  78.0 0.6 collective-permute-start.38
  78.6 0.4 collective-permute-start.42
  79.1 0.4 collective-permute-done.38.got
  79.6 0.9 collective-permute-start.39
  80.5 1.1 %collective-permute-start.41 = (bf16[16,4096]{1,0:T(8,128)(2,1)S(1)}, bf16[16,4096]{1,0:T(8,128)(2,1)S(1)}, u32[]{:S(2)}, u32[]{:S(2)}) collective-permute-start(bf16[16,4096]{1,0:T(8,128)(2,1)S(1)} %add.144), channel_id=1, source_target_pairs={{0,4},{1,5},{2,6},{3,7},{4,0},{5,1},{6,2},{7,3},{8,12},{9,13},{10,... | collective-permute-start | bytes 393224 | tf_op jit(solution)/shard_map/ppermute | solution.py:26
  81.6 1.7 %collective-permute-start.43 = (bf16[16,4096]{1,0:T(8,128)(2,1)S(1)}, bf16[16,4096]{1,0:T(8,128)(2,1)S(1)}, u32[]{:S(2)}, u32[]{:S(2)}) collective-permute-start(bf16[16,4096]{1,0:T(8,128)(2,1)S(1)} %add.145), channel_id=1, source_target_pairs={{0,6},{1,7},{2,4},{3,5},{4,2},{5,3},{6,0},{7,1},{8,14},{9,15},{10,... | collective-permute-start | bytes 393224 | tf_op jit(solution)/shard_map/ppermute | solution.py:26
  83.3 2.7 %collective-permute-done.39 = bf16[16,4096]{1,0:T(8,128)(2,1)S(1)} collective-permute-done((bf16[16,4096]{1,0:T(8,128)(2,1)S(1)}, bf16[16,4096]{1,0:T(8,128)(2,1)S(1)}, u32[]{:S(2)}, u32[]{:S(2)}) %collective-permute-start.39) | collective-permute-done | bytes 131104 | tf_op jit(solution)/shard_map/ppermute | solution.py:26
  86.0 2.9 %collective-permute-done.41 = bf16[16,4096]{1,0:T(8,128)(2,1)S(1)} collective-permute-done((bf16[16,4096]{1,0:T(8,128)(2,1)S(1)}, bf16[16,4096]{1,0:T(8,128)(2,1)S(1)}, u32[]{:S(2)}, u32[]{:S(2)}) %collective-permute-start.41) | collective-permute-done | bytes 131104 | tf_op jit(solution)/shard_map/ppermute | solution.py:26
  89.1 1.1 %collective-permute-start.45 = (bf16[4,4096]{1,0:T(4,128)(2,1)S(1)}, bf16[4,4096]{1,0:T(4,128)(2,1)S(1)}, u32[]{:S(2)}, u32[]{:S(2)}) collective-permute-start(bf16[4,4096]{1,0:T(4,128)(2,1)S(1)} %get-tuple-element.64), channel_id=1, source_target_pairs={{0,16},{1,17},{2,18},{3,19},{4,20},{5,21},{6,22},{7,23},{8,24},{9,... | collective-permute-start | bytes 98312 | tf_op jit(solution)/shard_map/ppermute | solution.py:26
  90.2 3.3 %collective-permute-start.46 = (bf16[4,4096]{1,0:T(4,128)(2,1)S(1)}, bf16[4,4096]{1,0:T(4,128)(2,1)S(1)}, u32[]{:S(2)}, u32[]{:S(2)}) collective-permute-start(bf16[4,4096]{1,0:T(4,128)(2,1)S(1)} %get-tuple-element.63), channel_id=1, source_target_pairs={{0,24},{1,25},{2,26},{3,27},{4,28},{5,29},{6,30},{7,31},{8,16},{9,... | collective-permute-start | bytes 98312 | tf_op jit(solution)/shard_map/ppermute | solution.py:26
  93.5 0.5 collective-permute-done.45
  94.0 1.9 %collective-permute-done.46 = bf16[4,4096]{1,0:T(4,128)(2,1)S(1)} collective-permute-done((bf16[4,4096]{1,0:T(4,128)(2,1)S(1)}, bf16[4,4096]{1,0:T(4,128)(2,1)S(1)}, u32[]{:S(2)}, u32[]{:S(2)}) %collective-permute-start.46) | collective-permute-done | bytes 32800 | tf_op jit(solution)/shard_map/ppermute | solution.py:26
  95.9 0.7 fusion.3
  (64 shorter events, 1.3 us)
Async XLA Ops:
  1.8 5.7 %collective-permute-start.3 = (bf16[88,256]{1,0:T(8,128)(2,1)S(1)}, bf16[88,256]{1,0:T(8,128)(2,1)S(1)}, u32[]{:S(2)}, u32[]{:S(2)}) collective-permute-start(bf16[88,256]{1,0:T(8,128)(2,1)S(1)} %get-tuple-element.35), channel_id=1, source_target_pairs={{0,8},{1,9},{2,10},{3,11},{4,12},{5,13},{6,14},{7,15},{8,0},{9,1},... | collective-permute-start | bytes 135176 | tf_op jit(solution)/shard_map/ppermute | solution.py:26
  4.9 5.8 %collective-permute-start.4 = (bf16[88,256]{1,0:T(8,128)(2,1)S(1)}, bf16[88,256]{1,0:T(8,128)(2,1)S(1)}, u32[]{:S(2)}, u32[]{:S(2)}) collective-permute-start(bf16[88,256]{1,0:T(8,128)(2,1)S(1)} %get-tuple-element.36), channel_id=1, source_target_pairs={{0,16},{1,17},{2,18},{3,19},{4,20},{5,21},{6,22},{7,23},{8,24},{9,... | collective-permute-start | bytes 135176 | tf_op jit(solution)/shard_map/ppermute | solution.py:26
  7.5 5.8 %collective-permute-start.5 = (bf16[88,256]{1,0:T(8,128)(2,1)S(1)}, bf16[88,256]{1,0:T(8,128)(2,1)S(1)}, u32[]{:S(2)}, u32[]{:S(2)}) collective-permute-start(bf16[88,256]{1,0:T(8,128)(2,1)S(1)} %get-tuple-element.37), channel_id=1, source_target_pairs={{0,24},{1,25},{2,26},{3,27},{4,28},{5,29},{6,30},{7,31},{8,16},{9,... | collective-permute-start | bytes 135176 | tf_op jit(solution)/shard_map/ppermute | solution.py:26
  13.4 13.5 %collective-permute-start.6 = (bf16[3,72,256]{2,1,0:T(8,128)(2,1)S(1)}, bf16[3,72,256]{2,1,0:T(8,128)(2,1)S(1)}, u32[]{:S(2)}, u32[]{:S(2)}) collective-permute-start(bf16[3,72,256]{2,1,0:T(8,128)(2,1)S(1)} %get-tuple-element.39), channel_id=1, source_target_pairs={{0,2},{1,3},{2,0},{3,1},{4,6},{5,7},{6,4},{7,5},{8,10},{9,11},{10,... | collective-permute-start | bytes 331784 | tf_op jit(solution)/shard_map/ppermute | solution.py:26
  14.9 12.1 %collective-permute-start.7 = (bf16[3,72,256]{2,1,0:T(8,128)(2,1)S(1)}, bf16[3,72,256]{2,1,0:T(8,128)(2,1)S(1)}, u32[]{:S(2)}, u32[]{:S(2)}) collective-permute-start(bf16[3,72,256]{2,1,0:T(8,128)(2,1)S(1)} %get-tuple-element.40), channel_id=1, source_target_pairs={{0,4},{1,5},{2,6},{3,7},{4,0},{5,1},{6,2},{7,3},{8,12},{9,13},{10,... | collective-permute-start | bytes 331784 | tf_op jit(solution)/shard_map/ppermute | solution.py:26
  16.4 11.0 %collective-permute-start.8 = (bf16[3,72,256]{2,1,0:T(8,128)(2,1)S(1)}, bf16[3,72,256]{2,1,0:T(8,128)(2,1)S(1)}, u32[]{:S(2)}, u32[]{:S(2)}) collective-permute-start(bf16[3,72,256]{2,1,0:T(8,128)(2,1)S(1)} %get-tuple-element.41), channel_id=1, source_target_pairs={{0,6},{1,7},{2,4},{3,5},{4,2},{5,3},{6,0},{7,1},{8,14},{9,15},{10,... | collective-permute-start | bytes 331784 | tf_op jit(solution)/shard_map/ppermute | solution.py:26
  16.9 4.6 %collective-permute-start = (bf16[72,256]{1,0:T(8,128)(2,1)S(1)}, bf16[72,256]{1,0:T(8,128)(2,1)S(1)}, u32[]{:S(2)}, u32[]{:S(2)}) collective-permute-start(bf16[72,256]{1,0:T(8,128)(2,1)S(1)} %get-tuple-element.32), channel_id=1, source_target_pairs={{0,2},{1,3},{2,0},{3,1},{4,6},{5,7},{6,4},{7,5},{8,10},{9,11},{10,... | collective-permute-start | bytes 110600 | tf_op jit(solution)/shard_map/ppermute | solution.py:26
  18.4 4.9 %collective-permute-start.1 = (bf16[72,256]{1,0:T(8,128)(2,1)S(1)}, bf16[72,256]{1,0:T(8,128)(2,1)S(1)}, u32[]{:S(2)}, u32[]{:S(2)}) collective-permute-start(bf16[72,256]{1,0:T(8,128)(2,1)S(1)} %get-tuple-element.33), channel_id=1, source_target_pairs={{0,4},{1,5},{2,6},{3,7},{4,0},{5,1},{6,2},{7,3},{8,12},{9,13},{10,... | collective-permute-start | bytes 110600 | tf_op jit(solution)/shard_map/ppermute | solution.py:26
  21.5 4.9 %collective-permute-start.2 = (bf16[72,256]{1,0:T(8,128)(2,1)S(1)}, bf16[72,256]{1,0:T(8,128)(2,1)S(1)}, u32[]{:S(2)}, u32[]{:S(2)}) collective-permute-start(bf16[72,256]{1,0:T(8,128)(2,1)S(1)} %get-tuple-element.34), channel_id=1, source_target_pairs={{0,6},{1,7},{2,4},{3,5},{4,2},{5,3},{6,0},{7,1},{8,14},{9,15},{10,... | collective-permute-start | bytes 110600 | tf_op jit(solution)/shard_map/ppermute | solution.py:26
  23.3 3.1 %collective-permute-start.9 = (bf16[72,256]{1,0:T(8,128)(2,1)S(1)}, bf16[72,256]{1,0:T(8,128)(2,1)S(1)}, u32[]{:S(2)}, u32[]{:S(2)}) collective-permute-start(bf16[72,256]{1,0:T(8,128)(2,1)S(1)} %get-tuple-element.31.refs_0_), channel_id=1, source_target_pairs={{0,1},{1,0},{2,3},{3,2},{4,5},{5,4},{6,7},{7,6},{8,9},{9,8},{10,11... | collective-permute-start | bytes 110600 | tf_op jit(solution)/shard_map/ppermute | solution.py:26
  26.4 1.2 %collective-permute-start.10 = (bf16[72,256]{1,0:T(8,128)(2,1)S(1)}, bf16[72,256]{1,0:T(8,128)(2,1)S(1)}, u32[]{:S(2)}, u32[]{:S(2)}) collective-permute-start(bf16[72,256]{1,0:T(8,128)(2,1)S(1)} %collective-permute-done.refs_1_), channel_id=1, source_target_pairs={{0,1},{1,0},{2,3},{3,2},{4,5},{5,4},{6,7},{7,6},{8,9},{9,8},{10,11... | collective-permute-start | bytes 110600 | tf_op jit(solution)/shard_map/ppermute | solution.py:26
  26.4 5.6 %collective-permute-start.13 = (bf16[3,72,256]{2,1,0:T(8,128)(2,1)S(1)}, bf16[3,72,256]{2,1,0:T(8,128)(2,1)S(1)}, u32[]{:S(2)}, u32[]{:S(2)}) collective-permute-start(bf16[3,72,256]{2,1,0:T(8,128)(2,1)S(1)} %get-tuple-element.38.refs_4_), channel_id=1, source_target_pairs={{0,1},{1,0},{2,3},{3,2},{4,5},{5,4},{6,7},{7,6},{8,9},{9,8},{10,11... | collective-permute-start | bytes 331784 | tf_op jit(solution)/shard_map/ppermute | solution.py:26
  26.9 5.1 %collective-permute-start.14 = (bf16[3,72,256]{2,1,0:T(8,128)(2,1)S(1)}, bf16[3,72,256]{2,1,0:T(8,128)(2,1)S(1)}, u32[]{:S(2)}, u32[]{:S(2)}) collective-permute-start(bf16[3,72,256]{2,1,0:T(8,128)(2,1)S(1)} %collective-permute-done.6.refs_5_), channel_id=1, source_target_pairs={{0,1},{1,0},{2,3},{3,2},{4,5},{5,4},{6,7},{7,6},{8,9},{9,8},{10,11... | collective-permute-start | bytes 331784 | tf_op jit(solution)/shard_map/ppermute | solution.py:26
  27.0 5.0 %collective-permute-start.15 = (bf16[3,72,256]{2,1,0:T(8,128)(2,1)S(1)}, bf16[3,72,256]{2,1,0:T(8,128)(2,1)S(1)}, u32[]{:S(2)}, u32[]{:S(2)}) collective-permute-start(bf16[3,72,256]{2,1,0:T(8,128)(2,1)S(1)} %collective-permute-done.7.refs_6_), channel_id=1, source_target_pairs={{0,1},{1,0},{2,3},{3,2},{4,5},{5,4},{6,7},{7,6},{8,9},{9,8},{10,11... | collective-permute-start | bytes 331784 | tf_op jit(solution)/shard_map/ppermute | solution.py:26
  27.4 4.6 %collective-permute-start.16 = (bf16[3,72,256]{2,1,0:T(8,128)(2,1)S(1)}, bf16[3,72,256]{2,1,0:T(8,128)(2,1)S(1)}, u32[]{:S(2)}, u32[]{:S(2)}) collective-permute-start(bf16[3,72,256]{2,1,0:T(8,128)(2,1)S(1)} %collective-permute-done.8.refs_7_), channel_id=1, source_target_pairs={{0,1},{1,0},{2,3},{3,2},{4,5},{5,4},{6,7},{7,6},{8,9},{9,8},{10,11... | collective-permute-start | bytes 331784 | tf_op jit(solution)/shard_map/ppermute | solution.py:26
  27.6 1.2 %collective-permute-start.11 = (bf16[72,256]{1,0:T(8,128)(2,1)S(1)}, bf16[72,256]{1,0:T(8,128)(2,1)S(1)}, u32[]{:S(2)}, u32[]{:S(2)}) collective-permute-start(bf16[72,256]{1,0:T(8,128)(2,1)S(1)} %collective-permute-done.1.refs_2_), channel_id=1, source_target_pairs={{0,1},{1,0},{2,3},{3,2},{4,5},{5,4},{6,7},{7,6},{8,9},{9,8},{10,11... | collective-permute-start | bytes 110600 | tf_op jit(solution)/shard_map/ppermute | solution.py:26
  28.8 3.2 %collective-permute-start.12 = (bf16[72,256]{1,0:T(8,128)(2,1)S(1)}, bf16[72,256]{1,0:T(8,128)(2,1)S(1)}, u32[]{:S(2)}, u32[]{:S(2)}) collective-permute-start(bf16[72,256]{1,0:T(8,128)(2,1)S(1)} %collective-permute-done.2.refs_3_), channel_id=1, source_target_pairs={{0,1},{1,0},{2,3},{3,2},{4,5},{5,4},{6,7},{7,6},{8,9},{9,8},{10,11... | collective-permute-start | bytes 110600 | tf_op jit(solution)/shard_map/ppermute | solution.py:26
  32.0 7.3 %copy-start.2 = (f32[4,8]{1,0:T(4,128)S(1)}, f32[4,8]{1,0:T(4,128)}, u32[]{:S(2)}) copy-start(f32[4,8]{1,0:T(4,128)} %param.27) | copy-start | bytes 388
  32.0 7.3 %copy-start.3 = (s32[4,8]{1,0:T(4,128)S(1)}, s32[4,8]{1,0:T(4,128)}, u32[]{:S(2)}) copy-start(s32[4,8]{1,0:T(4,128)} %param.26) | copy-start | bytes 388
  34.0 17.9 %copy-start = (bf16[4,4096]{1,0:T(4,128)(2,1)S(1)}, bf16[4,4096]{1,0:T(4,128)(2,1)}, u32[]{:S(2)}) copy-start(bf16[4,4096]{1,0:T(4,128)(2,1)} %param.23) | copy-start | bytes 98308
  34.0 18.0 %copy-start.1 = (f32[4096]{0:T(1024)S(1)}, f32[4096]{0:T(1024)}, u32[]{:S(2)}) copy-start(f32[4096]{0:T(1024)} %param.25) | copy-start | bytes 49156
  34.0 1.4 %collective-permute-start.18 = (bf16[16,4096]{1,0:T(8,128)(2,1)S(1)}, bf16[16,4096]{1,0:T(8,128)(2,1)S(1)}, u32[]{:S(2)}, u32[]{:S(2)}) collective-permute-start(bf16[16,4096]{1,0:T(8,128)(2,1)S(1)} %get-tuple-element.46), channel_id=1, source_target_pairs={{0,1},{1,0},{2,3},{3,2},{4,5},{5,4},{6,7},{7,6},{8,9},{9,8},{10,11... | collective-permute-start | bytes 393224 | tf_op jit(solution)/shard_map/ppermute | solution.py:26
  34.2 2.1 %collective-permute-start.20 = (bf16[16,4096]{1,0:T(8,128)(2,1)S(1)}, bf16[16,4096]{1,0:T(8,128)(2,1)S(1)}, u32[]{:S(2)}, u32[]{:S(2)}) collective-permute-start(bf16[16,4096]{1,0:T(8,128)(2,1)S(1)} %get-tuple-element.47), channel_id=1, source_target_pairs={{0,1},{1,0},{2,3},{3,2},{4,5},{5,4},{6,7},{7,6},{8,9},{9,8},{10,11... | collective-permute-start | bytes 393224 | tf_op jit(solution)/shard_map/ppermute | solution.py:26
  34.6 3.4 %collective-permute-start.22 = (bf16[16,4096]{1,0:T(8,128)(2,1)S(1)}, bf16[16,4096]{1,0:T(8,128)(2,1)S(1)}, u32[]{:S(2)}, u32[]{:S(2)}) collective-permute-start(bf16[16,4096]{1,0:T(8,128)(2,1)S(1)} %get-tuple-element.48), channel_id=1, source_target_pairs={{0,1},{1,0},{2,3},{3,2},{4,5},{5,4},{6,7},{7,6},{8,9},{9,8},{10,11... | collective-permute-start | bytes 393224 | tf_op jit(solution)/shard_map/ppermute | solution.py:26
  34.8 4.6 %collective-permute-start.17 = (bf16[16,4096]{1,0:T(8,128)(2,1)S(1)}, bf16[16,4096]{1,0:T(8,128)(2,1)S(1)}, u32[]{:S(2)}, u32[]{:S(2)}) collective-permute-start(bf16[16,4096]{1,0:T(8,128)(2,1)S(1)} %get-tuple-element.45), channel_id=1, source_target_pairs={{0,1},{1,0},{2,3},{3,2},{4,5},{5,4},{6,7},{7,6},{8,9},{9,8},{10,11... | collective-permute-start | bytes 393224 | tf_op jit(solution)/shard_map/ppermute | solution.py:26
  35.5 6.4 %collective-permute-start.19 = (bf16[16,4096]{1,0:T(8,128)(2,1)S(1)}, bf16[16,4096]{1,0:T(8,128)(2,1)S(1)}, u32[]{:S(2)}, u32[]{:S(2)}) collective-permute-start(bf16[16,4096]{1,0:T(8,128)(2,1)S(1)} %add.140), channel_id=1, source_target_pairs={{0,2},{1,3},{2,0},{3,1},{4,6},{5,7},{6,4},{7,5},{8,10},{9,11},{10,... | collective-permute-start | bytes 393224 | tf_op jit(solution)/shard_map/ppermute | solution.py:26
  36.4 7.2 %collective-permute-start.21 = (bf16[16,4096]{1,0:T(8,128)(2,1)S(1)}, bf16[16,4096]{1,0:T(8,128)(2,1)S(1)}, u32[]{:S(2)}, u32[]{:S(2)}) collective-permute-start(bf16[16,4096]{1,0:T(8,128)(2,1)S(1)} %add.141), channel_id=1, source_target_pairs={{0,4},{1,5},{2,6},{3,7},{4,0},{5,1},{6,2},{7,3},{8,12},{9,13},{10,... | collective-permute-start | bytes 393224 | tf_op jit(solution)/shard_map/ppermute | solution.py:26
  38.0 6.8 %collective-permute-start.23 = (bf16[16,4096]{1,0:T(8,128)(2,1)S(1)}, bf16[16,4096]{1,0:T(8,128)(2,1)S(1)}, u32[]{:S(2)}, u32[]{:S(2)}) collective-permute-start(bf16[16,4096]{1,0:T(8,128)(2,1)S(1)} %add.142), channel_id=1, source_target_pairs={{0,6},{1,7},{2,4},{3,5},{4,2},{5,3},{6,0},{7,1},{8,14},{9,15},{10,... | collective-permute-start | bytes 393224 | tf_op jit(solution)/shard_map/ppermute | solution.py:26
  45.0 4.5 %collective-permute-start.24 = (bf16[4,4096]{1,0:T(4,128)(2,1)S(1)}, bf16[4,4096]{1,0:T(4,128)(2,1)S(1)}, u32[]{:S(2)}, u32[]{:S(2)}) collective-permute-start(bf16[4,4096]{1,0:T(4,128)(2,1)S(1)} %get-tuple-element.65), channel_id=1, source_target_pairs={{0,8},{1,9},{2,10},{3,11},{4,12},{5,13},{6,14},{7,15},{8,0},{9,1},... | collective-permute-start | bytes 98312 | tf_op jit(solution)/shard_map/ppermute | solution.py:26
  45.1 5.0 %collective-permute-start.25 = (bf16[4,4096]{1,0:T(4,128)(2,1)S(1)}, bf16[4,4096]{1,0:T(4,128)(2,1)S(1)}, u32[]{:S(2)}, u32[]{:S(2)}) collective-permute-start(bf16[4,4096]{1,0:T(4,128)(2,1)S(1)} %get-tuple-element.67), channel_id=1, source_target_pairs={{0,16},{1,17},{2,18},{3,19},{4,20},{5,21},{6,22},{7,23},{8,24},{9,... | collective-permute-start | bytes 98312 | tf_op jit(solution)/shard_map/ppermute | solution.py:26
  46.2 5.7 %collective-permute-start.26 = (bf16[4,4096]{1,0:T(4,128)(2,1)S(1)}, bf16[4,4096]{1,0:T(4,128)(2,1)S(1)}, u32[]{:S(2)}, u32[]{:S(2)}) collective-permute-start(bf16[4,4096]{1,0:T(4,128)(2,1)S(1)} %get-tuple-element.66), channel_id=1, source_target_pairs={{0,24},{1,25},{2,26},{3,27},{4,28},{5,29},{6,30},{7,31},{8,16},{9,... | collective-permute-start | bytes 98312 | tf_op jit(solution)/shard_map/ppermute | solution.py:26
  52.3 4.4 %collective-permute-start.27 = (bf16[4,4224]{1,0:T(4,128)(2,1)S(1)}, bf16[4,4224]{1,0:T(4,128)(2,1)S(1)}, u32[]{:S(2)}, u32[]{:S(2)}) collective-permute-start(bf16[4,4224]{1,0:T(4,128)(2,1)S(1)} %concatenate.6.refs_0_), channel_id=1, source_target_pairs={{0,8},{1,9},{2,10},{3,11},{4,12},{5,13},{6,14},{7,15},{8,0},{9,1},... | collective-permute-start | bytes 101384 | tf_op jit(solution)/shard_map/ppermute | solution.py:26
  52.3 6.5 %collective-permute-start.28 = (bf16[4,4224]{1,0:T(4,128)(2,1)S(1)}, bf16[4,4224]{1,0:T(4,128)(2,1)S(1)}, u32[]{:S(2)}, u32[]{:S(2)}) collective-permute-start(bf16[4,4224]{1,0:T(4,128)(2,1)S(1)} %concatenate.6.refs_0_), channel_id=1, source_target_pairs={{0,16},{1,17},{2,18},{3,19},{4,20},{5,21},{6,22},{7,23},{8,24},{9,... | collective-permute-start | bytes 101384 | tf_op jit(solution)/shard_map/ppermute | solution.py:26
  56.4 5.7 %collective-permute-start.29 = (bf16[4,4224]{1,0:T(4,128)(2,1)S(1)}, bf16[4,4224]{1,0:T(4,128)(2,1)S(1)}, u32[]{:S(2)}, u32[]{:S(2)}) collective-permute-start(bf16[4,4224]{1,0:T(4,128)(2,1)S(1)} %concatenate.6.refs_0_), channel_id=1, source_target_pairs={{0,24},{1,25},{2,26},{3,27},{4,28},{5,29},{6,30},{7,31},{8,16},{9,... | collective-permute-start | bytes 101384 | tf_op jit(solution)/shard_map/ppermute | solution.py:26
  62.1 5.1 %collective-permute-start.30 = (bf16[16,4224]{1,0:T(8,128)(2,1)S(1)}, bf16[16,4224]{1,0:T(8,128)(2,1)S(1)}, u32[]{:S(2)}, u32[]{:S(2)}) collective-permute-start(bf16[16,4224]{1,0:T(8,128)(2,1)S(1)} %join.1.refs_0_), channel_id=1, source_target_pairs={{0,2},{1,3},{2,0},{3,1},{4,6},{5,7},{6,4},{7,5},{8,10},{9,11},{10,... | collective-permute-start | bytes 405512 | tf_op jit(solution)/shard_map/ppermute | solution.py:26
  63.0 5.0 %collective-permute-start.31 = (bf16[16,4224]{1,0:T(8,128)(2,1)S(1)}, bf16[16,4224]{1,0:T(8,128)(2,1)S(1)}, u32[]{:S(2)}, u32[]{:S(2)}) collective-permute-start(bf16[16,4224]{1,0:T(8,128)(2,1)S(1)} %join.1.refs_0_), channel_id=1, source_target_pairs={{0,4},{1,5},{2,6},{3,7},{4,0},{5,1},{6,2},{7,3},{8,12},{9,13},{10,... | collective-permute-start | bytes 405512 | tf_op jit(solution)/shard_map/ppermute | solution.py:26
  64.4 5.9 %collective-permute-start.32 = (bf16[16,4224]{1,0:T(8,128)(2,1)S(1)}, bf16[16,4224]{1,0:T(8,128)(2,1)S(1)}, u32[]{:S(2)}, u32[]{:S(2)}) collective-permute-start(bf16[16,4224]{1,0:T(8,128)(2,1)S(1)} %join.1.refs_0_), channel_id=1, source_target_pairs={{0,6},{1,7},{2,4},{3,5},{4,2},{5,3},{6,0},{7,1},{8,14},{9,15},{10,... | collective-permute-start | bytes 405512 | tf_op jit(solution)/shard_map/ppermute | solution.py:26
  65.7 10.0 %collective-permute-start.33 = (bf16[16,4224]{1,0:T(8,128)(2,1)S(1)}, bf16[16,4224]{1,0:T(8,128)(2,1)S(1)}, u32[]{:S(2)}, u32[]{:S(2)}) collective-permute-start(bf16[16,4224]{1,0:T(8,128)(2,1)S(1)} %join.1.refs_0_), channel_id=1, source_target_pairs={{0,1},{1,0},{2,3},{3,2},{4,5},{5,4},{6,7},{7,6},{8,9},{9,8},{10,11... | collective-permute-start | bytes 405512 | tf_op jit(solution)/shard_map/ppermute | solution.py:26
  67.2 8.5 %collective-permute-start.34 = (bf16[16,4224]{1,0:T(8,128)(2,1)S(1)}, bf16[16,4224]{1,0:T(8,128)(2,1)S(1)}, u32[]{:S(2)}, u32[]{:S(2)}) collective-permute-start(bf16[16,4224]{1,0:T(8,128)(2,1)S(1)} %collective-permute-done.30.refs_1_), channel_id=1, source_target_pairs={{0,1},{1,0},{2,3},{3,2},{4,5},{5,4},{6,7},{7,6},{8,9},{9,8},{10,11... | collective-permute-start | bytes 405512 | tf_op jit(solution)/shard_map/ppermute | solution.py:26
  68.0 7.8 %collective-permute-start.35 = (bf16[16,4224]{1,0:T(8,128)(2,1)S(1)}, bf16[16,4224]{1,0:T(8,128)(2,1)S(1)}, u32[]{:S(2)}, u32[]{:S(2)}) collective-permute-start(bf16[16,4224]{1,0:T(8,128)(2,1)S(1)} %collective-permute-done.31.refs_2_), channel_id=1, source_target_pairs={{0,1},{1,0},{2,3},{3,2},{4,5},{5,4},{6,7},{7,6},{8,9},{9,8},{10,11... | collective-permute-start | bytes 405512 | tf_op jit(solution)/shard_map/ppermute | solution.py:26
  70.3 5.4 %collective-permute-start.36 = (bf16[16,4224]{1,0:T(8,128)(2,1)S(1)}, bf16[16,4224]{1,0:T(8,128)(2,1)S(1)}, u32[]{:S(2)}, u32[]{:S(2)}) collective-permute-start(bf16[16,4224]{1,0:T(8,128)(2,1)S(1)} %collective-permute-done.32.refs_3_), channel_id=1, source_target_pairs={{0,1},{1,0},{2,3},{3,2},{4,5},{5,4},{6,7},{7,6},{8,9},{9,8},{10,11... | collective-permute-start | bytes 405512 | tf_op jit(solution)/shard_map/ppermute | solution.py:26
  78.0 1.6 %collective-permute-start.38 = (bf16[16,4096]{1,0:T(8,128)(2,1)S(1)}, bf16[16,4096]{1,0:T(8,128)(2,1)S(1)}, u32[]{:S(2)}, u32[]{:S(2)}) collective-permute-start(bf16[16,4096]{1,0:T(8,128)(2,1)S(1)} %get-tuple-element.53), channel_id=1, source_target_pairs={{0,1},{1,0},{2,3},{3,2},{4,5},{5,4},{6,7},{7,6},{8,9},{9,8},{10,11... | collective-permute-start | bytes 393224 | tf_op jit(solution)/shard_map/ppermute | solution.py:26
  78.6 1.9 %collective-permute-start.40 = (bf16[16,4096]{1,0:T(8,128)(2,1)S(1)}, bf16[16,4096]{1,0:T(8,128)(2,1)S(1)}, u32[]{:S(2)}, u32[]{:S(2)}) collective-permute-start(bf16[16,4096]{1,0:T(8,128)(2,1)S(1)} %get-tuple-element.54), channel_id=1, source_target_pairs={{0,1},{1,0},{2,3},{3,2},{4,5},{5,4},{6,7},{7,6},{8,9},{9,8},{10,11... | collective-permute-start | bytes 393224 | tf_op jit(solution)/shard_map/ppermute | solution.py:26
  78.6 3.0 %collective-permute-start.42 = (bf16[16,4096]{1,0:T(8,128)(2,1)S(1)}, bf16[16,4096]{1,0:T(8,128)(2,1)S(1)}, u32[]{:S(2)}, u32[]{:S(2)}) collective-permute-start(bf16[16,4096]{1,0:T(8,128)(2,1)S(1)} %get-tuple-element.55), channel_id=1, source_target_pairs={{0,1},{1,0},{2,3},{3,2},{4,5},{5,4},{6,7},{7,6},{8,9},{9,8},{10,11... | collective-permute-start | bytes 393224 | tf_op jit(solution)/shard_map/ppermute | solution.py:26
  79.1 4.3 %collective-permute-start.37 = (bf16[16,4096]{1,0:T(8,128)(2,1)S(1)}, bf16[16,4096]{1,0:T(8,128)(2,1)S(1)}, u32[]{:S(2)}, u32[]{:S(2)}) collective-permute-start(bf16[16,4096]{1,0:T(8,128)(2,1)S(1)} %get-tuple-element.52), channel_id=1, source_target_pairs={{0,1},{1,0},{2,3},{3,2},{4,5},{5,4},{6,7},{7,6},{8,9},{9,8},{10,11... | collective-permute-start | bytes 393224 | tf_op jit(solution)/shard_map/ppermute | solution.py:26
  79.6 6.4 %collective-permute-start.39 = (bf16[16,4096]{1,0:T(8,128)(2,1)S(1)}, bf16[16,4096]{1,0:T(8,128)(2,1)S(1)}, u32[]{:S(2)}, u32[]{:S(2)}) collective-permute-start(bf16[16,4096]{1,0:T(8,128)(2,1)S(1)} %add.143), channel_id=1, source_target_pairs={{0,2},{1,3},{2,0},{3,1},{4,6},{5,7},{6,4},{7,5},{8,10},{9,11},{10,... | collective-permute-start | bytes 393224 | tf_op jit(solution)/shard_map/ppermute | solution.py:26
  80.5 8.4 %collective-permute-start.41 = (bf16[16,4096]{1,0:T(8,128)(2,1)S(1)}, bf16[16,4096]{1,0:T(8,128)(2,1)S(1)}, u32[]{:S(2)}, u32[]{:S(2)}) collective-permute-start(bf16[16,4096]{1,0:T(8,128)(2,1)S(1)} %add.144), channel_id=1, source_target_pairs={{0,4},{1,5},{2,6},{3,7},{4,0},{5,1},{6,2},{7,3},{8,12},{9,13},{10,... | collective-permute-start | bytes 393224 | tf_op jit(solution)/shard_map/ppermute | solution.py:26
  81.6 7.2 %collective-permute-start.43 = (bf16[16,4096]{1,0:T(8,128)(2,1)S(1)}, bf16[16,4096]{1,0:T(8,128)(2,1)S(1)}, u32[]{:S(2)}, u32[]{:S(2)}) collective-permute-start(bf16[16,4096]{1,0:T(8,128)(2,1)S(1)} %add.145), channel_id=1, source_target_pairs={{0,6},{1,7},{2,4},{3,5},{4,2},{5,3},{6,0},{7,1},{8,14},{9,15},{10,... | collective-permute-start | bytes 393224 | tf_op jit(solution)/shard_map/ppermute | solution.py:26
  89.0 4.5 %collective-permute-start.44 = (bf16[4,4096]{1,0:T(4,128)(2,1)S(1)}, bf16[4,4096]{1,0:T(4,128)(2,1)S(1)}, u32[]{:S(2)}, u32[]{:S(2)}) collective-permute-start(bf16[4,4096]{1,0:T(4,128)(2,1)S(1)} %get-tuple-element.62), channel_id=1, source_target_pairs={{0,8},{1,9},{2,10},{3,11},{4,12},{5,13},{6,14},{7,15},{8,0},{9,1},... | collective-permute-start | bytes 98312 | tf_op jit(solution)/shard_map/ppermute | solution.py:26
  89.1 4.9 %collective-permute-start.45 = (bf16[4,4096]{1,0:T(4,128)(2,1)S(1)}, bf16[4,4096]{1,0:T(4,128)(2,1)S(1)}, u32[]{:S(2)}, u32[]{:S(2)}) collective-permute-start(bf16[4,4096]{1,0:T(4,128)(2,1)S(1)} %get-tuple-element.64), channel_id=1, source_target_pairs={{0,16},{1,17},{2,18},{3,19},{4,20},{5,21},{6,22},{7,23},{8,24},{9,... | collective-permute-start | bytes 98312 | tf_op jit(solution)/shard_map/ppermute | solution.py:26
  90.2 5.7 %collective-permute-start.46 = (bf16[4,4096]{1,0:T(4,128)(2,1)S(1)}, bf16[4,4096]{1,0:T(4,128)(2,1)S(1)}, u32[]{:S(2)}, u32[]{:S(2)}) collective-permute-start(bf16[4,4096]{1,0:T(4,128)(2,1)S(1)} %get-tuple-element.63), channel_id=1, source_target_pairs={{0,24},{1,25},{2,26},{3,27},{4,28},{5,29},{6,30},{7,31},{8,16},{9,... | collective-permute-start | bytes 98312 | tf_op jit(solution)/shard_map/ppermute | solution.py:26
